TPU v7x, 32 devices: a whole 2x2x4 slice. The times are simulated.
32 devices in a mesh: grp: 2 (over y), slab: 4 (over z), row: 2 (over x), col: 2 (over core).
Axes of the slice: x: 2, y: 2, z: 4, core: 2. Of those that a mesh axis runs over, the one named last changes fastest.
Arguments:
- image: float32 [3, 64, 32, 256], P(None, ('grp', 'slab'), 'row', 'col'), parts along dimension 1, may hold values from -28 to 28, as said below
- brain_mask: int32 [64, 32, 256], P(('grp', 'slab'), 'row', 'col'), parts along dimension 0, may hold values from 0 to 1, as said below
- labels: int32 [64, 32, 256], P(('grp', 'slab'), 'row', 'col'), parts along dimension 0, may hold values from 0 to 7
Outputs:
- posterior: bfloat16 [8, 64, 32, 256], P(None, ('grp', 'slab'), 'row', 'col'), parts along dimension 1
- bias_field: float32 [3, 64, 32, 256], P(None, ('grp', 'slab'), 'row', 'col'), parts along dimension 1
- class_means: float32 [16, 3], P('grp'), parts along dimension 0
There are 2 independent parts, one for each index of `grp`. A program takes and returns all parts, laid end to end along the dimension named above; each array names one. Nothing has to cross between parts.
Inputs may be any that keep to these rules, and one draw needn't show every extreme that they name: `image`: log intensities of 3 modalities. `brain_mask`: 1 marks a brain cell, 0 a cell outside.
All inputs are finite; a program needn't handle non-finite values.
Results may differ from a plain program's by a relative error of at most 0.001.
Values sent between devices are 32-bit elements; how exact they have to be, the bound alone decides.
No kernel may reach another device: no remote copies, remote signals or barrier semaphores. Data moves between devices by JAX's collectives and lax.ppermute only.
A program may use at most 64 MiB of HBM per device.

v0:
```python
import math

import jax
import jax.numpy as jnp
from jax import lax
from jax.sharding import PartitionSpec as P

M = 3
K = 8
EM_ITERS = 2
MF_PASSES = 2


highest = lax.Precision.HIGHEST
coupling = 1.0
breadth = 8.0


def extended(cells, sides, width):
    for axis, dim in sides:
        count = lax.axis_size(axis)
        ends = count - 1
        head = lax.slice_in_dim(cells, 0, width, axis=dim)
        tail = lax.slice_in_dim(cells, cells.shape[dim] - width, cells.shape[dim], axis=dim)
        cells = jnp.concatenate(
            [
                lax.ppermute(tail, axis, [(i, (i + 1) % count) for i in range(ends)]),
                cells,
                lax.ppermute(head, axis, [((i + 1) % count, i) for i in range(ends)]),
            ],
            axis=dim,
        )
    return cells


def circulant(length):
    index = jnp.arange(length, dtype=jnp.int32)
    folded = jnp.minimum(index, length - index).astype(jnp.float32) / length
    response = jnp.exp(-2.0 * math.pi**2 * (length / breadth) ** 2 * folded * folded)
    product = index[:, None] * index[None, :] % length
    angles = 2.0 * math.pi / length * product.astype(jnp.float32)
    cosine = jnp.cos(angles)
    sine = jnp.sin(angles)
    even_part = jnp.dot(cosine * response[None, :], cosine.T, precision=highest)
    odd_part = jnp.dot(sine * response[None, :], sine.T, precision=highest)
    return (even_part + odd_part) / length


def neighbour_sum(belief):
    padded = extended(belief, (("slab", 1), ("row", 2), ("col", 3)), 1)
    total = padded[:, 2:, 1:-1, 1:-1] + padded[:, :-2, 1:-1, 1:-1]
    total = total + padded[:, 1:-1, 2:, 1:-1] + padded[:, 1:-1, :-2, 1:-1]
    total = total + padded[:, 1:-1, 1:-1, 2:] + padded[:, 1:-1, 1:-1, :-2]
    return total


def class_moments(belief, corrected):
    flat = belief.reshape(K, -1)
    values = corrected.reshape(M, -1)
    count, first, squares = lax.psum(
        (
            jnp.sum(flat, axis=1),
            jnp.dot(flat, values.T, precision=highest),
            jnp.dot(flat, (values * values).T, precision=highest),
        ),
        ("slab", "row", "col"),
    )
    means = first / (count + 1.0)[:, None]
    spread = squares - 2.0 * means * first + means * means * count[:, None]
    variance = (spread + 1.0) / (count + 1.0)[:, None]
    return (count, means, variance)


def log_density(corrected, means, variance, prior):
    offset = corrected[None] - means[:, :, None, None, None]
    terms = (
        offset * offset / variance[:, :, None, None, None]
        + jnp.log(variance)[:, :, None, None, None]
    )
    return jnp.log(prior)[:, None, None, None] - 0.5 * jnp.sum(terms, axis=1)


def smoothed(residual, column_local, row_table, slab_table):
    across = jnp.einsum(
        "msrc,cd->msrd",
        lax.all_gather(residual, "col", axis=3, tiled=True),
        column_local,
        precision=highest,
    )
    mixed = jnp.einsum(
        "msrc,rq->msqc",
        lax.all_to_all(across, "row", split_axis=1, concat_axis=2, tiled=True),
        row_table,
        precision=highest,
    )
    across = lax.all_to_all(mixed, "row", split_axis=2, concat_axis=1, tiled=True)
    mixed = jnp.einsum(
        "msrc,sq->mqrc",
        lax.all_to_all(across, "slab", split_axis=2, concat_axis=1, tiled=True),
        slab_table,
        precision=highest,
    )
    return lax.all_to_all(mixed, "slab", split_axis=1, concat_axis=2, tiled=True)


def local(image, brain_mask, labels):
    channels, slabs, rows, columns = image.shape
    inside = brain_mask.astype(jnp.float32)
    kinds = jnp.arange(K, dtype=jnp.int32)
    belief = (labels[None] == kinds[:, None, None, None]).astype(jnp.float32) * inside[None]
    column_table = circulant(columns * lax.axis_size("col"))
    column_local = lax.dynamic_slice_in_dim(
        column_table, lax.axis_index("col") * columns, columns, 1
    )
    row_table = circulant(rows * lax.axis_size("row"))
    slab_table = circulant(slabs * lax.axis_size("slab"))
    bias_field = jnp.zeros_like(image)
    means = jnp.zeros((K, channels), jnp.float32)
    for iteration in range(EM_ITERS):
        corrected = image - bias_field
        count, means, variance = class_moments(belief, corrected)
        prior = (count + 1.0) / (jnp.sum(count) + K)
        total = jnp.sum(belief, axis=0)
        removed = jnp.dot(means.T, belief.reshape(K, -1), precision=highest).reshape(image.shape)
        residual = image * total[None] - removed
        bias_field = smoothed(residual, column_local, row_table, slab_table)
        corrected = image - bias_field
        density = log_density(corrected, means, variance, prior)
        for sweep_index in range(MF_PASSES):
            belief = (
                jax.nn.softmax(density + coupling * neighbour_sum(belief), axis=0) * inside[None]
            )
    return (belief.astype(jnp.bfloat16), bias_field, means)


def solution(mesh):
    placed = (
        P(None, ("grp", "slab"), "row", "col"),
        P(("grp", "slab"), "row", "col"),
        P(("grp", "slab"), "row", "col"),
    )
    return jax.shard_map(
        local,
        mesh=mesh,
        in_specs=placed,
        out_specs=(
            P(None, ("grp", "slab"), "row", "col"),
            P(None, ("grp", "slab"), "row", "col"),
            P("grp", None),
        ),
        check_vma=False,
    )
```

profile of v0, /device:TPU:16, one launch (start us, length us, event | category | flops | bytes accessed | tf_op | source)
XLA Modules:
  0.0 239.0 jit_solution(11587355852781525625)
XLA Ops:
  6.4 23.6 %all-reduce.1 = (f32[8,3]{0,1:T(4,128)S(1)}, f32[8,3]{0,1:T(4,128)S(1)}, f32[8]{0:T(128)S(1)}) all-reduce(f32[8,3]{0,1:T(4,128)S(1)} %fusion.2, f32[8,3]{0,1:T(4,128)S(1)} %convolution_bitcast_fusion.6, f32[8]{0:T(128)S(1)} %select_reduce_fusion), channel_id=1, replica_groups=mesh['grp'=2,'slab'=4,'row'=2,'col'=2] {'slab','row','col'}, use_global_device_ids=true, to_apply=%region_5.6 | all-reduce | flops 56 | bytes 448 | tf_op jit(solution)/shard_map/psum | solution.py:60
  32.5 2.2 all_gather.6
  35.9 3.4 %all-to-all-start = ((f32[3,8,16,128]{3,2,0,1:T(8,128)}), f32[3,8,16,128]{3,2,0,1:T(8,128)S(1)}, u32[]{:S(2)}, u32[]{:S(2)}) async-start(f32[3,8,16,128]{3,2,0,1:T(8,128)} %fusion.39), calls=%async_computation | async-start | bytes 393216 | tf_op jit(solution)/shard_map/all_to_all | solution.py:92
  39.8 4.5 %all-to-all-done = f32[3,8,16,128]{3,2,0,1:T(8,128)S(1)} async-done(((f32[3,8,16,128]{3,2,0,1:T(8,128)}), f32[3,8,16,128]{3,2,0,1:T(8,128)S(1)}, u32[]{:S(2)}, u32[]{:S(2)}) %all-to-all-start) | async-done | bytes 196640 | tf_op jit(solution)/shard_map/all_to_all | solution.py:92
  45.5 3.4 %all-to-all-start.1 = ((f32[3,4,32,128]{3,1,0,2:T(4,128)}), f32[3,4,32,128]{3,1,0,2:T(4,128)S(1)}, u32[]{:S(2)}, u32[]{:S(2)}) async-start(f32[3,4,32,128]{3,1,0,2:T(4,128)} %copy.240), calls=%async_computation.1 | async-start | bytes 393216 | tf_op jit(solution)/shard_map/all_to_all | solution.py:96
  49.0 8.7 %collective-permute-start.1 = (f32[8,1,16,128]{3,2,1,0:T(8,128)S(1)}, f32[8,1,16,128]{3,2,1,0:T(8,128)S(1)}, u32[]{:S(2)}, u32[]{:S(2)}) collective-permute-start(f32[8,1,16,128]{3,2,1,0:T(8,128)S(1)} %get-tuple-element.55), channel_id=1, source_target_pairs={{0,4},{4,8},{8,12},{1,5},{5,9},{9,13},{2,6},{6,10},{10,14},{3,7},{... | collective-permute-start | bytes 196616 | tf_op jit(solution)/shard_map/ppermute | solution.py:27
  57.8 1.9 collective-permute-start
  60.5 8.1 %all-to-all-start.2 = ((f32[3,8,16,128]{3,1,0,2:T(8,128)}), f32[3,8,16,128]{3,1,0,2:T(8,128)S(1)}, u32[]{:S(2)}, u32[]{:S(2)}) async-start(f32[3,8,16,128]{3,1,0,2:T(8,128)} %copy.243), calls=%async_computation.2 | async-start | bytes 393216 | tf_op jit(solution)/shard_map/all_to_all | solution.py:99
  70.0 4.5 %collective-permute-start.3 = (f32[8,10,1,128]{3,0,2,1:T(8,128)S(1)}, f32[8,10,1,128]{3,0,2,1:T(8,128)S(1)}, u32[]{:S(2)}, u32[]{:S(2)}) collective-permute-start(f32[8,10,1,128]{3,0,2,1:T(8,128)S(1)} %copy.339), channel_id=1, source_target_pairs={{0,2},{1,3},{4,6},{5,7},{8,10},{9,11},{12,14},{13,15},{16,18},{17,... | collective-permute-start | bytes 122888 | tf_op jit(solution)/shard_map/ppermute | solution.py:27
  77.6 5.1 %all-to-all-start.3 = ((f32[3,32,4,128]{3,2,0,1:T(4,128)}), f32[3,32,4,128]{3,2,0,1:T(4,128)S(1)}, u32[]{:S(2)}, u32[]{:S(2)}) async-start(f32[3,32,4,128]{3,2,0,1:T(4,128)} %copy.247), calls=%async_computation.3 | async-start | bytes 393216 | tf_op jit(solution)/shard_map/all_to_all | solution.py:103
  83.9 1.8 copy.258
  95.0 3.4 %collective-permute-start.7 = (f32[8,1,16,128]{3,2,1,0:T(8,128)S(1)}, f32[8,1,16,128]{3,2,1,0:T(8,128)S(1)}, u32[]{:S(2)}, u32[]{:S(2)}) collective-permute-start(f32[8,1,16,128]{3,2,1,0:T(8,128)S(1)} %get-tuple-element.53), channel_id=1, source_target_pairs={{0,4},{4,8},{8,12},{1,5},{5,9},{9,13},{2,6},{6,10},{10,14},{3,7},{... | collective-permute-start | bytes 196616 | tf_op jit(solution)/shard_map/ppermute | solution.py:27
  98.4 2.5 %collective-permute-start.6 = (f32[8,1,16,128]{3,2,1,0:T(8,128)S(1)}, f32[8,1,16,128]{3,2,1,0:T(8,128)S(1)}, u32[]{:S(2)}, u32[]{:S(2)}) collective-permute-start(f32[8,1,16,128]{3,2,1,0:T(8,128)S(1)} %get-tuple-element.54), channel_id=1, source_target_pairs={{4,0},{8,4},{12,8},{5,1},{9,5},{13,9},{6,2},{10,6},{14,10},{7,3},{... | collective-permute-start | bytes 196616 | tf_op jit(solution)/shard_map/ppermute | solution.py:29
  101.2 3.4 %collective-permute-done.6 = f32[8,1,16,128]{3,2,1,0:T(8,128)S(1)} collective-permute-done((f32[8,1,16,128]{3,2,1,0:T(8,128)S(1)}, f32[8,1,16,128]{3,2,1,0:T(8,128)S(1)}, u32[]{:S(2)}, u32[]{:S(2)}) %collective-permute-start.6) | collective-permute-done | bytes 65568 | tf_op jit(solution)/shard_map/ppermute | solution.py:29
  106.0 4.7 %collective-permute-start.9 = (f32[8,10,1,128]{3,0,2,1:T(8,128)S(1)}, f32[8,10,1,128]{3,0,2,1:T(8,128)S(1)}, u32[]{:S(2)}, u32[]{:S(2)}) collective-permute-start(f32[8,10,1,128]{3,0,2,1:T(8,128)S(1)} %copy.341), channel_id=1, source_target_pairs={{0,2},{1,3},{4,6},{5,7},{8,10},{9,11},{12,14},{13,15},{16,18},{17,... | collective-permute-start | bytes 122888 | tf_op jit(solution)/shard_map/ppermute | solution.py:27
  116.4 3.8 %collective-permute-start.11 = (f32[8,10,18,1]{2,0,3,1:T(8,128)S(1)}, f32[8,10,18,1]{2,0,3,1:T(8,128)}, u32[]{:S(2)}, u32[]{:S(2)}) collective-permute-start(f32[8,10,18,1]{2,0,3,1:T(8,128)S(1)} %copy.270), channel_id=1, source_target_pairs={{0,1},{2,3},{4,5},{6,7},{8,9},{10,11},{12,13},{14,15},{16,17},{18,... | collective-permute-start | bytes 17288 | tf_op jit(solution)/shard_map/ppermute | solution.py:27
  126.7 24.8 %all-reduce = (f32[8,3]{0,1:T(4,128)S(1)}, f32[8]{0:T(128)S(1)}, f32[8,3]{0,1:T(4,128)S(1)}) all-reduce(f32[8,3]{0,1:T(4,128)S(1)} %convolution_bitcast_fusion.5, f32[8]{0:T(128)S(1)} %get-tuple-element.10, f32[8,3]{0,1:T(4,128)S(1)} %convolution_bitcast_fusion.4), channel_id=1, replica_groups=mesh['grp'=2,'slab'=4,'row'=2,'col'=2] {'slab','row','col'}, use_global_device_ids=true, to_apply=%region_15.16 | all-reduce | flops 56 | bytes 448 | tf_op jit(solution)/shard_map/psum | solution.py:60
  153.8 2.2 all_gather.7
  156.5 7.4 %all_to_all.144 = f32[3,8,16,128]{3,2,0,1:T(8,128)S(1)} all-to-all(f32[3,8,16,128]{3,2,0,1:T(8,128)S(1)} %fusion.37), channel_id=1, replica_groups=mesh['grp'=2,'slab'=4,'row'=2,'col'=2] {'row'}, dimensions={1} | all-to-all | bytes 393216 | tf_op jit(solution)/shard_map/all_to_all | solution.py:92
  165.2 3.4 %all-to-all-start.5 = ((f32[3,4,32,128]{3,1,0,2:T(4,128)}), f32[3,4,32,128]{3,1,0,2:T(4,128)S(1)}, u32[]{:S(2)}, u32[]{:S(2)}) async-start(f32[3,4,32,128]{3,1,0,2:T(4,128)} %copy.281), calls=%async_computation.5 | async-start | bytes 393216 | tf_op jit(solution)/shard_map/all_to_all | solution.py:96
  168.6 6.9 %collective-permute-start.13 = (f32[8,1,16,128]{3,2,1,0:T(8,128)S(1)}, f32[8,1,16,128]{3,2,1,0:T(8,128)S(1)}, u32[]{:S(2)}, u32[]{:S(2)}) collective-permute-start(f32[8,1,16,128]{3,2,1,0:T(8,128)S(1)} %get-tuple-element.51), channel_id=1, source_target_pairs={{0,4},{4,8},{8,12},{1,5},{5,9},{9,13},{2,6},{6,10},{10,14},{3,7},{... | collective-permute-start | bytes 196616 | tf_op jit(solution)/shard_map/ppermute | solution.py:27
  175.5 1.9 collective-permute-start.12
  178.3 7.9 %all-to-all-start.6 = ((f32[3,8,16,128]{3,1,0,2:T(8,128)}), f32[3,8,16,128]{3,1,0,2:T(8,128)S(1)}, u32[]{:S(2)}, u32[]{:S(2)}) async-start(f32[3,8,16,128]{3,1,0,2:T(8,128)} %copy.284), calls=%async_computation.6 | async-start | bytes 393216 | tf_op jit(solution)/shard_map/all_to_all | solution.py:99
  187.6 4.5 %collective-permute-start.15 = (f32[8,10,1,128]{3,0,2,1:T(8,128)S(1)}, f32[8,10,1,128]{3,0,2,1:T(8,128)S(1)}, u32[]{:S(2)}, u32[]{:S(2)}) collective-permute-start(f32[8,10,1,128]{3,0,2,1:T(8,128)S(1)} %copy.343), channel_id=1, source_target_pairs={{0,2},{1,3},{4,6},{5,7},{8,10},{9,11},{12,14},{13,15},{16,18},{17,... | collective-permute-start | bytes 122888 | tf_op jit(solution)/shard_map/ppermute | solution.py:27
  195.2 5.1 %all-to-all-start.7 = ((f32[3,32,4,128]{3,2,0,1:T(4,128)}), f32[3,32,4,128]{3,2,0,1:T(4,128)S(1)}, u32[]{:S(2)}, u32[]{:S(2)}) async-start(f32[3,32,4,128]{3,2,0,1:T(4,128)} %copy.288), calls=%async_computation.7 | async-start | bytes 393216 | tf_op jit(solution)/shard_map/all_to_all | solution.py:103
  201.6 1.8 copy.301
  205.2 3.0 %collective-permute-start.17 = (f32[8,10,18,1]{2,0,3,1:T(8,128)S(1)}, f32[8,10,18,1]{2,0,3,1:T(8,128)S(1)}, u32[]{:S(2)}, u32[]{:S(2)}) collective-permute-start(f32[8,10,18,1]{2,0,3,1:T(8,128)S(1)} %copy.303), channel_id=1, source_target_pairs={{0,1},{2,3},{4,5},{6,7},{8,9},{10,11},{12,13},{14,15},{16,17},{18,... | collective-permute-start | bytes 17288 | tf_op jit(solution)/shard_map/ppermute | solution.py:27
  212.8 3.4 %collective-permute-start.19 = (f32[8,1,16,128]{3,2,1,0:T(8,128)S(1)}, f32[8,1,16,128]{3,2,1,0:T(8,128)S(1)}, u32[]{:S(2)}, u32[]{:S(2)}) collective-permute-start(f32[8,1,16,128]{3,2,1,0:T(8,128)S(1)} %get-tuple-element.49), channel_id=1, source_target_pairs={{0,4},{4,8},{8,12},{1,5},{5,9},{9,13},{2,6},{6,10},{10,14},{3,7},{... | collective-permute-start | bytes 196616 | tf_op jit(solution)/shard_map/ppermute | solution.py:27
  216.2 2.5 %collective-permute-start.18 = (f32[8,1,16,128]{3,2,1,0:T(8,128)S(1)}, f32[8,1,16,128]{3,2,1,0:T(8,128)S(1)}, u32[]{:S(2)}, u32[]{:S(2)}) collective-permute-start(f32[8,1,16,128]{3,2,1,0:T(8,128)S(1)} %get-tuple-element.50), channel_id=1, source_target_pairs={{4,0},{8,4},{12,8},{5,1},{9,5},{13,9},{6,2},{10,6},{14,10},{7,3},{... | collective-permute-start | bytes 196616 | tf_op jit(solution)/shard_map/ppermute | solution.py:29
  219.1 3.3 %collective-permute-done.18 = f32[8,1,16,128]{3,2,1,0:T(8,128)S(1)} collective-permute-done((f32[8,1,16,128]{3,2,1,0:T(8,128)S(1)}, f32[8,1,16,128]{3,2,1,0:T(8,128)S(1)}, u32[]{:S(2)}, u32[]{:S(2)}) %collective-permute-start.18) | collective-permute-done | bytes 65568 | tf_op jit(solution)/shard_map/ppermute | solution.py:29
  223.8 4.8 %collective-permute-start.21 = (f32[8,10,1,128]{3,0,2,1:T(8,128)S(1)}, f32[8,10,1,128]{3,0,2,1:T(8,128)S(1)}, u32[]{:S(2)}, u32[]{:S(2)}) collective-permute-start(f32[8,10,1,128]{3,0,2,1:T(8,128)S(1)} %copy.345), channel_id=1, source_target_pairs={{0,2},{1,3},{4,6},{5,7},{8,10},{9,11},{12,14},{13,15},{16,18},{17,... | collective-permute-start | bytes 122888 | tf_op jit(solution)/shard_map/ppermute | solution.py:27
  232.9 3.0 %collective-permute-start.23 = (f32[8,10,18,1]{2,0,3,1:T(8,128)S(1)}, f32[8,10,18,1]{2,0,3,1:T(8,128)S(1)}, u32[]{:S(2)}, u32[]{:S(2)}) collective-permute-start(f32[8,10,18,1]{2,0,3,1:T(8,128)S(1)} %copy.313), channel_id=1, source_target_pairs={{0,1},{2,3},{4,5},{6,7},{8,9},{10,11},{12,13},{14,15},{16,17},{18,... | collective-permute-start | bytes 17288 | tf_op jit(solution)/shard_map/ppermute | solution.py:27
  (186 shorter events, 65.0 us)
Async XLA Ops:
  35.9 8.5 %all-to-all-start = ((f32[3,8,16,128]{3,2,0,1:T(8,128)}), f32[3,8,16,128]{3,2,0,1:T(8,128)S(1)}, u32[]{:S(2)}, u32[]{:S(2)}) async-start(f32[3,8,16,128]{3,2,0,1:T(8,128)} %fusion.39), calls=%async_computation | async-start | bytes 393216 | tf_op jit(solution)/shard_map/all_to_all | solution.py:92
  45.5 14.1 %all-to-all-start.1 = ((f32[3,4,32,128]{3,1,0,2:T(4,128)}), f32[3,4,32,128]{3,1,0,2:T(4,128)S(1)}, u32[]{:S(2)}, u32[]{:S(2)}) async-start(f32[3,4,32,128]{3,1,0,2:T(4,128)} %copy.240), calls=%async_computation.1 | async-start | bytes 393216 | tf_op jit(solution)/shard_map/all_to_all | solution.py:96
  49.0 19.6 %collective-permute-start.1 = (f32[8,1,16,128]{3,2,1,0:T(8,128)S(1)}, f32[8,1,16,128]{3,2,1,0:T(8,128)S(1)}, u32[]{:S(2)}, u32[]{:S(2)}) collective-permute-start(f32[8,1,16,128]{3,2,1,0:T(8,128)S(1)} %get-tuple-element.55), channel_id=1, source_target_pairs={{0,4},{4,8},{8,12},{1,5},{5,9},{9,13},{2,6},{6,10},{10,14},{3,7},{... | collective-permute-start | bytes 196616 | tf_op jit(solution)/shard_map/ppermute | solution.py:27
  57.8 10.8 %collective-permute-start = (f32[8,1,16,128]{3,2,1,0:T(8,128)S(1)}, f32[8,1,16,128]{3,2,1,0:T(8,128)S(1)}, u32[]{:S(2)}, u32[]{:S(2)}) collective-permute-start(f32[8,1,16,128]{3,2,1,0:T(8,128)S(1)} %get-tuple-element.56), channel_id=1, source_target_pairs={{4,0},{8,4},{12,8},{5,1},{9,5},{13,9},{6,2},{10,6},{14,10},{7,3},{... | collective-permute-start | bytes 196616 | tf_op jit(solution)/shard_map/ppermute | solution.py:29
  60.5 15.9 %all-to-all-start.2 = ((f32[3,8,16,128]{3,1,0,2:T(8,128)}), f32[3,8,16,128]{3,1,0,2:T(8,128)S(1)}, u32[]{:S(2)}, u32[]{:S(2)}) async-start(f32[3,8,16,128]{3,1,0,2:T(8,128)} %copy.243), calls=%async_computation.2 | async-start | bytes 393216 | tf_op jit(solution)/shard_map/all_to_all | solution.py:99
  68.6 5.9 %collective-permute-start.2 = (f32[8,10,1,128]{3,0,2,1:T(8,128)S(1)}, f32[8,10,1,128]{3,0,2,1:T(8,128)S(1)}, u32[]{:S(2)}, u32[]{:S(2)}) collective-permute-start(f32[8,10,1,128]{3,0,2,1:T(8,128)S(1)} %copy.338), channel_id=1, source_target_pairs={{2,0},{3,1},{6,4},{7,5},{10,8},{11,9},{14,12},{15,13},{18,16},{19,... | collective-permute-start | bytes 122888 | tf_op jit(solution)/shard_map/ppermute | solution.py:29
  70.0 6.2 %collective-permute-start.3 = (f32[8,10,1,128]{3,0,2,1:T(8,128)S(1)}, f32[8,10,1,128]{3,0,2,1:T(8,128)S(1)}, u32[]{:S(2)}, u32[]{:S(2)}) collective-permute-start(f32[8,10,1,128]{3,0,2,1:T(8,128)S(1)} %copy.339), channel_id=1, source_target_pairs={{0,2},{1,3},{4,6},{5,7},{8,10},{9,11},{12,14},{13,15},{16,18},{17,... | collective-permute-start | bytes 122888 | tf_op jit(solution)/shard_map/ppermute | solution.py:27
  77.6 15.3 %all-to-all-start.3 = ((f32[3,32,4,128]{3,2,0,1:T(4,128)}), f32[3,32,4,128]{3,2,0,1:T(4,128)S(1)}, u32[]{:S(2)}, u32[]{:S(2)}) async-start(f32[3,32,4,128]{3,2,0,1:T(4,128)} %copy.247), calls=%async_computation.3 | async-start | bytes 393216 | tf_op jit(solution)/shard_map/all_to_all | solution.py:103
  86.3 5.0 %collective-permute-start.5 = (f32[8,10,18,1]{2,0,3,1:T(8,128)S(1)}, f32[8,10,18,1]{2,0,3,1:T(8,128)S(1)}, u32[]{:S(2)}, u32[]{:S(2)}) collective-permute-start(f32[8,10,18,1]{2,0,3,1:T(8,128)S(1)} %copy.260), channel_id=1, source_target_pairs={{0,1},{2,3},{4,5},{6,7},{8,9},{10,11},{12,13},{14,15},{16,17},{18,... | collective-permute-start | bytes 17288 | tf_op jit(solution)/shard_map/ppermute | solution.py:27
  87.6 3.1 %collective-permute-start.4 = (f32[8,10,18,1]{2,0,3,1:T(8,128)S(1)}, f32[8,10,18,1]{2,0,3,1:T(8,128)S(1)}, u32[]{:S(2)}, u32[]{:S(2)}) collective-permute-start(f32[8,10,18,1]{2,0,3,1:T(8,128)S(1)} %copy.258), channel_id=1, source_target_pairs={{1,0},{3,2},{5,4},{7,6},{9,8},{11,10},{13,12},{15,14},{17,16},{19,... | collective-permute-start | bytes 17288 | tf_op jit(solution)/shard_map/ppermute | solution.py:29
  95.0 6.2 %collective-permute-start.7 = (f32[8,1,16,128]{3,2,1,0:T(8,128)S(1)}, f32[8,1,16,128]{3,2,1,0:T(8,128)S(1)}, u32[]{:S(2)}, u32[]{:S(2)}) collective-permute-start(f32[8,1,16,128]{3,2,1,0:T(8,128)S(1)} %get-tuple-element.53), channel_id=1, source_target_pairs={{0,4},{4,8},{8,12},{1,5},{5,9},{9,13},{2,6},{6,10},{10,14},{3,7},{... | collective-permute-start | bytes 196616 | tf_op jit(solution)/shard_map/ppermute | solution.py:27
  98.4 6.2 %collective-permute-start.6 = (f32[8,1,16,128]{3,2,1,0:T(8,128)S(1)}, f32[8,1,16,128]{3,2,1,0:T(8,128)S(1)}, u32[]{:S(2)}, u32[]{:S(2)}) collective-permute-start(f32[8,1,16,128]{3,2,1,0:T(8,128)S(1)} %get-tuple-element.54), channel_id=1, source_target_pairs={{4,0},{8,4},{12,8},{5,1},{9,5},{13,9},{6,2},{10,6},{14,10},{7,3},{... | collective-permute-start | bytes 196616 | tf_op jit(solution)/shard_map/ppermute | solution.py:29
  104.7 6.0 %collective-permute-start.8 = (f32[8,10,1,128]{3,0,2,1:T(8,128)S(1)}, f32[8,10,1,128]{3,0,2,1:T(8,128)S(1)}, u32[]{:S(2)}, u32[]{:S(2)}) collective-permute-start(f32[8,10,1,128]{3,0,2,1:T(8,128)S(1)} %copy.340), channel_id=1, source_target_pairs={{2,0},{3,1},{6,4},{7,5},{10,8},{11,9},{14,12},{15,13},{18,16},{19,... | collective-permute-start | bytes 122888 | tf_op jit(solution)/shard_map/ppermute | solution.py:29
  106.0 6.2 %collective-permute-start.9 = (f32[8,10,1,128]{3,0,2,1:T(8,128)S(1)}, f32[8,10,1,128]{3,0,2,1:T(8,128)S(1)}, u32[]{:S(2)}, u32[]{:S(2)}) collective-permute-start(f32[8,10,1,128]{3,0,2,1:T(8,128)S(1)} %copy.341), channel_id=1, source_target_pairs={{0,2},{1,3},{4,6},{5,7},{8,10},{9,11},{12,14},{13,15},{16,18},{17,... | collective-permute-start | bytes 122888 | tf_op jit(solution)/shard_map/ppermute | solution.py:27
  114.5 5.6 %collective-permute-start.10 = (f32[8,10,18,1]{2,0,3,1:T(8,128)}, f32[8,10,18,1]{2,0,3,1:T(8,128)S(1)}, u32[]{:S(2)}, u32[]{:S(2)}) collective-permute-start(f32[8,10,18,1]{2,0,3,1:T(8,128)} %copy.268), channel_id=1, source_target_pairs={{1,0},{3,2},{5,4},{7,6},{9,8},{11,10},{13,12},{15,14},{17,16},{19,... | collective-permute-start | bytes 17288 | tf_op jit(solution)/shard_map/ppermute | solution.py:29
  116.4 4.4 %collective-permute-start.11 = (f32[8,10,18,1]{2,0,3,1:T(8,128)S(1)}, f32[8,10,18,1]{2,0,3,1:T(8,128)}, u32[]{:S(2)}, u32[]{:S(2)}) collective-permute-start(f32[8,10,18,1]{2,0,3,1:T(8,128)S(1)} %copy.270), channel_id=1, source_target_pairs={{0,1},{2,3},{4,5},{6,7},{8,9},{10,11},{12,13},{14,15},{16,17},{18,... | collective-permute-start | bytes 17288 | tf_op jit(solution)/shard_map/ppermute | solution.py:27
  153.2 55.1 %copy-start.16 = (f32[8,3]{0,1:T(4,128)}, f32[8,3]{0,1:T(4,128)S(1)}, u32[]{:S(2)}) copy-start(f32[8,3]{0,1:T(4,128)S(1)} %get-tuple-element.23) | copy-start | bytes 292
  165.2 12.3 %all-to-all-start.5 = ((f32[3,4,32,128]{3,1,0,2:T(4,128)}), f32[3,4,32,128]{3,1,0,2:T(4,128)S(1)}, u32[]{:S(2)}, u32[]{:S(2)}) async-start(f32[3,4,32,128]{3,1,0,2:T(4,128)} %copy.281), calls=%async_computation.5 | async-start | bytes 393216 | tf_op jit(solution)/shard_map/all_to_all | solution.py:96
  168.6 17.6 %collective-permute-start.13 = (f32[8,1,16,128]{3,2,1,0:T(8,128)S(1)}, f32[8,1,16,128]{3,2,1,0:T(8,128)S(1)}, u32[]{:S(2)}, u32[]{:S(2)}) collective-permute-start(f32[8,1,16,128]{3,2,1,0:T(8,128)S(1)} %get-tuple-element.51), channel_id=1, source_target_pairs={{0,4},{4,8},{8,12},{1,5},{5,9},{9,13},{2,6},{6,10},{10,14},{3,7},{... | collective-permute-start | bytes 196616 | tf_op jit(solution)/shard_map/ppermute | solution.py:27
  175.5 10.7 %collective-permute-start.12 = (f32[8,1,16,128]{3,2,1,0:T(8,128)S(1)}, f32[8,1,16,128]{3,2,1,0:T(8,128)S(1)}, u32[]{:S(2)}, u32[]{:S(2)}) collective-permute-start(f32[8,1,16,128]{3,2,1,0:T(8,128)S(1)} %get-tuple-element.52), channel_id=1, source_target_pairs={{4,0},{8,4},{12,8},{5,1},{9,5},{13,9},{6,2},{10,6},{14,10},{7,3},{... | collective-permute-start | bytes 196616 | tf_op jit(solution)/shard_map/ppermute | solution.py:29
  178.3 15.8 %all-to-all-start.6 = ((f32[3,8,16,128]{3,1,0,2:T(8,128)}), f32[3,8,16,128]{3,1,0,2:T(8,128)S(1)}, u32[]{:S(2)}, u32[]{:S(2)}) async-start(f32[3,8,16,128]{3,1,0,2:T(8,128)} %copy.284), calls=%async_computation.6 | async-start | bytes 393216 | tf_op jit(solution)/shard_map/all_to_all | solution.py:99
  186.3 5.9 %collective-permute-start.14 = (f32[8,10,1,128]{3,0,2,1:T(8,128)S(1)}, f32[8,10,1,128]{3,0,2,1:T(8,128)S(1)}, u32[]{:S(2)}, u32[]{:S(2)}) collective-permute-start(f32[8,10,1,128]{3,0,2,1:T(8,128)S(1)} %copy.342), channel_id=1, source_target_pairs={{2,0},{3,1},{6,4},{7,5},{10,8},{11,9},{14,12},{15,13},{18,16},{19,... | collective-permute-start | bytes 122888 | tf_op jit(solution)/shard_map/ppermute | solution.py:29
  187.6 6.2 %collective-permute-start.15 = (f32[8,10,1,128]{3,0,2,1:T(8,128)S(1)}, f32[8,10,1,128]{3,0,2,1:T(8,128)S(1)}, u32[]{:S(2)}, u32[]{:S(2)}) collective-permute-start(f32[8,10,1,128]{3,0,2,1:T(8,128)S(1)} %copy.343), channel_id=1, source_target_pairs={{0,2},{1,3},{4,6},{5,7},{8,10},{9,11},{12,14},{13,15},{16,18},{17,... | collective-permute-start | bytes 122888 | tf_op jit(solution)/shard_map/ppermute | solution.py:27
  195.2 15.5 %all-to-all-start.7 = ((f32[3,32,4,128]{3,2,0,1:T(4,128)}), f32[3,32,4,128]{3,2,0,1:T(4,128)S(1)}, u32[]{:S(2)}, u32[]{:S(2)}) async-start(f32[3,32,4,128]{3,2,0,1:T(4,128)} %copy.288), calls=%async_computation.7 | async-start | bytes 393216 | tf_op jit(solution)/shard_map/all_to_all | solution.py:103
  203.3 5.2 %collective-permute-start.16 = (f32[8,10,18,1]{2,0,3,1:T(8,128)S(1)}, f32[8,10,18,1]{2,0,3,1:T(8,128)S(1)}, u32[]{:S(2)}, u32[]{:S(2)}) collective-permute-start(f32[8,10,18,1]{2,0,3,1:T(8,128)S(1)} %copy.301), channel_id=1, source_target_pairs={{1,0},{3,2},{5,4},{7,6},{9,8},{11,10},{13,12},{15,14},{17,16},{19,... | collective-permute-start | bytes 17288 | tf_op jit(solution)/shard_map/ppermute | solution.py:29
  205.2 3.9 %collective-permute-start.17 = (f32[8,10,18,1]{2,0,3,1:T(8,128)S(1)}, f32[8,10,18,1]{2,0,3,1:T(8,128)S(1)}, u32[]{:S(2)}, u32[]{:S(2)}) collective-permute-start(f32[8,10,18,1]{2,0,3,1:T(8,128)S(1)} %copy.303), channel_id=1, source_target_pairs={{0,1},{2,3},{4,5},{6,7},{8,9},{10,11},{12,13},{14,15},{16,17},{18,... | collective-permute-start | bytes 17288 | tf_op jit(solution)/shard_map/ppermute | solution.py:27
  212.8 6.2 %collective-permute-start.19 = (f32[8,1,16,128]{3,2,1,0:T(8,128)S(1)}, f32[8,1,16,128]{3,2,1,0:T(8,128)S(1)}, u32[]{:S(2)}, u32[]{:S(2)}) collective-permute-start(f32[8,1,16,128]{3,2,1,0:T(8,128)S(1)} %get-tuple-element.49), channel_id=1, source_target_pairs={{0,4},{4,8},{8,12},{1,5},{5,9},{9,13},{2,6},{6,10},{10,14},{3,7},{... | collective-permute-start | bytes 196616 | tf_op jit(solution)/shard_map/ppermute | solution.py:27
  216.2 6.2 %collective-permute-start.18 = (f32[8,1,16,128]{3,2,1,0:T(8,128)S(1)}, f32[8,1,16,128]{3,2,1,0:T(8,128)S(1)}, u32[]{:S(2)}, u32[]{:S(2)}) collective-permute-start(f32[8,1,16,128]{3,2,1,0:T(8,128)S(1)} %get-tuple-element.50), channel_id=1, source_target_pairs={{4,0},{8,4},{12,8},{5,1},{9,5},{13,9},{6,2},{10,6},{14,10},{7,3},{... | collective-permute-start | bytes 196616 | tf_op jit(solution)/shard_map/ppermute | solution.py:29
  222.4 6.1 %collective-permute-start.20 = (f32[8,10,1,128]{3,0,2,1:T(8,128)S(1)}, f32[8,10,1,128]{3,0,2,1:T(8,128)S(1)}, u32[]{:S(2)}, u32[]{:S(2)}) collective-permute-start(f32[8,10,1,128]{3,0,2,1:T(8,128)S(1)} %copy.344), channel_id=1, source_target_pairs={{2,0},{3,1},{6,4},{7,5},{10,8},{11,9},{14,12},{15,13},{18,16},{19,... | collective-permute-start | bytes 122888 | tf_op jit(solution)/shard_map/ppermute | solution.py:29
  223.8 6.2 %collective-permute-start.21 = (f32[8,10,1,128]{3,0,2,1:T(8,128)S(1)}, f32[8,10,1,128]{3,0,2,1:T(8,128)S(1)}, u32[]{:S(2)}, u32[]{:S(2)}) collective-permute-start(f32[8,10,1,128]{3,0,2,1:T(8,128)S(1)} %copy.345), channel_id=1, source_target_pairs={{0,2},{1,3},{4,6},{5,7},{8,10},{9,11},{12,14},{13,15},{16,18},{17,... | collective-permute-start | bytes 122888 | tf_op jit(solution)/shard_map/ppermute | solution.py:27
  231.1 4.9 %collective-permute-start.22 = (f32[8,10,18,1]{2,0,3,1:T(8,128)S(1)}, f32[8,10,18,1]{2,0,3,1:T(8,128)S(1)}, u32[]{:S(2)}, u32[]{:S(2)}) collective-permute-start(f32[8,10,18,1]{2,0,3,1:T(8,128)S(1)} %copy.311), channel_id=1, source_target_pairs={{1,0},{3,2},{5,4},{7,6},{9,8},{11,10},{13,12},{15,14},{17,16},{19,... | collective-permute-start | bytes 17288 | tf_op jit(solution)/shard_map/ppermute | solution.py:29
  232.9 3.9 %collective-permute-start.23 = (f32[8,10,18,1]{2,0,3,1:T(8,128)S(1)}, f32[8,10,18,1]{2,0,3,1:T(8,128)S(1)}, u32[]{:S(2)}, u32[]{:S(2)}) collective-permute-start(f32[8,10,18,1]{2,0,3,1:T(8,128)S(1)} %copy.313), channel_id=1, source_target_pairs={{0,1},{2,3},{4,5},{6,7},{8,9},{10,11},{12,13},{14,15},{16,17},{18,... | collective-permute-start | bytes 17288 | tf_op jit(solution)/shard_map/ppermute | solution.py:27
  (18 other events, 141.3 us)
where the time goes:
time: 242 us; the launch traced here: 239 us
  starting transfers between devices  108 us (45%)
  blocking collectives  60.3 us (25%)
  local copies, waits for them, and re-layouts  26 us (11%)
  waiting for transfers between devices  19.7 us (8%)
  matrix products  12.9 us (5%)
  other arithmetic  9.53 us (4%)
  between operations  2.86 us (1%)
    ppermute x12, starting transfers between devices, extended(): lax.ppermute(tail, axis, [(i, (i + 1) % count) for i in range(ends)])  52.1 us
    psum x2, blocking collectives, class_moments(): lax.psum((jnp.sum(flat, axis=1), jnp.dot(flat, values.T, precision=highes...  48.4 us
    ppermute x12, starting transfers between devices, extended(): lax.ppermute(head, axis, [((i + 1) % count, i) for i in range(ends)])  19.1 us
    all_to_all x2, starting transfers between devices, smoothed(): lax.all_to_all(across, 'slab', split_axis=2, concat_axis=1, tiled=True)  16 us
    all_to_all x2, starting transfers between devices, smoothed(): lax.all_to_all(mixed, 'slab', split_axis=1, concat_axis=2, tiled=True)  10.2 us
    slice x8, local copies, waits for them, and re-layouts, extended(): head = lax.slice_in_dim(cells, 0, width, axis=dim)  8.48 us
    ppermute x12, waiting for transfers between devices, extended(): lax.ppermute(head, axis, [((i + 1) % count, i) for i in range(ends)])  8.32 us
    all_to_all x1, blocking collectives, smoothed(): lax.all_to_all(across, 'row', split_axis=1, concat_axis=2, tiled=True)  7.42 us
  transfers between devices with their start and end apart: 31, of which 11 were waited for; matrix products, arithmetic and copies ran while one was open for 7% of the time, Pallas kernels for 0%

commit v1 on v0

--- a/solution.py
+++ b/solution.py
@@ -1,8 +1,12 @@
+import functools
 import math
 
 import jax
 import jax.numpy as jnp
+import numpy as np
 from jax import lax
+from jax.experimental import pallas as pl
+from jax.experimental.pallas import tpu as pltpu
 from jax.sharding import PartitionSpec as P
 
 M = 3
@@ -103,7 +107,7 @@
     return lax.all_to_all(mixed, "slab", split_axis=1, concat_axis=2, tiled=True)
 
 
-def local(image, brain_mask, labels):
+def general(image, brain_mask, labels):
     channels, slabs, rows, columns = image.shape
     inside = brain_mask.astype(jnp.float32)
     kinds = jnp.arange(K, dtype=jnp.int32)
@@ -133,6 +137,465 @@
     return (belief.astype(jnp.bfloat16), bias_field, means)
 
 
+LANES = 128
+SUB = 8
+EDGE = 4
+MARGIN = 8
+STATS = 1 + 2 * M
+
+
+def impulse(length):
+    index = np.arange(length)
+    folded = np.minimum(index, length - index) / length
+    response = np.exp(-2.0 * np.pi**2 * (length / breadth) ** 2 * folded * folded)
+    angles = 2.0 * np.pi / length * (index[:, None] * index[None, :] % length)
+    return np.cos(angles) @ response / length
+
+
+def dense(length):
+    index = np.arange(length)
+    return impulse(length)[(index[:, None] - index[None, :]) % length]
+
+
+def dot(left, right, dims=((1,), (0,))):
+    return lax.dot_general(
+        left, right, (dims, ((), ())), precision=highest, preferred_element_type=jnp.float32
+    )
+
+
+def wide(row, shape=(SUB, LANES)):
+    return jnp.broadcast_to(row, shape)
+
+
+def stat_tile(sums):
+    sub = lax.broadcasted_iota(jnp.int32, (SUB, LANES), 0)
+    lane = lax.broadcasted_iota(jnp.int32, (SUB, LANES), 1)
+    tile = jnp.zeros((SUB, LANES), jnp.float32)
+    for q in range(STATS):
+        rows = jnp.zeros((SUB, LANES), jnp.float32)
+        for k in range(K):
+            line = jnp.sum(sums[k][q], axis=0, keepdims=True)
+            rows = jnp.where(sub == k, line, rows)
+        tile = jnp.where(lane == q, jnp.sum(rows, axis=1, keepdims=True), tile)
+    return tile
+
+
+def fold(x):
+    return jnp.sum(x.reshape(x.shape[0] // SUB, SUB, LANES), axis=0)
+
+
+def class_stats(tile):
+    count = tile[:, 0:1]
+    means, halves = [], []
+    shift = jnp.zeros_like(count)
+    for m in range(M):
+        first = tile[:, 1 + m : 2 + m]
+        squares = tile[:, 1 + M + m : 2 + M + m]
+        mean = first / (count + 1.0)
+        spread = squares - 2.0 * mean * first + mean * mean * count
+        variance = (spread + 1.0) / (count + 1.0)
+        means.append(wide(mean))
+        halves.append(wide(0.5 / variance))
+        shift = shift - 0.5 * jnp.log(variance)
+    prior = (count + 1.0) / (jnp.sum(count, axis=0, keepdims=True) + K)
+    return means, halves, wide(jnp.log(prior) + shift)
+
+
+def mean_rows(tile):
+    return [wide(tile[:, 1 + m : 2 + m] / (tile[:, 0:1] + 1.0)) for m in range(M)]
+
+
+def log_terms(corrected, means, halves, shift):
+    out = []
+    for k in range(K):
+        total = wide(shift[k : k + 1, :], corrected[0].shape)
+        for m in range(M):
+            offset = corrected[m] - means[m][k : k + 1, :]
+            total = total - offset * offset * halves[m][k : k + 1, :]
+        out.append(total)
+    return out
+
+
+def soft(logits, inside):
+    top = functools.reduce(jnp.maximum, logits)
+    exps = [jnp.exp(x - top) for x in logits]
+    scale = inside / functools.reduce(jnp.add, exps)
+    return [x * scale for x in exps]
+
+
+def prepare_kernel(own, oth, place, send, ext):
+    window = send.shape[1] // (M + 1) // SUB * SUB
+    peers = send.shape[0]
+    step = LANES // peers
+    first = jnp.full((SUB, LANES), place[2], jnp.int32) == 0
+    for f in range(M + 1):
+        blank = jnp.full((SUB, LANES), float(K) if f == M else 0.0, jnp.float32)
+        other = oth[f].T
+        ext[f, 0:MARGIN, :] = jnp.where(first, blank, other[LANES - MARGIN :, :])
+        ext[f, MARGIN : MARGIN + LANES, :] = own[f].T
+        ext[f, MARGIN + LANES :, :] = jnp.where(first, other[:MARGIN, :], blank)
+    sums = []
+    for k in range(K):
+        line = [jnp.zeros((SUB, LANES), jnp.float32) for _ in range(STATS)]
+        for ref in (own, oth):
+            flag = (ref[M] == float(k)).astype(jnp.float32)
+            line[0] = line[0] + fold(flag)
+            for m in range(M):
+                value = flag * ref[m]
+                line[1 + m] = line[1 + m] + fold(value)
+                line[1 + M + m] = line[1 + M + m] + fold(value * ref[m])
+        sums.append(line)
+    tile = stat_tile(sums)
+    for p in range(peers):
+        for f in range(M + 1):
+            base = MARGIN - EDGE + step * p
+            send[p, f * window : (f + 1) * window, :] = ext[f, base : base + window, :]
+        send[p, (M + 1) * window :, :] = tile
+
+
+def column_kernel(own, oth, got, table, send, flat, out):
+    peers = send.shape[0]
+    window = send.shape[1] // M
+    step = LANES // peers
+    tile = got[0, (M + 1) * window :, :]
+    for j in range(1, peers):
+        tile = tile + got[j, (M + 1) * window :, :]
+    means = mean_rows(tile)
+    for h, ref in enumerate((own, oth)):
+        code = ref[M]
+        flags = [code == float(k) for k in range(K)]
+        for m in range(M):
+            center = jnp.zeros_like(code)
+            for k in range(K):
+                center = jnp.where(flags[k], means[m][k : k + 1, :], center)
+            flat[m * LANES : (m + 1) * LANES, h * LANES : (h + 1) * LANES] = jnp.where(
+                code < float(K), ref[m] - center, 0.0
+            )
+    out[...] = dot(table[...], flat[...], ((1,), (1,)))
+    for p in range(peers):
+        base = MARGIN - EDGE + step * p
+        for m in range(M):
+            send[p, m * window : (m + 1) * window, :] = out[
+                base : base + window, m * LANES : (m + 1) * LANES
+            ]
+
+
+def slab_row_filter(pieces, slab_table, row_table, first, second, grid):
+    ns, nr = grid
+    rows = pieces[0].shape[0]
+    for sb in range(ns):
+        for rb in range(nr):
+            first[rb * rows : (rb + 1) * rows, sb * LANES : (sb + 1) * LANES] = pieces[sb * nr + rb]
+    mixed = dot(first[...], slab_table[...])
+    for sb in range(ns):
+        for rb in range(nr):
+            second[sb * rows : (sb + 1) * rows, rb * LANES : (rb + 1) * LANES] = mixed[
+                rb * rows : (rb + 1) * rows, sb * LANES : (sb + 1) * LANES
+            ]
+    return dot(second[...], row_table[...])
+
+
+def around(get, sb, rb, grid, rows, fill):
+    ns, nr = grid
+    lane = lax.broadcasted_iota(jnp.int32, (1, LANES), 1)
+    place = lane % rows
+    here = get(sb, rb)
+    empty = jnp.full_like(here, fill)
+    above = get(sb + 1, rb) if sb + 1 < ns else empty
+    below = get(sb - 1, rb) if sb > 0 else empty
+    out = [
+        pltpu.roll(jnp.where(lane >= rows, here, above), LANES - rows, 1),
+        pltpu.roll(jnp.where(lane < LANES - rows, here, below), rows, 1),
+    ]
+    right = pltpu.roll(get(sb, rb + 1), rows - 1, 1) if rb + 1 < nr else empty
+    left = pltpu.roll(get(sb, rb - 1), LANES - rows + 1, 1) if rb > 0 else empty
+    out.append(jnp.where(place < rows - 1, pltpu.roll(here, LANES - 1, 1), right))
+    out.append(jnp.where(place > 0, pltpu.roll(here, 1, 1), left))
+    return out
+
+
+def pencil_kernel(grid, rows, got, raw, slab_table, row_table, send, keep, first, second, bias, dens, one, two):
+    ns, nr = grid
+    peers = ns * nr
+    window = got.shape[1] // M
+    core = window - 2 * EDGE
+    tile = raw[0, (M + 1) * window :, :]
+    for j in range(1, peers):
+        tile = tile + raw[j, (M + 1) * window :, :]
+    means, halves, shift = class_stats(tile)
+    bias[...] = slab_row_filter(
+        [got[j] for j in range(peers)], slab_table, row_table, first, second, grid
+    )
+
+    def shade(sb, rb, m, low=0, size=window):
+        j = sb * nr + rb
+        base = (sb * M + m) * window + low
+        field = raw[j, m * window + low : m * window + low + size, :]
+        return field - bias[base : base + size, rb * LANES : (rb + 1) * LANES]
+
+    def code_at(sb, rb):
+        return raw[sb * nr + rb, M * window : (M + 1) * window, :]
+
+    for sb in range(ns):
+        for rb in range(nr):
+            j = sb * nr + rb
+            logits = log_terms([shade(sb, rb, m) for m in range(M)], means, halves, shift)
+            code = code_at(sb, rb)
+            near = around(code_at, sb, rb, grid, rows, float(K))
+            near = near + [pltpu.roll(code, 1, 0), pltpu.roll(code, window - 1, 0)]
+            for k in range(K):
+                dens[k, j] = logits[k]
+                for x in near:
+                    logits[k] = logits[k] + (x == float(k)).astype(jnp.float32)
+            inside = (code < float(K)).astype(jnp.float32)
+            for k, value in enumerate(soft(logits, inside)):
+                one[k, j] = value
+    for sb in range(ns):
+        for rb in range(nr):
+            j = sb * nr + rb
+            logits = []
+            for k in range(K):
+                here = one[k, j]
+                near = around(lambda a, b: one[k, a * nr + b], sb, rb, grid, rows, 0.0)
+                near = near + [pltpu.roll(here, 1, 0), pltpu.roll(here, window - 1, 0)]
+                logits.append(dens[k, j] + functools.reduce(jnp.add, near))
+            inside = (code_at(sb, rb) < float(K)).astype(jnp.float32)
+            for k, value in enumerate(soft(logits, inside)):
+                two[k, j] = value
+    sums = [[jnp.zeros((SUB, LANES), jnp.float32) for _ in range(STATS)] for _ in range(K)]
+    for sb in range(ns):
+        for rb in range(nr):
+            j = sb * nr + rb
+            values = [shade(sb, rb, m, EDGE, core) for m in range(M)]
+            for k in range(K):
+                here = two[k, j, EDGE : EDGE + core, :]
+                keep[k, j] = here
+                line = sums[k]
+                line[0] = line[0] + fold(here)
+                for m in range(M):
+                    value = here * values[m]
+                    line[1 + m] = line[1 + m] + fold(value)
+                    line[1 + M + m] = line[1 + M + m] + fold(value * values[m])
+                near = around(
+                    lambda a, b: two[k, a * nr + b, EDGE : EDGE + core, :], sb, rb, grid, rows, 0.0
+                )
+                near = near + [
+                    two[k, j, EDGE - 1 : EDGE - 1 + core, :],
+                    two[k, j, EDGE + 1 : EDGE + 1 + core, :],
+                ]
+                send[j, k * core : (k + 1) * core, :] = functools.reduce(jnp.add, near)
+    tile = stat_tile(sums)
+    for p in range(peers):
+        send[p, K * core :, :] = tile
+
+
+def residual_kernel(grid, stat_a, stat_b, keep, raw, slab_table, row_table, send, first, second):
+    ns, nr = grid
+    core = keep.shape[2]
+    window = core + 2 * EDGE
+    means = mean_rows(stat_a[...] + stat_b[...])
+    pieces = []
+    for j in range(ns * nr):
+        parts = []
+        for m in range(M):
+            field = raw[j, m * window + EDGE : m * window + EDGE + core, :]
+            total = jnp.zeros_like(field)
+            for k in range(K):
+                total = total + keep[k, j] * (field - means[m][k : k + 1, :])
+            parts.append(total)
+        pieces.append(jnp.concatenate(parts, axis=0))
+    done = slab_row_filter(pieces, slab_table, row_table, first, second, grid)
+    rows = M * core
+    for sb in range(ns):
+        for rb in range(nr):
+            send[sb * nr + rb] = done[sb * rows : (sb + 1) * rows, rb * LANES : (rb + 1) * LANES]
+
+
+def third_kernel(rows, got, oth, near, own, stat_a, stat_b, table, place, bias, centers, dens, belief, up, down, side, edge):
+    peers = got.shape[0]
+    core = got.shape[1] // M
+    tile = stat_a[...] + stat_b[...]
+    means, halves, shift = class_stats(tile)
+    centers[...] = tile[:, 1 : 1 + M] / (tile[:, 0:1] + 1.0)
+    corrected = []
+    for m in range(M):
+        mine = got[:, m * core : (m + 1) * core, :].reshape(LANES, LANES).T
+        yours = oth[:, m * core : (m + 1) * core, :].reshape(LANES, LANES).T
+        field = dot(jnp.concatenate([mine, yours], axis=1), table[...])
+        bias[m] = field
+        corrected.append(own[m] - field)
+    logits = log_terms(corrected, means, halves, shift)
+    for k in range(K):
+        dens[k] = logits[k]
+        logits[k] = logits[k] + near[:, k * core : (k + 1) * core, :].reshape(LANES, LANES).T
+    inside = (own[M] < float(K)).astype(jnp.float32)
+    lane = lax.broadcasted_iota(jnp.int32, (1, LANES), 1)
+    odd = place[0] % 2
+    column = jnp.zeros((LANES, LANES), jnp.float32)
+    for k, value in enumerate(soft(logits, inside)):
+        belief[k] = value
+        low = value[:rows, :]
+        high = value[LANES - rows :, :]
+        even = jnp.full(low.shape, odd, jnp.int32) == 0
+        up[k] = jnp.where(even, high, low)
+        down[k] = jnp.where(even, low, high)
+        amount = jnp.where(place[2] == 0, k + 1, k)
+        column = jnp.where(lane == k, pltpu.roll(value, amount, 1), column)
+    edge[...] = column
+    lead = jnp.full((LANES // rows, LANES), place[1], jnp.int32) == 0
+    for k in range(K):
+        head = belief[k, pl.ds(0, LANES // rows, rows), :]
+        tail = belief[k, pl.ds(rows - 1, LANES // rows, rows), :]
+        side[k] = jnp.where(lead, tail, head)
+
+
+def last_kernel(rows, dens, belief, own, up, down, side, edge, place, post):
+    lane = lax.broadcasted_iota(jnp.int32, (1, LANES), 1)
+    line = lax.broadcasted_iota(jnp.int32, (LANES, 1), 0) % rows
+    even = jnp.full((rows, LANES), place[0] % 2, jnp.int32) == 0
+    spot = jnp.where(place[2] == 0, LANES - 1, 0)
+    face = jnp.where(place[1] == 0, rows - 1, 0)
+    column = edge[...]
+    logits = []
+    for k in range(K):
+        here = belief[k]
+        high = jnp.where(even, up[k], down[k])
+        low = jnp.where(even, down[k], up[k])
+        total = jnp.concatenate([low, here[: LANES - rows, :]], axis=0)
+        total = total + jnp.concatenate([here[rows:, :], high], axis=0)
+        beside = jnp.broadcast_to(side[k][:, None, :], (LANES // rows, rows, LANES))
+        total = total + jnp.where(line == face, beside.reshape(LANES, LANES), 0.0)
+        total = total + jnp.where(line > 0, pltpu.roll(here, 1, 0), 0.0)
+        total = total + jnp.where(line < rows - 1, pltpu.roll(here, LANES - 1, 0), 0.0)
+        shifted = pltpu.roll(column, jnp.where(place[2] == 0, LANES - 1 - k, (LANES - k) % LANES), 1)
+        total = total + jnp.where(lane == spot, shifted, 0.0)
+        total = total + jnp.where(lane > 0, pltpu.roll(here, 1, 1), 0.0)
+        total = total + jnp.where(lane < LANES - 1, pltpu.roll(here, LANES - 1, 1), 0.0)
+        logits.append(dens[k] + total)
+    inside = (own[M] < float(K)).astype(jnp.float32)
+    for k, value in enumerate(soft(logits, inside)):
+        post[k] = value.astype(jnp.bfloat16)
+
+
+def call(kernel, outs, scratch=(), scalars=()):
+    vmem = pl.BlockSpec(memory_space=pltpu.VMEM)
+    smem = pl.BlockSpec(memory_space=pltpu.SMEM)
+    shapes = [jax.ShapeDtypeStruct(shape, kind) for shape, kind in outs]
+
+    def run(*args):
+        return pl.pallas_call(
+            kernel,
+            out_shape=shapes,
+            in_specs=[smem if i in scalars else vmem for i in range(len(args))],
+            out_specs=[vmem] * len(shapes),
+            scratch_shapes=[pltpu.VMEM(shape, jnp.float32) for shape in scratch],
+            name=(kernel.func if isinstance(kernel, functools.partial) else kernel).__name__,
+        )(*args)
+
+    return run
+
+
+def pencils(image, brain_mask, labels):
+    _, slabs, rows, columns = image.shape
+    ns, nr, nc = (lax.axis_size(a) for a in ("slab", "row", "col"))
+    grid = (ns, nr)
+    peers = ns * nr
+    core = columns // peers
+    window = core + 2 * EDGE
+    f32 = jnp.float32
+    place = jnp.stack([lax.axis_index(a) for a in ("slab", "row", "col")]).astype(jnp.int32)
+    swap = [(0, 1), (1, 0)]
+
+    taps = impulse(columns * nc)
+    reach = np.arange(-MARGIN, columns + MARGIN)
+    source = np.concatenate([np.arange(columns), np.arange(columns) + columns])
+    spread = taps[(reach[:, None] - source[None, :]) % (columns * nc)].astype(np.float32)
+    gather = np.ascontiguousarray(spread[MARGIN : MARGIN + columns].T)
+    slab_table = np.kron(dense(slabs * ns), np.eye(rows)).astype(np.float32)
+    row_table = np.einsum(
+        "arbq,st->asrbtq", dense(rows * nr).reshape(nr, rows, nr, rows), np.eye(slabs)
+    )
+    row_table = row_table.reshape(nr * LANES, nr * LANES).astype(np.float32)
+
+    code = jnp.where(brain_mask > 0, labels, K).astype(f32)
+    own = jnp.concatenate([image, code[None]]).reshape(M + 1, LANES, columns)
+    oth = lax.ppermute(own, "col", swap)
+
+    def trade(x):
+        return lax.all_to_all(x, ("slab", "row"), split_axis=0, concat_axis=0, tiled=True)
+
+    (sent,) = call(
+        prepare_kernel,
+        [((peers, (M + 1) * window + SUB, LANES), f32)],
+        [(M + 1, columns + 2 * MARGIN, LANES)],
+        (2,),
+    )(own, oth, place)
+    raw = trade(sent)
+    (sent,) = call(
+        column_kernel,
+        [((peers, M * window, LANES), f32)],
+        [(M * LANES, 2 * columns), (columns + 2 * MARGIN, M * LANES)],
+    )(own, oth, raw, spread)
+    got = trade(sent)
+    sent, keep = call(
+        functools.partial(pencil_kernel, grid, rows),
+        [((peers, K * core + SUB, LANES), f32), ((K, peers, core, LANES), f32)],
+        [
+            (nr * M * window, ns * LANES),
+            (ns * M * window, nr * LANES),
+            (ns * M * window, nr * LANES),
+            (K, peers, window, LANES),
+            (K, peers, window, LANES),
+            (K, peers, window, LANES),
+        ],
+    )(got, raw, slab_table, row_table)
+    near = trade(sent)
+    stat_a = jnp.sum(near[:, K * core :, :], axis=0)
+    stat_b = lax.ppermute(stat_a, "col", swap)
+    (sent,) = call(
+        functools.partial(residual_kernel, grid),
+        [((peers, M * core, LANES), f32)],
+        [(nr * M * core, ns * LANES), (ns * M * core, nr * LANES)],
+    )(stat_a, stat_b, keep, raw, slab_table, row_table)
+    got = trade(sent)
+    yours = lax.ppermute(got, "col", swap)
+    bias, centers, dens, belief, up, down, side, edge = call(
+        functools.partial(third_kernel, rows),
+        [
+            ((M, LANES, columns), f32),
+            ((K, M), f32),
+            ((K, LANES, columns), f32),
+            ((K, LANES, columns), f32),
+            ((K, rows, columns), f32),
+            ((K, rows, columns), f32),
+            ((K, slabs, columns), f32),
+            ((LANES, LANES), f32),
+        ],
+        (),
+        (7,),
+    )(got, yours, near, own, stat_a, stat_b, gather, place)
+    pairs = [(i, i + 1) for i in range(0, ns - 1, 2)]
+    between = [(i, i + 1) for i in range(1, ns - 1, 2)]
+    up = lax.ppermute(up, "slab", pairs + [(b, a) for a, b in pairs])
+    down = lax.ppermute(down, "slab", between + [(b, a) for a, b in between])
+    side = lax.ppermute(side, "row", swap)
+    edge = lax.ppermute(edge, "col", swap)
+    (post,) = call(
+        functools.partial(last_kernel, rows), [((K, LANES, columns), jnp.bfloat16)], (), (7,)
+    )(dens, belief, own, up, down, side, edge, place)
+    shape = (slabs, rows, columns)
+    return post.reshape((K,) + shape), bias.reshape((M,) + shape), centers
+
+
+def local(image, brain_mask, labels):
+    _, slabs, rows, columns = image.shape
+    peers = lax.axis_size("slab") * lax.axis_size("row")
+    fits = slabs * rows == LANES and columns == LANES and slabs % SUB == 0 and rows % SUB == 0
+    fits = fits and lax.axis_size("row") == 2 and lax.axis_size("col") == 2
+    fits = fits and columns % (SUB * peers) == 0
+    return (pencils if fits else general)(image, brain_mask, labels)
+
+
 def solution(mesh):
     placed = (
         P(None, ("grp", "slab"), "row", "col"),

time: 242 us -> 100 us (0.41)
  starting transfers between devices: 108 us -> 6 us
  local copies, waits for them, and re-layouts: 26 us -> 3.35 us
  Pallas kernels: 0 us -> 20.9 us
  waiting for transfers between devices: 19.7 us -> 5.97 us
  matrix products: 12.9 us -> 0 us
  other arithmetic: 9.53 us -> 1.6 us
    ppermute x24 -> x7, starting transfers between devices: 71.1 us -> 6 us  [the longest x1 4.11 us: pencils(): down = lax.ppermute(down, 'slab', between + [(b, a) for a, b in between])]
    all_to_all x1 -> x4, blocking collectives: 7.42 us -> 60.8 us  [trade(): lax.all_to_all(x, ('slab', 'row'), split_axis=0, concat_axis=0, tiled=True)]
    psum x2 -> x0, blocking collectives: 48.4 us -> none  [class_moments(): lax.psum((jnp.sum(flat, axis=1), jnp.dot(flat, values.T, precision=highes...]
    all_to_all x7 -> x0, starting transfers between devices: 36.5 us -> none  [the longest x2 16 us: smoothed(): lax.all_to_all(across, 'slab', split_axis=2, concat_axis=1, tiled=True)]
    pallas_call x0 -> x6, Pallas kernels: none -> 20.9 us  [run(): pl.pallas_call(kernel, out_shape=shapes, in_specs=[smem if i in scalars e...]
    dot_general x16 -> x0, matrix products: 12.9 us -> none  [the longest x2 2.73 us: class_moments(): jnp.dot(flat, values.T, precision=highest)]
    slice x16 -> x0, local copies, waits for them, and re-layouts: 10.8 us -> none  [the longest x8 8.48 us: extended(): head = lax.slice_in_dim(cells, 0, width, axis=dim)]
    ppermute x24 -> x7, waiting for transfers between devices: 15.2 us -> 5.97 us  [the longest x1 2.5 us: pencils(): side = lax.ppermute(side, 'row', swap)]
  transfers between devices with their start and end apart: 31 -> 7, of which waited for: 11 -> 4; matrix products, arithmetic and copies ran while one was open for 7% -> 1% of each run, Pallas kernels for 0% -> 0%
where the time goes in v1:
time: 100 us; the launch traced here: 99.4 us
  blocking collectives  60.8 us (61%)
  Pallas kernels  20.9 us (21%)
  starting transfers between devices  6 us (6%)
  waiting for transfers between devices  5.97 us (6%)
  local copies, waits for them, and re-layouts  3.35 us (3%)
  other arithmetic  1.6 us (2%)
    all_to_all x4, blocking collectives, trade(): lax.all_to_all(x, ('slab', 'row'), split_axis=0, concat_axis=0, tiled=True)  60.8 us
    pallas_call x6, Pallas kernels, run(): pl.pallas_call(kernel, out_shape=shapes, in_specs=[smem if i in scalars e...  20.9 us
    ppermute x1, starting transfers between devices, pencils(): down = lax.ppermute(down, 'slab', between + [(b, a) for a, b in between])  4.11 us
    unnamed x27, local copies, waits for them, and re-layouts  3.35 us
    ppermute x1, waiting for transfers between devices, pencils(): side = lax.ppermute(side, 'row', swap)  2.5 us
  transfers between devices with their start and end apart: 7, of which 4 were waited for; matrix products, arithmetic and copies ran while one was open for 1% of the time, Pallas kernels for 0%

profile of v1, /device:TPU:16, one launch (start us, length us, event | category | flops | bytes accessed | tf_op | source)
XLA Modules:
  0.0 99.4 jit_solution(16206781798229882102)
XLA Ops:
  0.6 0.9 select_convert_fusion
  1.6 0.1 copy-done.5
  1.7 0.1 collective-permute-start
  1.7 0.6 pad_add_fusion.place
  2.4 0.9 collective-permute-done.oth
  3.3 0.7 copy-done.2
  4.0 2.6 %prepare_kernel.1 = f32[8,104,128]{2,1,0:T(8,128)} custom-call(f32[4,128,128]{2,1,0:T(8,128)} %copy-done, f32[4,128,128]{2,1,0:T(8,128)} %copy-done.2, s32[3]{0:T(128)} %pad_add_fusion.place), custom_call_target="tpu_custom_call" | custom-call | tf_op jit(solution)/shard_map/prepare_kernel/pallas_call | solution.py:486
  6.6 17.2 %all_to_all.20.got.raw = f32[8,104,128]{2,1,0:T(8,128)} all-to-all(f32[8,104,128]{2,1,0:T(8,128)} %prepare_kernel.1), channel_id=1, replica_groups=mesh['grp'=2,'slab'=4,'row'=2,'col'=2] {'slab','row'}, dimensions={0} | all-to-all | bytes 851968 | tf_op jit(solution)/shard_map/all_to_all | solution.py:525
  23.8 2.8 %column_kernel.1 = f32[8,72,128]{2,1,0:T(8,128)} custom-call(f32[4,128,128]{2,1,0:T(8,128)} %copy-done, f32[4,128,128]{2,1,0:T(8,128)} %copy-done.2, f32[8,104,128]{2,1,0:T(8,128)} %all_to_all.20.got.raw, f32[144,256]{1,0:T(8,128)} %constant.25.clone.table), custom_call_target="tpu_custom_call" | custom-call | tf_op jit(solution)/shard_map/column_kernel/pallas_call | solution.py:486
  26.7 13.3 %all_to_all.21.got = f32[8,72,128]{2,1,0:T(8,128)} all-to-all(f32[8,72,128]{2,1,0:T(8,128)} %column_kernel.1), channel_id=1, replica_groups=mesh['grp'=2,'slab'=4,'row'=2,'col'=2] {'slab','row'}, dimensions={0} | all-to-all | bytes 589824 | tf_op jit(solution)/shard_map/all_to_all | solution.py:525
  39.9 5.9 %pencil_kernel.1 = (f32[8,136,128]{2,1,0:T(8,128)}, f32[8,8,16,128]{3,2,1,0:T(8,128)}) custom-call(f32[8,72,128]{2,1,0:T(8,128)} %all_to_all.21.got, f32[8,104,128]{2,1,0:T(8,128)} %all_to_all.20.got.raw, f32[512,512]{1,0:T(8,128)} %constant.26.clone.slab_table, f32[256,256]{1,0:T(8,128)} %constant.27.clone.row_table), custom_call_target="tpu_custom_call" | custom-call | tf_op jit(solution)/shard_map/pencil_kernel/pallas_call | solution.py:486
  45.8 18.4 %all_to_all.22.near = f32[8,136,128]{2,1,0:T(8,128)S(1)} all-to-all(f32[8,136,128]{2,1,0:T(8,128)} %get-tuple-element.13), channel_id=1, replica_groups=mesh['grp'=2,'slab'=4,'row'=2,'col'=2] {'slab','row'}, dimensions={0} | all-to-all | bytes 1114112 | tf_op jit(solution)/shard_map/all_to_all | solution.py:525
  64.2 0.1 collective-permute-start.1
  64.3 1.2 %collective-permute-done.1.stat_b = f32[8,128]{1,0:T(8,128)S(1)} collective-permute-done((f32[8,128]{1,0:T(8,128)S(1)}, f32[8,128]{1,0:T(8,128)S(1)}, u32[]{:S(2)}, u32[]{:S(2)}) %collective-permute-start.1) | collective-permute-done | bytes 4128 | tf_op jit(solution)/shard_map/ppermute | solution.py:554
  65.5 0.6 copy-done.11
  66.0 3.4 %residual_kernel.1 = f32[8,48,128]{2,1,0:T(8,128)} custom-call(f32[8,128]{1,0:T(8,128)} %copy-done.9, f32[8,128]{1,0:T(8,128)} %copy-done.11, f32[8,8,16,128]{3,2,1,0:T(8,128)} %get-tuple-element.14.keep, f32[8,104,128]{2,1,0:T(8,128)} %all_to_all.20.got.raw, f32[512,512]{1,0:T(8,128)} %constant.26.clone.slab_table, f32[256,256]{1,0:T(8,128)} %constant.27.clone.row_table), custom_call_target="tpu_custom_call" | custom-call | tf_op jit(solution)/shard_map/residual_kernel/pallas_call | solution.py:486
  69.5 11.9 %all_to_all.23.got = f32[8,48,128]{2,1,0:T(8,128)S(1)} all-to-all(f32[8,48,128]{2,1,0:T(8,128)} %residual_kernel.1), channel_id=1, replica_groups=mesh['grp'=2,'slab'=4,'row'=2,'col'=2] {'slab','row'}, dimensions={0} | all-to-all | bytes 393216 | tf_op jit(solution)/shard_map/all_to_all | solution.py:525
  81.4 0.0 collective-permute-start.2
  81.4 1.4 %collective-permute-done.2.oth = f32[8,48,128]{2,1,0:T(8,128)S(1)} collective-permute-done((f32[8,48,128]{2,1,0:T(8,128)S(1)}, f32[8,48,128]{2,1,0:T(8,128)S(1)}, u32[]{:S(2)}, u32[]{:S(2)}) %collective-permute-start.2) | collective-permute-done | bytes 196640 | tf_op jit(solution)/shard_map/ppermute | solution.py:561
  82.8 0.7 copy-done.4
  83.5 3.5 %third_kernel.1 = (f32[3,128,128]{2,1,0:T(8,128)}, f32[8,3]{1,0:T(8,128)}, f32[8,128,128]{2,1,0:T(8,128)}, f32[8,128,128]{2,1,0:T(8,128)}, f32[8,16,128]{2,1,0:T...) custom-call(f32[8,48,128]{2,1,0:T(8,128)} %copy-done.3, f32[8,48,128]{2,1,0:T(8,128)} %copy-done.4, ...), custom_call_target="tpu_custom_call" | custom-call | tf_op jit(solution)/shard_map/third_kernel/pallas_call | solution.py:486
  87.0 0.6 collective-permute-start.3
  87.6 4.1 %collective-permute-start.4 = (f32[8,16,128]{2,1,0:T(8,128)}, f32[8,16,128]{2,1,0:T(8,128)S(1)}, u32[]{:S(2)}, u32[]{:S(2)}) collective-permute-start(f32[8,16,128]{2,1,0:T(8,128)} %get-tuple-element.18), channel_id=1, source_target_pairs={{4,8},{8,4},{5,9},{9,5},{6,10},{10,6},{7,11},{11,7},{20,24},{24,20... | collective-permute-start | bytes 196616 | tf_op jit(solution)/shard_map/ppermute | solution.py:580
  91.7 0.1 collective-permute-start.6
  91.8 1.0 %collective-permute-start.5 = (f32[8,8,128]{2,1,0:T(8,128)}, f32[8,8,128]{2,1,0:T(8,128)S(1)}, u32[]{:S(2)}, u32[]{:S(2)}) collective-permute-start(f32[8,8,128]{2,1,0:T(8,128)} %get-tuple-element.19), channel_id=1, source_target_pairs={{0,2},{2,0},{1,3},{3,1},{4,6},{6,4},{5,7},{7,5},{8,10},{10,8},{9,1... | collective-permute-start | bytes 98312 | tf_op jit(solution)/shard_map/ppermute | solution.py:581
  92.9 0.7 copy.10
  93.5 2.5 %collective-permute-done.5.side = f32[8,8,128]{2,1,0:T(8,128)S(1)} collective-permute-done((f32[8,8,128]{2,1,0:T(8,128)}, f32[8,8,128]{2,1,0:T(8,128)S(1)}, u32[]{:S(2)}, u32[]{:S(2)}) %collective-permute-start.5) | collective-permute-done | bytes 32800 | tf_op jit(solution)/shard_map/ppermute | solution.py:581
  96.1 0.6 copy-done.10
  96.6 0.0 copy-done.6
  96.7 0.0 copy-done.7
  96.7 0.0 copy-done.8
  96.7 2.6 %last_kernel.1 = bf16[8,128,128]{2,1,0:T(8,128)(2,1)} custom-call(f32[8,128,128]{2,1,0:T(8,128)} %get-tuple-element.15.dens, f32[8,128,128]{2,1,0:T(8,128)} %get-tuple-element.16.belief, f32[4,128,128]{2,1,0:T(8,128)} %copy-done, f32[8,16,128]{2,1,0:T(8,128)} %copy-done.6, f32[8,16,128]{2,1,0:T(8,128)} %copy-done.7, f32[8,8,128]{2,1,0:T(8,128)} %copy-done.10, ...), custom_call_target="tpu_custom_call" | custom-call | tf_op jit(solution)/shard_map/last_kernel/pallas_call | solution.py:486
  (23 shorter events, 0.1 us)
Async XLA Ops:
  0.6 1.0 copy-start.5
  1.6 1.6 %copy-start = (f32[4,128,128]{2,1,0:T(8,128)}, f32[4,128,128]{2,1,0:T(8,128)S(1)}, u32[]{:S(2)}) copy-start(f32[4,128,128]{2,1,0:T(8,128)S(1)} %pad_maximum_fusion.own) | copy-start | bytes 786436
  1.7 1.6 %collective-permute-start = (f32[4,128,128]{2,1,0:T(8,128)S(1)}, f32[4,128,128]{2,1,0:T(8,128)S(1)}, u32[]{:S(2)}, u32[]{:S(2)}) collective-permute-start(f32[4,128,128]{2,1,0:T(8,128)S(1)} %pad_maximum_fusion.own), channel_id=1, source_target_pairs={{0,1},{1,0},{2,3},{3,2},{4,5},{5,4},{6,7},{7,6},{8,9},{9,8},{10,11... | collective-permute-start | bytes 786440 | tf_op jit(solution)/shard_map/ppermute | solution.py:522
  3.3 0.7 copy-start.2
  64.2 5.3 %copy-start.1 = (f32[8,136,128]{2,1,0:T(8,128)}, f32[8,136,128]{2,1,0:T(8,128)S(1)}, u32[]{:S(2)}) copy-start(f32[8,136,128]{2,1,0:T(8,128)S(1)} %all_to_all.22.near) | copy-start | bytes 1671172
  64.2 1.2 %copy-start.9 = (f32[8,128]{1,0:T(8,128)}, f32[8,128]{1,0:T(8,128)S(1)}, u32[]{:S(2)}) copy-start(f32[8,128]{1,0:T(8,128)S(1)} %slice_reduce_fusion.stat_a) | copy-start | bytes 12292
  64.2 1.2 %collective-permute-start.1 = (f32[8,128]{1,0:T(8,128)S(1)}, f32[8,128]{1,0:T(8,128)S(1)}, u32[]{:S(2)}, u32[]{:S(2)}) collective-permute-start(f32[8,128]{1,0:T(8,128)S(1)} %slice_reduce_fusion.stat_a), channel_id=1, source_target_pairs={{0,1},{1,0},{2,3},{3,2},{4,5},{5,4},{6,7},{7,6},{8,9},{9,8},{10,11... | collective-permute-start | bytes 12296 | tf_op jit(solution)/shard_map/ppermute | solution.py:554
  65.4 0.6 copy-start.11
  81.4 1.4 %copy-start.3 = (f32[8,48,128]{2,1,0:T(8,128)}, f32[8,48,128]{2,1,0:T(8,128)S(1)}, u32[]{:S(2)}) copy-start(f32[8,48,128]{2,1,0:T(8,128)S(1)} %all_to_all.23.got) | copy-start | bytes 589828
  81.4 1.4 %collective-permute-start.2 = (f32[8,48,128]{2,1,0:T(8,128)S(1)}, f32[8,48,128]{2,1,0:T(8,128)S(1)}, u32[]{:S(2)}, u32[]{:S(2)}) collective-permute-start(f32[8,48,128]{2,1,0:T(8,128)S(1)} %all_to_all.23.got), channel_id=1, source_target_pairs={{0,1},{1,0},{2,3},{3,2},{4,5},{5,4},{6,7},{7,6},{8,9},{9,8},{10,11... | collective-permute-start | bytes 589832 | tf_op jit(solution)/shard_map/ppermute | solution.py:561
  82.8 0.7 copy-start.4
  87.0 5.9 %copy-start.12 = (f32[8,3]{1,0:T(8,128)S(1)}, f32[8,3]{1,0:T(8,128)}, u32[]{:S(2)}) copy-start(f32[8,3]{1,0:T(8,128)} %get-tuple-element.25) | copy-start | bytes 292
  87.0 9.0 %collective-permute-start.3 = (f32[8,16,128]{2,1,0:T(8,128)}, f32[8,16,128]{2,1,0:T(8,128)S(1)}, u32[]{:S(2)}, u32[]{:S(2)}) collective-permute-start(f32[8,16,128]{2,1,0:T(8,128)} %get-tuple-element.17), channel_id=1, source_target_pairs={{0,4},{8,12},{4,0},{12,8},{1,5},{9,13},{5,1},{13,9},{2,6},{10,14},... | collective-permute-start | bytes 196616 | tf_op jit(solution)/shard_map/ppermute | solution.py:579
  87.6 8.4 %collective-permute-start.4 = (f32[8,16,128]{2,1,0:T(8,128)}, f32[8,16,128]{2,1,0:T(8,128)S(1)}, u32[]{:S(2)}, u32[]{:S(2)}) collective-permute-start(f32[8,16,128]{2,1,0:T(8,128)} %get-tuple-element.18), channel_id=1, source_target_pairs={{4,8},{8,4},{5,9},{9,5},{6,10},{10,6},{7,11},{11,7},{20,24},{24,20... | collective-permute-start | bytes 196616 | tf_op jit(solution)/shard_map/ppermute | solution.py:580
  91.7 4.3 %collective-permute-start.6 = (f32[128,128]{1,0:T(8,128)}, f32[128,128]{1,0:T(8,128)S(1)}, u32[]{:S(2)}, u32[]{:S(2)}) collective-permute-start(f32[128,128]{1,0:T(8,128)} %get-tuple-element.20), channel_id=1, source_target_pairs={{0,1},{1,0},{2,3},{3,2},{4,5},{5,4},{6,7},{7,6},{8,9},{9,8},{10,11... | collective-permute-start | bytes 196616 | tf_op jit(solution)/shard_map/ppermute | solution.py:582
  91.8 4.2 %collective-permute-start.5 = (f32[8,8,128]{2,1,0:T(8,128)}, f32[8,8,128]{2,1,0:T(8,128)S(1)}, u32[]{:S(2)}, u32[]{:S(2)}) collective-permute-start(f32[8,8,128]{2,1,0:T(8,128)} %get-tuple-element.19), channel_id=1, source_target_pairs={{0,2},{2,0},{1,3},{3,1},{4,6},{6,4},{5,7},{7,5},{8,10},{10,8},{9,1... | collective-permute-start | bytes 98312 | tf_op jit(solution)/shard_map/ppermute | solution.py:581
  96.0 0.6 copy-start.10
  96.0 0.6 copy-start.6
  96.0 0.6 copy-start.7
  96.1 0.7 copy-start.8

commit v2 on v1

--- a/solution.py
+++ b/solution.py
@@ -142,6 +142,7 @@
 EDGE = 4
 MARGIN = 8
 STATS = 1 + 2 * M
+VMEM_BYTES = 16 * 2**20
 
 
 def impulse(length):
@@ -489,6 +490,7 @@
             in_specs=[smem if i in scalars else vmem for i in range(len(args))],
             out_specs=[vmem] * len(shapes),
             scratch_shapes=[pltpu.VMEM(shape, jnp.float32) for shape in scratch],
+            compiler_params=pltpu.CompilerParams(vmem_limit_bytes=VMEM_BYTES),
             name=(kernel.func if isinstance(kernel, functools.partial) else kernel).__name__,
         )(*args)
 

time: 100 us -> 85.9 us (0.86)
  Pallas kernels: 20.9 us -> 11.2 us
  local copies, waits for them, and re-layouts: 3.35 us -> 0.73 us
  blocking collectives: 60.8 us -> 59.7 us
    pallas_call x6, Pallas kernels: 20.9 us -> 11.2 us  [run(): pl.pallas_call(kernel, out_shape=shapes, in_specs=[smem if i in scalars e...]
    unnamed x27 -> x11, local copies, waits for them, and re-layouts: 3.35 us -> 0.73 us
    all_to_all x4, blocking collectives: 60.8 us -> 59.7 us  [trade(): lax.all_to_all(x, ('slab', 'row'), split_axis=0, concat_axis=0, tiled=True)]
where the time goes in v2:
time: 85.9 us; the launch traced here: 85.6 us
  blocking collectives  59.7 us (69%)
  Pallas kernels  11.2 us (13%)
  waiting for transfers between devices  6.35 us (7%)
  starting transfers between devices  5.87 us (7%)
  other arithmetic  1.02 us (1%)
    all_to_all x4, blocking collectives, trade(): lax.all_to_all(x, ('slab', 'row'), split_axis=0, concat_axis=0, tiled=True)  59.7 us
    pallas_call x6, Pallas kernels, run(): pl.pallas_call(kernel, out_shape=shapes, in_specs=[smem if i in scalars e...  11.2 us
    ppermute x1, starting transfers between devices, pencils(): down = lax.ppermute(down, 'slab', between + [(b, a) for a, b in between])  4.13 us
    ppermute x1, waiting for transfers between devices, pencils(): side = lax.ppermute(side, 'row', swap)  2.3 us
  transfers between devices with their start and end apart: 7, of which 4 were waited for; matrix products, arithmetic and copies ran while one was open for 1% of the time, Pallas kernels for 0%

profile of v2, /device:TPU:16, one launch (start us, length us, event | category | flops | bytes accessed | tf_op | source)
XLA Modules:
  0.0 85.6 jit_solution(10490284307146943483)
XLA Ops:
  0.6 0.0 copy-start.4
  0.6 0.9 %select_convert_fusion = f32[8,16,128]{2,1,0:T(8,128)S(1)} fusion(s32[8,16,128]{2,1,0:T(8,128)} %param.9, s32[8,16,128]{2,1,0:T(8,128)} %param.8), kind=kLoop, calls=%fused_computation.1 | loop fusion | flops 49152 | bytes 196608 | tf_op jit(solution)/shard_map/convert_element_type | solution.py:522
  1.6 0.1 copy-done.4
  1.6 0.1 collective-permute-start
  1.7 0.1 pad_add_fusion.place
  1.8 1.4 %collective-permute-done.oth = f32[4,128,128]{2,1,0:T(8,128)S(1)} collective-permute-done((f32[4,128,128]{2,1,0:T(8,128)S(1)}, f32[4,128,128]{2,1,0:T(8,128)S(1)}, u32[]{:S(2)}, u32[]{:S(2)}) %collective-permute-start) | collective-permute-done | bytes 262176 | tf_op jit(solution)/shard_map/ppermute | solution.py:524
  3.2 1.4 %prepare_kernel.1 = f32[8,104,128]{2,1,0:T(8,128)S(1)} custom-call(f32[4,128,128]{2,1,0:T(8,128)S(1)} %pad_maximum_fusion.own, f32[4,128,128]{2,1,0:T(8,128)S(1)} %collective-permute-done.oth, s32[3]{0:T(128)S(1)} %pad_add_fusion.place), custom_call_target="tpu_custom_call" | custom-call | tf_op jit(solution)/shard_map/prepare_kernel/pallas_call | solution.py:487
  4.6 0.0 copy-start.2
  4.6 17.1 %all_to_all.20.got.raw = f32[8,104,128]{2,1,0:T(8,128)S(1)} all-to-all(f32[8,104,128]{2,1,0:T(8,128)S(1)} %prepare_kernel.1), channel_id=1, replica_groups=mesh['grp'=2,'slab'=4,'row'=2,'col'=2] {'slab','row'}, dimensions={0} | all-to-all | bytes 851968 | tf_op jit(solution)/shard_map/all_to_all | solution.py:527
  21.7 0.9 %column_kernel.1 = f32[8,72,128]{2,1,0:T(8,128)S(1)} custom-call(f32[4,128,128]{2,1,0:T(8,128)S(1)} %pad_maximum_fusion.own, f32[4,128,128]{2,1,0:T(8,128)S(1)} %collective-permute-done.oth, f32[8,104,128]{2,1,0:T(8,128)S(1)} %all_to_all.20.got.raw, f32[144,256]{1,0:T(8,128)S(1)} %copy-done.2), custom_call_target="tpu_custom_call" | custom-call | tf_op jit(solution)/shard_map/column_kernel/pallas_call | solution.py:487
  22.6 0.0 copy-start.1
  22.6 13.1 %all_to_all.21.got = f32[8,72,128]{2,1,0:T(8,128)S(1)} all-to-all(f32[8,72,128]{2,1,0:T(8,128)S(1)} %column_kernel.1), channel_id=1, replica_groups=mesh['grp'=2,'slab'=4,'row'=2,'col'=2] {'slab','row'}, dimensions={0} | all-to-all | bytes 589824 | tf_op jit(solution)/shard_map/all_to_all | solution.py:527
  35.7 3.6 %pencil_kernel.1 = (f32[8,136,128]{2,1,0:T(8,128)S(1)}, f32[8,8,16,128]{3,2,1,0:T(8,128)S(1)}) custom-call(f32[8,72,128]{2,1,0:T(8,128)S(1)} %all_to_all.21.got, f32[8,104,128]{2,1,0:T(8,128)S(1)} %all_to_all.20.got.raw, f32[512,512]{1,0:T(8,128)S(1)} %copy-done, f32[256,256]{1,0:T(8,128)S(1)} %copy-done.1), custom_call_target="tpu_custom_call" | custom-call | tf_op jit(solution)/shard_map/pencil_kernel/pallas_call | solution.py:487
  39.3 18.3 %all_to_all.22.near = f32[8,136,128]{2,1,0:T(8,128)S(1)} all-to-all(f32[8,136,128]{2,1,0:T(8,128)S(1)} %get-tuple-element.13), channel_id=1, replica_groups=mesh['grp'=2,'slab'=4,'row'=2,'col'=2] {'slab','row'}, dimensions={0} | all-to-all | bytes 1114112 | tf_op jit(solution)/shard_map/all_to_all | solution.py:527
  57.7 0.0 collective-permute-start.1
  57.7 1.2 %collective-permute-done.1.stat_b = f32[8,128]{1,0:T(8,128)S(1)} collective-permute-done((f32[8,128]{1,0:T(8,128)S(1)}, f32[8,128]{1,0:T(8,128)S(1)}, u32[]{:S(2)}, u32[]{:S(2)}) %collective-permute-start.1) | collective-permute-done | bytes 4128 | tf_op jit(solution)/shard_map/ppermute | solution.py:556
  58.8 1.2 %residual_kernel.1 = f32[8,48,128]{2,1,0:T(8,128)S(1)} custom-call(f32[8,128]{1,0:T(8,128)S(1)} %slice_reduce_fusion.stat_a, f32[8,128]{1,0:T(8,128)S(1)} %collective-permute-done.1.stat_b, f32[8,8,16,128]{3,2,1,0:T(8,128)S(1)} %get-tuple-element.14.keep, f32[8,104,128]{2,1,0:T(8,128)S(1)} %all_to_all.20.got.raw, f32[512,512]{1,0:T(8,128)S(1)} %copy-done, ...), custom_call_target="tpu_custom_call" | custom-call | tf_op jit(solution)/shard_map/residual_kernel/pallas_call | solution.py:487
  60.0 0.0 copy-start.3
  60.0 11.2 %all_to_all.23.got = f32[8,48,128]{2,1,0:T(8,128)S(1)} all-to-all(f32[8,48,128]{2,1,0:T(8,128)S(1)} %residual_kernel.1), channel_id=1, replica_groups=mesh['grp'=2,'slab'=4,'row'=2,'col'=2] {'slab','row'}, dimensions={0} | all-to-all | bytes 393216 | tf_op jit(solution)/shard_map/all_to_all | solution.py:527
  71.2 0.0 collective-permute-start.2
  71.2 1.4 %collective-permute-done.2.oth = f32[8,48,128]{2,1,0:T(8,128)S(1)} collective-permute-done((f32[8,48,128]{2,1,0:T(8,128)S(1)}, f32[8,48,128]{2,1,0:T(8,128)S(1)}, u32[]{:S(2)}, u32[]{:S(2)}) %collective-permute-start.2) | collective-permute-done | bytes 196640 | tf_op jit(solution)/shard_map/ppermute | solution.py:563
  72.7 2.3 %third_kernel.1 = (f32[3,128,128]{2,1,0:T(8,128)}, f32[8,3]{1,0:T(8,128)S(1)}, f32[8,128,128]{2,1,0:T(8,128)S(1)}, f32[8,128,128]{2,1,0:T(8,128)S(1)}, f32[8,16,...) custom-call(f32[8,48,128]{2,1,0:T(8,128)S(1)} %all_to_all.23.got, ...), custom_call_target="tpu_custom_call" | custom-call | tf_op jit(solution)/shard_map/third_kernel/pallas_call | solution.py:487
  74.9 0.6 collective-permute-start.3
  75.5 4.1 %collective-permute-start.4 = (f32[8,16,128]{2,1,0:T(8,128)S(1)}, f32[8,16,128]{2,1,0:T(8,128)S(1)}, u32[]{:S(2)}, u32[]{:S(2)}) collective-permute-start(f32[8,16,128]{2,1,0:T(8,128)S(1)} %get-tuple-element.18), channel_id=1, source_target_pairs={{4,8},{8,4},{5,9},{9,5},{6,10},{10,6},{7,11},{11,7},{20,24},{24,20... | collective-permute-start | bytes 196616 | tf_op jit(solution)/shard_map/ppermute | solution.py:582
  79.6 0.1 collective-permute-start.6
  79.7 1.0 %collective-permute-start.5 = (f32[8,8,128]{2,1,0:T(8,128)S(1)}, f32[8,8,128]{2,1,0:T(8,128)S(1)}, u32[]{:S(2)}, u32[]{:S(2)}) collective-permute-start(f32[8,8,128]{2,1,0:T(8,128)S(1)} %get-tuple-element.19), channel_id=1, source_target_pairs={{0,2},{2,0},{1,3},{3,1},{4,6},{6,4},{5,7},{7,5},{8,10},{10,8},{9,1... | collective-permute-start | bytes 98312 | tf_op jit(solution)/shard_map/ppermute | solution.py:583
  80.8 0.7 copy.10
  81.4 2.3 %collective-permute-done.5.side = f32[8,8,128]{2,1,0:T(8,128)S(1)} collective-permute-done((f32[8,8,128]{2,1,0:T(8,128)S(1)}, f32[8,8,128]{2,1,0:T(8,128)S(1)}, u32[]{:S(2)}, u32[]{:S(2)}) %collective-permute-start.5) | collective-permute-done | bytes 32800 | tf_op jit(solution)/shard_map/ppermute | solution.py:583
  83.7 0.0 collective-permute-done.3.up
  83.7 0.0 collective-permute-done.4.down
  83.7 0.0 collective-permute-done.6.edge
  83.7 1.9 %last_kernel.1 = bf16[8,128,128]{2,1,0:T(8,128)(2,1)} custom-call(f32[8,128,128]{2,1,0:T(8,128)S(1)} %get-tuple-element.15.dens, f32[8,128,128]{2,1,0:T(8,128)S(1)} %get-tuple-element.16.belief, f32[4,128,128]{2,1,0:T(8,128)S(1)} %pad_maximum_fusion.own, f32[8,16,128]{2,1,0:T(8,128)S(1)} %collective-permute-done.3.up, ...), custom_call_target="tpu_custom_call" | custom-call | tf_op jit(solution)/shard_map/last_kernel/pallas_call | solution.py:487
  (7 shorter events, 0.0 us)
Async XLA Ops:
  0.6 1.0 %copy-start.4 = (f32[3,8,16,128]{3,2,1,0:T(8,128)S(1)}, f32[3,8,16,128]{3,2,1,0:T(8,128)}, u32[]{:S(2)}) copy-start(f32[3,8,16,128]{3,2,1,0:T(8,128)} %param.7) | copy-start | bytes 589828
  1.6 1.6 %collective-permute-start = (f32[4,128,128]{2,1,0:T(8,128)S(1)}, f32[4,128,128]{2,1,0:T(8,128)S(1)}, u32[]{:S(2)}, u32[]{:S(2)}) collective-permute-start(f32[4,128,128]{2,1,0:T(8,128)S(1)} %pad_maximum_fusion.own), channel_id=1, source_target_pairs={{0,1},{1,0},{2,3},{3,2},{4,5},{5,4},{6,7},{7,6},{8,9},{9,8},{10,11... | collective-permute-start | bytes 786440 | tf_op jit(solution)/shard_map/ppermute | solution.py:524
  4.6 17.1 %copy-start.2 = (f32[144,256]{1,0:T(8,128)S(1)}, f32[144,256]{1,0:T(8,128)}, u32[]{:S(2)}) copy-start(f32[144,256]{1,0:T(8,128)} %constant.25.clone.table) | copy-start | bytes 442372
  21.7 14.0 %copy-start = (f32[512,512]{1,0:T(8,128)S(1)}, f32[512,512]{1,0:T(8,128)}, u32[]{:S(2)}) copy-start(f32[512,512]{1,0:T(8,128)} %constant.26.clone.slab_table) | copy-start | bytes 3145732
  22.6 13.1 %copy-start.1 = (f32[256,256]{1,0:T(8,128)S(1)}, f32[256,256]{1,0:T(8,128)}, u32[]{:S(2)}) copy-start(f32[256,256]{1,0:T(8,128)} %constant.27.clone.row_table) | copy-start | bytes 786436
  57.7 1.2 %collective-permute-start.1 = (f32[8,128]{1,0:T(8,128)S(1)}, f32[8,128]{1,0:T(8,128)S(1)}, u32[]{:S(2)}, u32[]{:S(2)}) collective-permute-start(f32[8,128]{1,0:T(8,128)S(1)} %slice_reduce_fusion.stat_a), channel_id=1, source_target_pairs={{0,1},{1,0},{2,3},{3,2},{4,5},{5,4},{6,7},{7,6},{8,9},{9,8},{10,11... | collective-permute-start | bytes 12296 | tf_op jit(solution)/shard_map/ppermute | solution.py:556
  60.0 12.6 %copy-start.3 = (f32[256,128]{1,0:T(8,128)S(1)}, f32[256,128]{1,0:T(8,128)}, u32[]{:S(2)}) copy-start(f32[256,128]{1,0:T(8,128)} %constant.28.clone.table) | copy-start | bytes 393220
  71.2 1.4 %collective-permute-start.2 = (f32[8,48,128]{2,1,0:T(8,128)S(1)}, f32[8,48,128]{2,1,0:T(8,128)S(1)}, u32[]{:S(2)}, u32[]{:S(2)}) collective-permute-start(f32[8,48,128]{2,1,0:T(8,128)S(1)} %all_to_all.23.got), channel_id=1, source_target_pairs={{0,1},{1,0},{2,3},{3,2},{4,5},{5,4},{6,7},{7,6},{8,9},{9,8},{10,11... | collective-permute-start | bytes 589832 | tf_op jit(solution)/shard_map/ppermute | solution.py:563
  74.9 8.8 %collective-permute-start.3 = (f32[8,16,128]{2,1,0:T(8,128)S(1)}, f32[8,16,128]{2,1,0:T(8,128)S(1)}, u32[]{:S(2)}, u32[]{:S(2)}) collective-permute-start(f32[8,16,128]{2,1,0:T(8,128)S(1)} %get-tuple-element.17), channel_id=1, source_target_pairs={{0,4},{8,12},{4,0},{12,8},{1,5},{9,13},{5,1},{13,9},{2,6},{10,14},... | collective-permute-start | bytes 196616 | tf_op jit(solution)/shard_map/ppermute | solution.py:581
  75.5 8.2 %collective-permute-start.4 = (f32[8,16,128]{2,1,0:T(8,128)S(1)}, f32[8,16,128]{2,1,0:T(8,128)S(1)}, u32[]{:S(2)}, u32[]{:S(2)}) collective-permute-start(f32[8,16,128]{2,1,0:T(8,128)S(1)} %get-tuple-element.18), channel_id=1, source_target_pairs={{4,8},{8,4},{5,9},{9,5},{6,10},{10,6},{7,11},{11,7},{20,24},{24,20... | collective-permute-start | bytes 196616 | tf_op jit(solution)/shard_map/ppermute | solution.py:582
  79.6 4.1 %collective-permute-start.6 = (f32[128,128]{1,0:T(8,128)S(1)}, f32[128,128]{1,0:T(8,128)S(1)}, u32[]{:S(2)}, u32[]{:S(2)}) collective-permute-start(f32[128,128]{1,0:T(8,128)S(1)} %get-tuple-element.20), channel_id=1, source_target_pairs={{0,1},{1,0},{2,3},{3,2},{4,5},{5,4},{6,7},{7,6},{8,9},{9,8},{10,11... | collective-permute-start | bytes 196616 | tf_op jit(solution)/shard_map/ppermute | solution.py:584
  79.7 4.0 %collective-permute-start.5 = (f32[8,8,128]{2,1,0:T(8,128)S(1)}, f32[8,8,128]{2,1,0:T(8,128)S(1)}, u32[]{:S(2)}, u32[]{:S(2)}) collective-permute-start(f32[8,8,128]{2,1,0:T(8,128)S(1)} %get-tuple-element.19), channel_id=1, source_target_pairs={{0,2},{2,0},{1,3},{3,1},{4,6},{6,4},{5,7},{7,5},{8,10},{10,8},{9,1... | collective-permute-start | bytes 98312 | tf_op jit(solution)/shard_map/ppermute | solution.py:583

commit v3 on v2

--- a/solution.py
+++ b/solution.py
@@ -1,5 +1,6 @@
 import functools
 import math
+import typing
 
 import jax
 import jax.numpy as jnp
@@ -141,6 +142,7 @@
 SUB = 8
 EDGE = 4
 MARGIN = 8
+FIELD = 4
 STATS = 1 + 2 * M
 VMEM_BYTES = 16 * 2**20
 
@@ -168,7 +170,7 @@
     return jnp.broadcast_to(row, shape)
 
 
-def stat_tile(sums):
+def stat_row(sums):
     sub = lax.broadcasted_iota(jnp.int32, (SUB, LANES), 0)
     lane = lax.broadcasted_iota(jnp.int32, (SUB, LANES), 1)
     tile = jnp.zeros((SUB, LANES), jnp.float32)
@@ -177,21 +179,29 @@
         for k in range(K):
             line = jnp.sum(sums[k][q], axis=0, keepdims=True)
             rows = jnp.where(sub == k, line, rows)
-        tile = jnp.where(lane == q, jnp.sum(rows, axis=1, keepdims=True), tile)
-    return tile
+        tile = jnp.where(lane == q * K + sub, jnp.sum(rows, axis=1, keepdims=True), tile)
+    return jnp.sum(tile, axis=0, keepdims=True)
+
+
+def stat_columns(row, number):
+    sub = lax.broadcasted_iota(jnp.int32, (SUB, LANES), 0)
+    lane = lax.broadcasted_iota(jnp.int32, (SUB, LANES), 1)
+    return [
+        jnp.sum(jnp.where(lane == q * K + sub, row, 0.0), axis=1, keepdims=True)
+        for q in range(number)
+    ]
 
 
 def fold(x):
     return jnp.sum(x.reshape(x.shape[0] // SUB, SUB, LANES), axis=0)
 
 
-def class_stats(tile):
-    count = tile[:, 0:1]
+def class_stats(row):
+    count, *rest = stat_columns(row, STATS)
     means, halves = [], []
     shift = jnp.zeros_like(count)
     for m in range(M):
-        first = tile[:, 1 + m : 2 + m]
-        squares = tile[:, 1 + M + m : 2 + M + m]
+        first, squares = rest[m], rest[M + m]
         mean = first / (count + 1.0)
         spread = squares - 2.0 * mean * first + mean * mean * count
         variance = (spread + 1.0) / (count + 1.0)
@@ -202,8 +212,9 @@
     return means, halves, wide(jnp.log(prior) + shift)
 
 
-def mean_rows(tile):
-    return [wide(tile[:, 1 + m : 2 + m] / (tile[:, 0:1] + 1.0)) for m in range(M)]
+def mean_rows(row):
+    count, *rest = stat_columns(row, 1 + M)
+    return [wide(x / (count + 1.0)) for x in rest]
 
 
 def log_terms(corrected, means, halves, shift):
@@ -224,44 +235,56 @@
     return [x * scale for x in exps]
 
 
-def prepare_kernel(own, oth, place, send, ext):
-    window = send.shape[1] // (M + 1) // SUB * SUB
+def peer_sum(ref, line):
+    row = ref[0, line : line + 1, :]
+    for j in range(1, ref.shape[0]):
+        row = row + ref[j, line : line + 1, :]
+    return row
+
+
+def class_sums(code, image):
+    sums = []
+    for k in range(K):
+        flag = (code == float(k)).astype(jnp.float32)
+        line = [fold(flag)]
+        weighted = [flag * image[m] for m in range(M)]
+        line += [fold(x) for x in weighted]
+        line += [fold(x * image[m]) for m, x in enumerate(weighted)]
+        sums.append(line)
+    return sums
+
+
+def own_kernel(own, turned, stat):
+    stat[...] = wide(stat_row(class_sums(own[M], own)))
+    for f in range(M + 1):
+        turned[f] = own[f].T
+
+
+def prepare_kernel(pack, turned, stat, oth, place, send, rest, ext):
     peers = send.shape[0]
     step = LANES // peers
     first = jnp.full((SUB, LANES), place[2], jnp.int32) == 0
+    row = stat[0:1, :] + stat_row(class_sums(oth[M], oth))
     for f in range(M + 1):
         blank = jnp.full((SUB, LANES), float(K) if f == M else 0.0, jnp.float32)
         other = oth[f].T
         ext[f, 0:MARGIN, :] = jnp.where(first, blank, other[LANES - MARGIN :, :])
-        ext[f, MARGIN : MARGIN + LANES, :] = own[f].T
+        ext[f, MARGIN : MARGIN + LANES, :] = turned[f]
         ext[f, MARGIN + LANES :, :] = jnp.where(first, other[:MARGIN, :], blank)
-    sums = []
-    for k in range(K):
-        line = [jnp.zeros((SUB, LANES), jnp.float32) for _ in range(STATS)]
-        for ref in (own, oth):
-            flag = (ref[M] == float(k)).astype(jnp.float32)
-            line[0] = line[0] + fold(flag)
-            for m in range(M):
-                value = flag * ref[m]
-                line[1 + m] = line[1 + m] + fold(value)
-                line[1 + M + m] = line[1 + M + m] + fold(value * ref[m])
-        sums.append(line)
-    tile = stat_tile(sums)
     for p in range(peers):
-        for f in range(M + 1):
-            base = MARGIN - EDGE + step * p
-            send[p, f * window : (f + 1) * window, :] = ext[f, base : base + window, :]
-        send[p, (M + 1) * window :, :] = tile
-
-
-def column_kernel(own, oth, got, table, send, flat, out):
+        at = MARGIN + step * p
+        for m in range(M):
+            send[p, pack.wide * m : pack.wide * (m + 1), :] = ext[m, at - 2 : at + step + 2, :]
+        send[p, pack.code : pack.stat, :] = ext[M, at - 1 : at + step + 1, :]
+        send[p, pack.stat : pack.stat + 1, :] = row
+        rest[p, 0:2, :] = ext[M, at - 3 : at - 1, :]
+        rest[p, 2:4, :] = ext[M, at + step + 1 : at + step + 3, :]
+
+
+def column_kernel(pack, own, oth, got, rest, table, send, flat, out):
     peers = send.shape[0]
-    window = send.shape[1] // M
     step = LANES // peers
-    tile = got[0, (M + 1) * window :, :]
-    for j in range(1, peers):
-        tile = tile + got[j, (M + 1) * window :, :]
-    means = mean_rows(tile)
+    means = mean_rows(peer_sum(got, pack.stat))
     for h, ref in enumerate((own, oth)):
         code = ref[M]
         flags = [code == float(k) for k in range(K)]
@@ -274,19 +297,16 @@
             )
     out[...] = dot(table[...], flat[...], ((1,), (1,)))
     for p in range(peers):
-        base = MARGIN - EDGE + step * p
+        at = MARGIN + step * p
+        send[p, pack.code : pack.code + 4, :] = rest[p, 0:4, :]
         for m in range(M):
-            send[p, m * window : (m + 1) * window, :] = out[
-                base : base + window, m * LANES : (m + 1) * LANES
+            send[p, pack.wide * m : pack.wide * (m + 1), :] = out[
+                at - 2 : at + step + 2, m * LANES : (m + 1) * LANES
             ]
 
 
-def slab_row_filter(pieces, slab_table, row_table, first, second, grid):
+def slab_row_filter(rows, slab_table, row_table, first, second, grid):
     ns, nr = grid
-    rows = pieces[0].shape[0]
-    for sb in range(ns):
-        for rb in range(nr):
-            first[rb * rows : (rb + 1) * rows, sb * LANES : (sb + 1) * LANES] = pieces[sb * nr + rb]
     mixed = dot(first[...], slab_table[...])
     for sb in range(ns):
         for rb in range(nr):
@@ -315,39 +335,75 @@
     return out
 
 
-def pencil_kernel(grid, rows, got, raw, slab_table, row_table, send, keep, first, second, bias, dens, one, two):
+def pencil_kernel(
+    pack,
+    grid,
+    rows,
+    got,
+    raw,
+    slab_table,
+    row_table,
+    send,
+    keep,
+    first,
+    second,
+    bias,
+    codes,
+    marks,
+    shaded,
+    dens,
+    one,
+    two,
+):
     ns, nr = grid
     peers = ns * nr
-    window = got.shape[1] // M
-    core = window - 2 * EDGE
-    tile = raw[0, (M + 1) * window :, :]
-    for j in range(1, peers):
-        tile = tile + raw[j, (M + 1) * window :, :]
-    means, halves, shift = class_stats(tile)
-    bias[...] = slab_row_filter(
-        [got[j] for j in range(peers)], slab_table, row_table, first, second, grid
-    )
-
-    def shade(sb, rb, m, low=0, size=window):
-        j = sb * nr + rb
-        base = (sb * M + m) * window + low
-        field = raw[j, m * window + low : m * window + low + size, :]
-        return field - bias[base : base + size, rb * LANES : (rb + 1) * LANES]
-
-    def code_at(sb, rb):
-        return raw[sb * nr + rb, M * window : (M + 1) * window, :]
-
+    core = pack.core
+    window = core + 2 * EDGE
+    means, halves, shift = class_stats(peer_sum(raw, pack.stat))
+    first[...] = jnp.zeros_like(first)
+    for sb in range(ns):
+        for rb in range(nr):
+            for m in range(M):
+                base = (rb * M + m) * window + EDGE - 2
+                first[base : base + pack.wide, sb * LANES : (sb + 1) * LANES] = got[
+                    sb * nr + rb, m * pack.wide : (m + 1) * pack.wide, :
+                ]
+    bias[...] = slab_row_filter(M * window, slab_table, row_table, first, second, grid)
+    blank = jnp.full((window, LANES), float(K), jnp.float32)
     for sb in range(ns):
         for rb in range(nr):
             j = sb * nr + rb
-            logits = log_terms([shade(sb, rb, m) for m in range(M)], means, halves, shift)
-            code = code_at(sb, rb)
-            near = around(code_at, sb, rb, grid, rows, float(K))
-            near = near + [pltpu.roll(code, 1, 0), pltpu.roll(code, window - 1, 0)]
+            codes[j] = blank
+            codes[j, EDGE - 3 : EDGE - 1, :] = got[j, pack.code : pack.code + 2, :]
+            codes[j, EDGE - 1 : EDGE + core + 1, :] = raw[j, pack.code : pack.stat, :]
+            codes[j, EDGE + core + 1 : EDGE + core + 3, :] = got[j, pack.code + 2 : pack.code + 4, :]
+            for m in range(M):
+                base = (sb * M + m) * window
+                shaded[j, m] = -bias[base : base + window, rb * LANES : (rb + 1) * LANES]
+                shaded[j, m, EDGE - 2 : EDGE - 2 + pack.wide, :] += raw[
+                    j, m * pack.wide : (m + 1) * pack.wide, :
+                ]
+
+    def bits(x):
+        whole = x.astype(jnp.int32)
+        return jnp.where(whole < K, lax.shift_left(jnp.ones_like(whole), whole * FIELD), 0)
+
+    for j in range(peers):
+        marks[j] = bits(codes[j])
+
+    for sb in range(ns):
+        for rb in range(nr):
+            j = sb * nr + rb
+            logits = log_terms([shaded[j, m] for m in range(M)], means, halves, shift)
+            code = codes[j]
+            here = marks[j]
+            near = around(lambda a, b: marks[a * nr + b], sb, rb, grid, rows, 0)
+            near = near + [pltpu.roll(here, 1, 0), pltpu.roll(here, window - 1, 0)]
+            near = functools.reduce(jnp.add, near)
             for k in range(K):
                 dens[k, j] = logits[k]
-                for x in near:
-                    logits[k] = logits[k] + (x == float(k)).astype(jnp.float32)
+                number = lax.shift_right_logical(near, jnp.full_like(near, k * FIELD))
+                logits[k] = logits[k] + (number & (2**FIELD - 1)).astype(jnp.float32)
             inside = (code < float(K)).astype(jnp.float32)
             for k, value in enumerate(soft(logits, inside)):
                 one[k, j] = value
@@ -360,14 +416,15 @@
                 near = around(lambda a, b: one[k, a * nr + b], sb, rb, grid, rows, 0.0)
                 near = near + [pltpu.roll(here, 1, 0), pltpu.roll(here, window - 1, 0)]
                 logits.append(dens[k, j] + functools.reduce(jnp.add, near))
-            inside = (code_at(sb, rb) < float(K)).astype(jnp.float32)
+            inside = (codes[j] < float(K)).astype(jnp.float32)
             for k, value in enumerate(soft(logits, inside)):
                 two[k, j] = value
     sums = [[jnp.zeros((SUB, LANES), jnp.float32) for _ in range(STATS)] for _ in range(K)]
     for sb in range(ns):
         for rb in range(nr):
             j = sb * nr + rb
-            values = [shade(sb, rb, m, EDGE, core) for m in range(M)]
+            values = [shaded[j, m, EDGE : EDGE + core, :] for m in range(M)]
+            totals = []
             for k in range(K):
                 here = two[k, j, EDGE : EDGE + core, :]
                 keep[k, j] = here
@@ -384,103 +441,177 @@
                     two[k, j, EDGE - 1 : EDGE - 1 + core, :],
                     two[k, j, EDGE + 1 : EDGE + 1 + core, :],
                 ]
-                send[j, k * core : (k + 1) * core, :] = functools.reduce(jnp.add, near)
-    tile = stat_tile(sums)
+                totals.append(functools.reduce(jnp.add, near))
+            for k in range(K - 1):
+                send[j, k * core : (k + 1) * core, :] = totals[k] - totals[K - 1]
+    row = stat_row(sums)
     for p in range(peers):
-        send[p, K * core :, :] = tile
-
-
-def residual_kernel(grid, stat_a, stat_b, keep, raw, slab_table, row_table, send, first, second):
+        send[p, (K - 1) * core : (K - 1) * core + 1, :] = row
+
+
+def residual_kernel(
+    pack, grid, stat_a, stat_b, keep, raw, slab_table, row_table, send, first, second
+):
     ns, nr = grid
-    core = keep.shape[2]
-    window = core + 2 * EDGE
+    core = pack.core
     means = mean_rows(stat_a[...] + stat_b[...])
-    pieces = []
-    for j in range(ns * nr):
-        parts = []
-        for m in range(M):
-            field = raw[j, m * window + EDGE : m * window + EDGE + core, :]
-            total = jnp.zeros_like(field)
-            for k in range(K):
-                total = total + keep[k, j] * (field - means[m][k : k + 1, :])
-            parts.append(total)
-        pieces.append(jnp.concatenate(parts, axis=0))
-    done = slab_row_filter(pieces, slab_table, row_table, first, second, grid)
+    for sb in range(ns):
+        for rb in range(nr):
+            j = sb * nr + rb
+            for m in range(M):
+                base = m * pack.wide + 2
+                field = raw[j, base : base + core, :]
+                total = jnp.zeros_like(field)
+                for k in range(K):
+                    total = total + keep[k, j] * (field - means[m][k : k + 1, :])
+                base = (rb * M + m) * core
+                first[base : base + core, sb * LANES : (sb + 1) * LANES] = total
     rows = M * core
+    done = slab_row_filter(rows, slab_table, row_table, first, second, grid)
     for sb in range(ns):
         for rb in range(nr):
             send[sb * nr + rb] = done[sb * rows : (sb + 1) * rows, rb * LANES : (rb + 1) * LANES]
 
 
-def third_kernel(rows, got, oth, near, own, stat_a, stat_b, table, place, bias, centers, dens, belief, up, down, side, edge):
-    peers = got.shape[0]
+def columns_of(ref, m, core):
+    return ref[:, m * core : (m + 1) * core, :].reshape(LANES, LANES).T
+
+
+def half_kernel(got, near, table, field, around):
     core = got.shape[1] // M
-    tile = stat_a[...] + stat_b[...]
-    means, halves, shift = class_stats(tile)
-    centers[...] = tile[:, 1 : 1 + M] / (tile[:, 0:1] + 1.0)
-    corrected = []
     for m in range(M):
-        mine = got[:, m * core : (m + 1) * core, :].reshape(LANES, LANES).T
-        yours = oth[:, m * core : (m + 1) * core, :].reshape(LANES, LANES).T
-        field = dot(jnp.concatenate([mine, yours], axis=1), table[...])
-        bias[m] = field
-        corrected.append(own[m] - field)
-    logits = log_terms(corrected, means, halves, shift)
+        field[m] = dot(columns_of(got, m, core), table[:LANES, :])
+    for k in range(K - 1):
+        around[k] = columns_of(near, k, core)
+
+
+def third_kernel(
+    rows,
+    field,
+    got,
+    near,
+    own,
+    stat_a,
+    stat_b,
+    table,
+    place,
+    bias_h,
+    centers,
+    dens,
+    belief,
+    up,
+    down,
+    side,
+    edge,
+    bias,
+    sems,
+):
+    core = got.shape[1] // M
+    slabs = LANES // rows
+    means, halves, shift = class_stats(stat_a[...] + stat_b[...])
+    for m in range(M):
+        centers[:, m : m + 1] = means[m][:, :1]
+        bias[m] = field[m] + dot(columns_of(got, m, core), table[LANES:, :])
+    copy = pltpu.make_async_copy(bias, bias_h, sems.at[0])
+    copy.start()
+    lane = lax.broadcasted_iota(jnp.int32, (1, LANES), 1)
+    even = jnp.full((rows, LANES), place[0] % 2, jnp.int32) == 0
+    amounts = [jnp.where(place[2] == 0, k + 1, k) for k in range(K)]
+    for s in range(slabs):
+        low, high = s * rows, (s + 1) * rows
+        corrected = [own[m, low:high, :] - bias[m, low:high, :] for m in range(M)]
+        logits = log_terms(corrected, means, halves, shift)
+        for k in range(K):
+            dens[k, low:high, :] = logits[k]
+            if k < K - 1:
+                logits[k] = logits[k] + near[k, low:high, :]
+        inside = (own[M, low:high, :] < float(K)).astype(jnp.float32)
+        column = jnp.zeros((rows, LANES), jnp.float32)
+        for k, value in enumerate(soft(logits, inside)):
+            belief[k, low:high, :] = value
+            column = jnp.where(lane == k, pltpu.roll(value, amounts[k], 1), column)
+        edge[low:high, :] = column
     for k in range(K):
-        dens[k] = logits[k]
-        logits[k] = logits[k] + near[:, k * core : (k + 1) * core, :].reshape(LANES, LANES).T
-    inside = (own[M] < float(K)).astype(jnp.float32)
+        first = belief[k, :rows, :]
+        final = belief[k, LANES - rows :, :]
+        up[k] = jnp.where(even, final, first)
+        down[k] = jnp.where(even, first, final)
+    lead = jnp.full((slabs, LANES), place[1], jnp.int32) == 0
+    for k in range(K):
+        head = belief[k, pl.ds(0, slabs, rows), :]
+        tail = belief[k, pl.ds(rows - 1, slabs, rows), :]
+        side[k] = jnp.where(lead, tail, head)
+    copy.wait()
+
+
+def inner_kernel(rows, dens, belief, logits):
     lane = lax.broadcasted_iota(jnp.int32, (1, LANES), 1)
-    odd = place[0] % 2
-    column = jnp.zeros((LANES, LANES), jnp.float32)
-    for k, value in enumerate(soft(logits, inside)):
-        belief[k] = value
-        low = value[:rows, :]
-        high = value[LANES - rows :, :]
-        even = jnp.full(low.shape, odd, jnp.int32) == 0
-        up[k] = jnp.where(even, high, low)
-        down[k] = jnp.where(even, low, high)
-        amount = jnp.where(place[2] == 0, k + 1, k)
-        column = jnp.where(lane == k, pltpu.roll(value, amount, 1), column)
-    edge[...] = column
-    lead = jnp.full((LANES // rows, LANES), place[1], jnp.int32) == 0
+    line = lax.broadcasted_iota(jnp.int32, (rows, 1), 0)
     for k in range(K):
-        head = belief[k, pl.ds(0, LANES // rows, rows), :]
-        tail = belief[k, pl.ds(rows - 1, LANES // rows, rows), :]
-        side[k] = jnp.where(lead, tail, head)
-
-
-def last_kernel(rows, dens, belief, own, up, down, side, edge, place, post):
+        for low in range(0, LANES, rows):
+            here = belief[k, low : low + rows, :]
+            total = dens[k, low : low + rows, :]
+            if low > 0:
+                total = total + belief[k, low - rows : low, :]
+            if low + rows < LANES:
+                total = total + belief[k, low + rows : low + 2 * rows, :]
+            total = total + jnp.where(line > 0, pltpu.roll(here, 1, 0), 0.0)
+            total = total + jnp.where(line < rows - 1, pltpu.roll(here, rows - 1, 0), 0.0)
+            total = total + jnp.where(lane > 0, pltpu.roll(here, 1, 1), 0.0)
+            total = total + jnp.where(lane < LANES - 1, pltpu.roll(here, LANES - 1, 1), 0.0)
+            logits[k, low : low + rows, :] = total
+
+
+def last_kernel(rows, inner, own, up, down, side, edge, place, post_h, post, sems):
+    slabs = LANES // rows
     lane = lax.broadcasted_iota(jnp.int32, (1, LANES), 1)
-    line = lax.broadcasted_iota(jnp.int32, (LANES, 1), 0) % rows
+    line = lax.broadcasted_iota(jnp.int32, (rows, 1), 0)
     even = jnp.full((rows, LANES), place[0] % 2, jnp.int32) == 0
     spot = jnp.where(place[2] == 0, LANES - 1, 0)
     face = jnp.where(place[1] == 0, rows - 1, 0)
-    column = edge[...]
-    logits = []
-    for k in range(K):
-        here = belief[k]
-        high = jnp.where(even, up[k], down[k])
-        low = jnp.where(even, down[k], up[k])
-        total = jnp.concatenate([low, here[: LANES - rows, :]], axis=0)
-        total = total + jnp.concatenate([here[rows:, :], high], axis=0)
-        beside = jnp.broadcast_to(side[k][:, None, :], (LANES // rows, rows, LANES))
-        total = total + jnp.where(line == face, beside.reshape(LANES, LANES), 0.0)
-        total = total + jnp.where(line > 0, pltpu.roll(here, 1, 0), 0.0)
-        total = total + jnp.where(line < rows - 1, pltpu.roll(here, LANES - 1, 0), 0.0)
-        shifted = pltpu.roll(column, jnp.where(place[2] == 0, LANES - 1 - k, (LANES - k) % LANES), 1)
-        total = total + jnp.where(lane == spot, shifted, 0.0)
-        total = total + jnp.where(lane > 0, pltpu.roll(here, 1, 1), 0.0)
-        total = total + jnp.where(lane < LANES - 1, pltpu.roll(here, LANES - 1, 1), 0.0)
-        logits.append(dens[k] + total)
-    inside = (own[M] < float(K)).astype(jnp.float32)
-    for k, value in enumerate(soft(logits, inside)):
-        post[k] = value.astype(jnp.bfloat16)
-
-
-def call(kernel, outs, scratch=(), scalars=()):
+    amounts = [jnp.where(place[2] == 0, LANES - 1 - k, (LANES - k) % LANES) for k in range(K)]
+    copies = []
+    for s in range(slabs):
+        low, high = s * rows, (s + 1) * rows
+        column = edge[low:high, :]
+        logits = []
+        for k in range(K):
+            total = inner[k, low:high, :]
+            if s == 0:
+                total = total + jnp.where(even, down[k], up[k])
+            if s == slabs - 1:
+                total = total + jnp.where(even, up[k], down[k])
+            total = total + jnp.where(line == face, side[k, s : s + 1, :], 0.0)
+            total = total + jnp.where(lane == spot, pltpu.roll(column, amounts[k], 1), 0.0)
+            logits.append(total)
+        inside = (own[M, low:high, :] < float(K)).astype(jnp.float32)
+        for k, value in enumerate(soft(logits, inside)):
+            post[k, low:high, :] = value.astype(jnp.bfloat16)
+        if s % 2:
+            span = pl.ds(low - rows, 2 * rows)
+            copies.append(
+                pltpu.make_async_copy(post.at[:, span, :], post_h.at[:, span, :], sems.at[s // 2])
+            )
+            copies[-1].start()
+    for copy in copies:
+        copy.wait()
+
+
+class Pack(typing.NamedTuple):
+    core: int
+    wide: int
+    code: int
+    stat: int
+
+
+def padded(rows):
+    return -(-rows // SUB) * SUB
+
+
+def call(kernel, outs, scratch=(), scalars=(), micros=1, far_out=()):
     vmem = pl.BlockSpec(memory_space=pltpu.VMEM)
     smem = pl.BlockSpec(memory_space=pltpu.SMEM)
+    far = pl.BlockSpec(memory_space=pltpu.HBM)
     shapes = [jax.ShapeDtypeStruct(shape, kind) for shape, kind in outs]
 
     def run(*args):
@@ -488,9 +619,14 @@
             kernel,
             out_shape=shapes,
             in_specs=[smem if i in scalars else vmem for i in range(len(args))],
-            out_specs=[vmem] * len(shapes),
-            scratch_shapes=[pltpu.VMEM(shape, jnp.float32) for shape in scratch],
+            out_specs=[far if i in far_out else vmem for i in range(len(shapes))],
+            scratch_shapes=[
+                pltpu.VMEM(x, jnp.float32) if isinstance(x, tuple) else x for x in scratch
+            ],
             compiler_params=pltpu.CompilerParams(vmem_limit_bytes=VMEM_BYTES),
+            cost_estimate=pl.CostEstimate(
+                flops=micros * 10_000_000, bytes_accessed=2**20, transcendentals=0
+            ),
             name=(kernel.func if isinstance(kernel, functools.partial) else kernel).__name__,
         )(*args)
 
@@ -504,6 +640,8 @@
     peers = ns * nr
     core = columns // peers
     window = core + 2 * EDGE
+    wide_rows = core + 4
+    pack = Pack(core, wide_rows, M * wide_rows, M * wide_rows + core + 2)
     f32 = jnp.float32
     place = jnp.stack([lax.axis_index(a) for a in ("slab", "row", "col")]).astype(jnp.int32)
     swap = [(0, 1), (1, 0)]
@@ -526,41 +664,54 @@
     def trade(x):
         return lax.all_to_all(x, ("slab", "row"), split_axis=0, concat_axis=0, tiled=True)
 
-    (sent,) = call(
-        prepare_kernel,
-        [((peers, (M + 1) * window + SUB, LANES), f32)],
+    turned, stat = call(
+        own_kernel, [((M + 1, columns, LANES), f32), ((SUB, LANES), f32)]
+    )(own)
+    sent, rest = call(
+        functools.partial(prepare_kernel, pack),
+        [((peers, padded(pack.stat + 1), LANES), f32), ((peers, SUB, LANES), f32)],
         [(M + 1, columns + 2 * MARGIN, LANES)],
-        (2,),
-    )(own, oth, place)
+        (3,),
+    )(turned, stat, oth, place)
     raw = trade(sent)
     (sent,) = call(
-        column_kernel,
-        [((peers, M * window, LANES), f32)],
+        functools.partial(column_kernel, pack),
+        [((peers, padded(pack.code + 4), LANES), f32)],
         [(M * LANES, 2 * columns), (columns + 2 * MARGIN, M * LANES)],
-    )(own, oth, raw, spread)
+    )(own, oth, raw, rest, spread)
     got = trade(sent)
     sent, keep = call(
-        functools.partial(pencil_kernel, grid, rows),
-        [((peers, K * core + SUB, LANES), f32), ((K, peers, core, LANES), f32)],
+        functools.partial(pencil_kernel, pack, grid, rows),
+        [
+            ((peers, padded((K - 1) * core + 1), LANES), f32),
+            ((K, peers, core, LANES), f32),
+        ],
         [
             (nr * M * window, ns * LANES),
             (ns * M * window, nr * LANES),
             (ns * M * window, nr * LANES),
+            (peers, window, LANES),
+            pltpu.VMEM((peers, window, LANES), jnp.int32),
+            (peers, M, window, LANES),
             (K, peers, window, LANES),
             (K, peers, window, LANES),
             (K, peers, window, LANES),
         ],
+        micros=4,
     )(got, raw, slab_table, row_table)
     near = trade(sent)
-    stat_a = jnp.sum(near[:, K * core :, :], axis=0)
+    stat_a = jnp.sum(near[:, (K - 1) * core : (K - 1) * core + 1, :], axis=0)
     stat_b = lax.ppermute(stat_a, "col", swap)
     (sent,) = call(
-        functools.partial(residual_kernel, grid),
+        functools.partial(residual_kernel, pack, grid),
         [((peers, M * core, LANES), f32)],
         [(nr * M * core, ns * LANES), (ns * M * core, nr * LANES)],
     )(stat_a, stat_b, keep, raw, slab_table, row_table)
     got = trade(sent)
     yours = lax.ppermute(got, "col", swap)
+    field, near = call(
+        half_kernel, [((M, LANES, columns), f32), ((K - 1, LANES, columns), f32)]
+    )(got, near, gather)
     bias, centers, dens, belief, up, down, side, edge = call(
         functools.partial(third_kernel, rows),
         [
@@ -573,18 +724,30 @@
             ((K, slabs, columns), f32),
             ((LANES, LANES), f32),
         ],
-        (),
+        [(M, LANES, columns), pltpu.SemaphoreType.DMA((1,))],
         (7,),
-    )(got, yours, near, own, stat_a, stat_b, gather, place)
+        2,
+        far_out=(0,),
+    )(field, yours, near, own, stat_a, stat_b, gather, place)
     pairs = [(i, i + 1) for i in range(0, ns - 1, 2)]
     between = [(i, i + 1) for i in range(1, ns - 1, 2)]
     up = lax.ppermute(up, "slab", pairs + [(b, a) for a, b in pairs])
     down = lax.ppermute(down, "slab", between + [(b, a) for a, b in between])
     side = lax.ppermute(side, "row", swap)
     edge = lax.ppermute(edge, "col", swap)
+    (inner,) = call(functools.partial(inner_kernel, rows), [((K, LANES, columns), f32)])(
+        dens, belief
+    )
     (post,) = call(
-        functools.partial(last_kernel, rows), [((K, LANES, columns), jnp.bfloat16)], (), (7,)
-    )(dens, belief, own, up, down, side, edge, place)
+        functools.partial(last_kernel, rows),
+        [((K, LANES, columns), jnp.bfloat16)],
+        [
+            pltpu.VMEM((K, LANES, columns), jnp.bfloat16),
+            pltpu.SemaphoreType.DMA((slabs // 2,)),
+        ],
+        (6,),
+        far_out=(0,),
+    )(inner, own, up, down, side, edge, place)
     shape = (slabs, rows, columns)
     return post.reshape((K,) + shape), bias.reshape((M,) + shape), centers
 

time: 85.9 us -> 80.4 us (0.936)
  blocking collectives: 59.7 us -> 55.5 us
  waiting for transfers between devices: 6.35 us -> 5.12 us
    all_to_all x4, blocking collectives: 59.7 us -> 55.5 us  [trade(): lax.all_to_all(x, ('slab', 'row'), split_axis=0, concat_axis=0, tiled=True)]
    pallas_call x6 -> x9, Pallas kernels: 11.2 us -> 11 us  [run(): pl.pallas_call(kernel, out_shape=shapes, in_specs=[smem if i in scalars e...]
  transfers between devices with their start and end apart: 7 -> 7, of which waited for: 4 -> 4; matrix products, arithmetic and copies ran while one was open for 1% -> 1% of each run, Pallas kernels for 0% -> 1%
where the time goes in v3:
time: 80.4 us; the launch traced here: 80.1 us
  blocking collectives  55.5 us (69%)
  Pallas kernels  11 us (14%)
  starting transfers between devices  5.99 us (7%)
  waiting for transfers between devices  5.12 us (6%)
  other arithmetic  1.04 us (1%)
    all_to_all x4, blocking collectives, trade(): lax.all_to_all(x, ('slab', 'row'), split_axis=0, concat_axis=0, tiled=True)  55.5 us
    pallas_call x9, Pallas kernels, run(): pl.pallas_call(kernel, out_shape=shapes, in_specs=[smem if i in scalars e...  11 us
    ppermute x1, starting transfers between devices, pencils(): down = lax.ppermute(down, 'slab', between + [(b, a) for a, b in between])  4.11 us
    ppermute x1, waiting for transfers between devices, pencils(): side = lax.ppermute(side, 'row', swap)  1.95 us
  transfers between devices with their start and end apart: 7, of which 4 were waited for; matrix products, arithmetic and copies ran while one was open for 1% of the time, Pallas kernels for 1%

profile of v3, /device:TPU:16, one launch (start us, length us, event | category | flops | bytes accessed | tf_op | source)
XLA Modules:
  0.0 80.1 jit_solution(18101823076971638874)
XLA Ops:
  0.6 0.9 %select_convert_fusion = f32[8,16,128]{2,1,0:T(8,128)S(1)} fusion(s32[8,16,128]{2,1,0:T(8,128)} %param.9, s32[8,16,128]{2,1,0:T(8,128)} %param.8), kind=kLoop, calls=%fused_computation.1 | loop fusion | flops 49152 | bytes 196608 | tf_op jit(solution)/shard_map/convert_element_type | solution.py:660
  1.6 0.1 copy-done.4
  1.6 0.1 collective-permute-start
  1.7 0.5 own_kernel.1
  2.2 0.1 pad_add_fusion.place
  2.3 1.0 %collective-permute-done.oth = f32[4,128,128]{2,1,0:T(8,128)S(1)} collective-permute-done((f32[4,128,128]{2,1,0:T(8,128)S(1)}, f32[4,128,128]{2,1,0:T(8,128)S(1)}, u32[]{:S(2)}, u32[]{:S(2)}) %collective-permute-start) | collective-permute-done | bytes 262176 | tf_op jit(solution)/shard_map/ppermute | solution.py:662
  3.2 1.0 %prepare_kernel.1 = (f32[8,80,128]{2,1,0:T(8,128)S(1)}, f32[8,8,128]{2,1,0:T(8,128)S(1)}) custom-call(f32[4,128,128]{2,1,0:T(8,128)S(1)} %get-tuple-element.19.turned, f32[8,128]{1,0:T(8,128)S(1)} %get-tuple-element.20.stat, f32[4,128,128]{2,1,0:T(8,128)S(1)} %collective-permute-done.oth, s32[3]{0:T(128)S(1)} %pad_add_fusion.place), custom_call_target="tpu_custom_call" | custom-call | flops 10000000 | bytes 1048576 | tf_op jit(solution)/shard_map/prepare_kernel/pallas_call | solution.py:618
  4.3 0.0 copy-start.3
  4.3 15.1 %all_to_all.20.got.raw = f32[8,80,128]{2,1,0:T(8,128)S(1)} all-to-all(f32[8,80,128]{2,1,0:T(8,128)S(1)} %get-tuple-element.21), channel_id=1, replica_groups=mesh['grp'=2,'slab'=4,'row'=2,'col'=2] {'slab','row'}, dimensions={0} | all-to-all | bytes 655360 | tf_op jit(solution)/shard_map/all_to_all | solution.py:665
  19.4 0.8 %column_kernel.1 = f32[8,64,128]{2,1,0:T(8,128)S(1)} custom-call(f32[4,128,128]{2,1,0:T(8,128)S(1)} %pad_maximum_fusion.own, f32[4,128,128]{2,1,0:T(8,128)S(1)} %collective-permute-done.oth, f32[8,80,128]{2,1,0:T(8,128)S(1)} %all_to_all.20.got.raw, f32[8,8,128]{2,1,0:T(8,128)S(1)} %get-tuple-element.22.rest, f32[144,256]{1,0:T(8,128)S(1)} %copy-done.3), custom_call_target="tpu_custom_call" | custom-call | flops 10000000 | bytes 1048576 | tf_op jit(solution)/shard_map/column_kernel/pallas_call | solution.py:618
  20.2 0.0 copy-start.1
  20.2 12.1 %all_to_all.21.got = f32[8,64,128]{2,1,0:T(8,128)S(1)} all-to-all(f32[8,64,128]{2,1,0:T(8,128)S(1)} %column_kernel.1), channel_id=1, replica_groups=mesh['grp'=2,'slab'=4,'row'=2,'col'=2] {'slab','row'}, dimensions={0} | all-to-all | bytes 524288 | tf_op jit(solution)/shard_map/all_to_all | solution.py:665
  32.3 3.4 %pencil_kernel.1 = (f32[8,120,128]{2,1,0:T(8,128)S(1)}, f32[8,8,16,128]{3,2,1,0:T(8,128)S(1)}) custom-call(f32[8,64,128]{2,1,0:T(8,128)S(1)} %all_to_all.21.got, f32[8,80,128]{2,1,0:T(8,128)S(1)} %all_to_all.20.got.raw, f32[512,512]{1,0:T(8,128)S(1)} %copy-done, f32[256,256]{1,0:T(8,128)S(1)} %copy-done.1), custom_call_target="tpu_custom_call" | custom-call | flops 40000000 | bytes 1048576 | tf_op jit(solution)/shard_map/pencil_kernel/pallas_call | solution.py:618
  35.7 16.9 %all_to_all.22.near = f32[8,120,128]{2,1,0:T(8,128)S(1)} all-to-all(f32[8,120,128]{2,1,0:T(8,128)S(1)} %get-tuple-element.23), channel_id=1, replica_groups=mesh['grp'=2,'slab'=4,'row'=2,'col'=2] {'slab','row'}, dimensions={0} | all-to-all | bytes 983040 | tf_op jit(solution)/shard_map/all_to_all | solution.py:665
  52.7 0.1 collective-permute-start.1
  52.8 1.1 %collective-permute-done.1.stat_b = f32[1,128]{1,0:T(1,128)S(1)} collective-permute-done((f32[1,128]{1,0:T(1,128)S(1)}, f32[1,128]{1,0:T(1,128)S(1)}, u32[]{:S(2)}, u32[]{:S(2)}) %collective-permute-start.1) | collective-permute-done | bytes 544 | tf_op jit(solution)/shard_map/ppermute | solution.py:704
  53.9 1.1 %residual_kernel.1 = f32[8,48,128]{2,1,0:T(8,128)S(1)} custom-call(f32[1,128]{1,0:T(1,128)S(1)} %bitcast.9, f32[1,128]{1,0:T(1,128)S(1)} %collective-permute-done.1.stat_b, f32[8,8,16,128]{3,2,1,0:T(8,128)S(1)} %get-tuple-element.24.keep, f32[8,80,128]{2,1,0:T(8,128)S(1)} %all_to_all.20.got.raw, f32[512,512]{1,0:T(8,128)S(1)} %copy-done, ...), custom_call_target="tpu_custom_call" | custom-call | flops 10000000 | bytes 1048576 | tf_op jit(solution)/shard_map/residual_kernel/pallas_call | solution.py:618
  55.0 0.0 copy-start.2
  55.0 11.4 %all_to_all.23.got = f32[8,48,128]{2,1,0:T(8,128)S(1)} all-to-all(f32[8,48,128]{2,1,0:T(8,128)S(1)} %residual_kernel.1), channel_id=1, replica_groups=mesh['grp'=2,'slab'=4,'row'=2,'col'=2] {'slab','row'}, dimensions={0} | all-to-all | bytes 393216 | tf_op jit(solution)/shard_map/all_to_all | solution.py:665
  66.4 0.0 collective-permute-start.2
  66.4 0.4 half_kernel.1
  66.8 1.1 %collective-permute-done.2.got = f32[8,48,128]{2,1,0:T(8,128)S(1)} collective-permute-done((f32[8,48,128]{2,1,0:T(8,128)S(1)}, f32[8,48,128]{2,1,0:T(8,128)S(1)}, u32[]{:S(2)}, u32[]{:S(2)}) %collective-permute-start.2) | collective-permute-done | bytes 196640 | tf_op jit(solution)/shard_map/ppermute | solution.py:711
  67.9 1.9 %third_kernel.1 = (f32[3,128,128]{2,1,0:T(8,128)}, f32[8,3]{1,0:T(8,128)S(1)}, f32[8,128,128]{2,1,0:T(8,128)S(1)}, f32[8,128,128]{2,1,0:T(8,128)S(1)}, f32[8,16,...) custom-call(f32[3,128,128]{2,1,0:T(8,128)S(1)} %get-tuple-element.25.field, ...), custom_call_target="tpu_custom_call" | custom-call | flops 20000000 | bytes 1048576 | tf_op jit(solution)/shard_map/third_kernel/pallas_call | solution.py:618
  69.8 0.6 collective-permute-start.3
  70.5 4.1 %collective-permute-start.4 = (f32[8,16,128]{2,1,0:T(8,128)S(1)}, f32[8,16,128]{2,1,0:T(8,128)S(1)}, u32[]{:S(2)}, u32[]{:S(2)}) collective-permute-start(f32[8,16,128]{2,1,0:T(8,128)S(1)} %get-tuple-element.30), channel_id=1, source_target_pairs={{4,8},{8,4},{5,9},{9,5},{6,10},{10,6},{7,11},{11,7},{20,24},{24,20... | collective-permute-start | bytes 196616 | tf_op jit(solution)/shard_map/ppermute | solution.py:735
  74.6 0.1 collective-permute-start.6
  74.6 1.0 %collective-permute-start.5 = (f32[8,8,128]{2,1,0:T(8,128)S(1)}, f32[8,8,128]{2,1,0:T(8,128)S(1)}, u32[]{:S(2)}, u32[]{:S(2)}) collective-permute-start(f32[8,8,128]{2,1,0:T(8,128)S(1)} %get-tuple-element.31), channel_id=1, source_target_pairs={{0,2},{2,0},{1,3},{3,1},{4,6},{6,4},{5,7},{7,5},{8,10},{10,8},{9,1... | collective-permute-start | bytes 98312 | tf_op jit(solution)/shard_map/ppermute | solution.py:736
  75.7 0.7 copy.10
  76.3 0.3 inner_kernel.1.inner
  76.7 1.9 %collective-permute-done.5.side = f32[8,8,128]{2,1,0:T(8,128)S(1)} collective-permute-done((f32[8,8,128]{2,1,0:T(8,128)S(1)}, f32[8,8,128]{2,1,0:T(8,128)S(1)}, u32[]{:S(2)}, u32[]{:S(2)}) %collective-permute-start.5) | collective-permute-done | bytes 32800 | tf_op jit(solution)/shard_map/ppermute | solution.py:736
  78.6 0.0 collective-permute-done.3.up
  78.6 1.5 %last_kernel.1 = bf16[8,128,128]{2,1,0:T(8,128)(2,1)} custom-call(f32[8,128,128]{2,1,0:T(8,128)S(1)} %inner_kernel.1.inner, f32[4,128,128]{2,1,0:T(8,128)S(1)} %pad_maximum_fusion.own, f32[8,16,128]{2,1,0:T(8,128)S(1)} %collective-permute-done.3.up, f32[8,16,128]{2,1,0:T(8,128)S(1)} %collective-permute-done.4.down, ...), custom_call_target="tpu_custom_call" | custom-call | flops 10000000 | bytes 1048576 | tf_op jit(solution)/shard_map/last_kernel/pallas_call | solution.py:618
  (10 shorter events, 0.1 us)
Async XLA Ops:
  0.6 1.0 %copy-start.4 = (f32[3,8,16,128]{3,2,1,0:T(8,128)S(1)}, f32[3,8,16,128]{3,2,1,0:T(8,128)}, u32[]{:S(2)}) copy-start(f32[3,8,16,128]{3,2,1,0:T(8,128)} %param.7) | copy-start | bytes 589828
  1.6 1.6 %collective-permute-start = (f32[4,128,128]{2,1,0:T(8,128)S(1)}, f32[4,128,128]{2,1,0:T(8,128)S(1)}, u32[]{:S(2)}, u32[]{:S(2)}) collective-permute-start(f32[4,128,128]{2,1,0:T(8,128)S(1)} %pad_maximum_fusion.own), channel_id=1, source_target_pairs={{0,1},{1,0},{2,3},{3,2},{4,5},{5,4},{6,7},{7,6},{8,9},{9,8},{10,11... | collective-permute-start | bytes 786440 | tf_op jit(solution)/shard_map/ppermute | solution.py:662
  4.3 15.1 %copy-start.3 = (f32[144,256]{1,0:T(8,128)S(1)}, f32[144,256]{1,0:T(8,128)}, u32[]{:S(2)}) copy-start(f32[144,256]{1,0:T(8,128)} %constant.25.clone.table) | copy-start | bytes 442372
  19.4 13.0 %copy-start = (f32[512,512]{1,0:T(8,128)S(1)}, f32[512,512]{1,0:T(8,128)}, u32[]{:S(2)}) copy-start(f32[512,512]{1,0:T(8,128)} %constant.26.clone.slab_table) | copy-start | bytes 3145732
  20.2 12.1 %copy-start.1 = (f32[256,256]{1,0:T(8,128)S(1)}, f32[256,256]{1,0:T(8,128)}, u32[]{:S(2)}) copy-start(f32[256,256]{1,0:T(8,128)} %constant.27.clone.row_table) | copy-start | bytes 786436
  52.7 1.2 %collective-permute-start.1 = (f32[1,128]{1,0:T(1,128)S(1)}, f32[1,128]{1,0:T(1,128)S(1)}, u32[]{:S(2)}, u32[]{:S(2)}) collective-permute-start(f32[1,128]{1,0:T(1,128)S(1)} %bitcast.8), channel_id=1, source_target_pairs={{0,1},{1,0},{2,3},{3,2},{4,5},{5,4},{6,7},{7,6},{8,9},{9,8},{10,11... | collective-permute-start | bytes 1544 | tf_op jit(solution)/shard_map/ppermute | solution.py:704
  55.0 11.4 %copy-start.2 = (f32[256,128]{1,0:T(8,128)S(1)}, f32[256,128]{1,0:T(8,128)}, u32[]{:S(2)}) copy-start(f32[256,128]{1,0:T(8,128)} %constant.28.clone.table) | copy-start | bytes 393220
  66.4 1.4 %collective-permute-start.2 = (f32[8,48,128]{2,1,0:T(8,128)S(1)}, f32[8,48,128]{2,1,0:T(8,128)S(1)}, u32[]{:S(2)}, u32[]{:S(2)}) collective-permute-start(f32[8,48,128]{2,1,0:T(8,128)S(1)} %all_to_all.23.got), channel_id=1, source_target_pairs={{0,1},{1,0},{2,3},{3,2},{4,5},{5,4},{6,7},{7,6},{8,9},{9,8},{10,11... | collective-permute-start | bytes 589832 | tf_op jit(solution)/shard_map/ppermute | solution.py:711
  69.8 8.8 %collective-permute-start.3 = (f32[8,16,128]{2,1,0:T(8,128)S(1)}, f32[8,16,128]{2,1,0:T(8,128)S(1)}, u32[]{:S(2)}, u32[]{:S(2)}) collective-permute-start(f32[8,16,128]{2,1,0:T(8,128)S(1)} %get-tuple-element.29), channel_id=1, source_target_pairs={{0,4},{8,12},{4,0},{12,8},{1,5},{9,13},{5,1},{13,9},{2,6},{10,14},... | collective-permute-start | bytes 196616 | tf_op jit(solution)/shard_map/ppermute | solution.py:734
  70.5 8.2 %collective-permute-start.4 = (f32[8,16,128]{2,1,0:T(8,128)S(1)}, f32[8,16,128]{2,1,0:T(8,128)S(1)}, u32[]{:S(2)}, u32[]{:S(2)}) collective-permute-start(f32[8,16,128]{2,1,0:T(8,128)S(1)} %get-tuple-element.30), channel_id=1, source_target_pairs={{4,8},{8,4},{5,9},{9,5},{6,10},{10,6},{7,11},{11,7},{20,24},{24,20... | collective-permute-start | bytes 196616 | tf_op jit(solution)/shard_map/ppermute | solution.py:735
  74.6 4.1 %collective-permute-start.6 = (f32[128,128]{1,0:T(8,128)S(1)}, f32[128,128]{1,0:T(8,128)S(1)}, u32[]{:S(2)}, u32[]{:S(2)}) collective-permute-start(f32[128,128]{1,0:T(8,128)S(1)} %get-tuple-element.32), channel_id=1, source_target_pairs={{0,1},{1,0},{2,3},{3,2},{4,5},{5,4},{6,7},{7,6},{8,9},{9,8},{10,11... | collective-permute-start | bytes 196616 | tf_op jit(solution)/shard_map/ppermute | solution.py:737
  74.6 4.0 %collective-permute-start.5 = (f32[8,8,128]{2,1,0:T(8,128)S(1)}, f32[8,8,128]{2,1,0:T(8,128)S(1)}, u32[]{:S(2)}, u32[]{:S(2)}) collective-permute-start(f32[8,8,128]{2,1,0:T(8,128)S(1)} %get-tuple-element.31), channel_id=1, source_target_pairs={{0,2},{2,0},{1,3},{3,1},{4,6},{6,4},{5,7},{7,5},{8,10},{10,8},{9,1... | collective-permute-start | bytes 98312 | tf_op jit(solution)/shard_map/ppermute | solution.py:736

commit v4 on v3

--- a/solution.py
+++ b/solution.py
@@ -160,10 +160,24 @@
     return impulse(length)[(index[:, None] - index[None, :]) % length]
 
 
+def halves_of(x):
+    high = x.astype(jnp.bfloat16)
+    return high, (x - high.astype(jnp.float32)).astype(jnp.bfloat16)
+
+
+def table_of(x):
+    high = x.astype(jnp.bfloat16)
+    low = (x - high.astype(np.float64)).astype(jnp.bfloat16)
+    return np.stack([high, low])
+
+
 def dot(left, right, dims=((1,), (0,))):
-    return lax.dot_general(
-        left, right, (dims, ((), ())), precision=highest, preferred_element_type=jnp.float32
-    )
+    left, right = (x if isinstance(x, tuple) else halves_of(x) for x in (left, right))
+
+    def one(a, b):
+        return lax.dot_general(a, b, (dims, ((), ())), preferred_element_type=jnp.float32)
+
+    return one(left[0], right[0]) + (one(left[1], right[0]) + one(left[0], right[1]))
 
 
 def wide(row, shape=(SUB, LANES)):
@@ -263,7 +277,7 @@
 def prepare_kernel(pack, turned, stat, oth, place, send, rest, ext):
     peers = send.shape[0]
     step = LANES // peers
-    first = jnp.full((SUB, LANES), place[2], jnp.int32) == 0
+    first = place[2] == 0
     row = stat[0:1, :] + stat_row(class_sums(oth[M], oth))
     for f in range(M + 1):
         blank = jnp.full((SUB, LANES), float(K) if f == M else 0.0, jnp.float32)
@@ -295,7 +309,7 @@
             flat[m * LANES : (m + 1) * LANES, h * LANES : (h + 1) * LANES] = jnp.where(
                 code < float(K), ref[m] - center, 0.0
             )
-    out[...] = dot(table[...], flat[...], ((1,), (1,)))
+    out[...] = dot((table[0], table[1]), flat[...], ((1,), (1,)))
     for p in range(peers):
         at = MARGIN + step * p
         send[p, pack.code : pack.code + 4, :] = rest[p, 0:4, :]
@@ -307,13 +321,13 @@
 
 def slab_row_filter(rows, slab_table, row_table, first, second, grid):
     ns, nr = grid
-    mixed = dot(first[...], slab_table[...])
+    mixed = dot(first[...], (slab_table[0], slab_table[1]))
     for sb in range(ns):
         for rb in range(nr):
             second[sb * rows : (sb + 1) * rows, rb * LANES : (rb + 1) * LANES] = mixed[
                 rb * rows : (rb + 1) * rows, sb * LANES : (sb + 1) * LANES
             ]
-    return dot(second[...], row_table[...])
+    return dot(second[...], (row_table[0], row_table[1]))
 
 
 def around(get, sb, rb, grid, rows, fill):
@@ -366,13 +380,13 @@
             for m in range(M):
                 base = (rb * M + m) * window + EDGE - 2
                 first[base : base + pack.wide, sb * LANES : (sb + 1) * LANES] = got[
-                    sb * nr + rb, m * pack.wide : (m + 1) * pack.wide, :
+                    rb * ns + sb, m * pack.wide : (m + 1) * pack.wide, :
                 ]
     bias[...] = slab_row_filter(M * window, slab_table, row_table, first, second, grid)
     blank = jnp.full((window, LANES), float(K), jnp.float32)
     for sb in range(ns):
         for rb in range(nr):
-            j = sb * nr + rb
+            j = rb * ns + sb
             codes[j] = blank
             codes[j, EDGE - 3 : EDGE - 1, :] = got[j, pack.code : pack.code + 2, :]
             codes[j, EDGE - 1 : EDGE + core + 1, :] = raw[j, pack.code : pack.stat, :]
@@ -393,11 +407,11 @@
 
     for sb in range(ns):
         for rb in range(nr):
-            j = sb * nr + rb
+            j = rb * ns + sb
             logits = log_terms([shaded[j, m] for m in range(M)], means, halves, shift)
             code = codes[j]
             here = marks[j]
-            near = around(lambda a, b: marks[a * nr + b], sb, rb, grid, rows, 0)
+            near = around(lambda a, b: marks[b * ns + a], sb, rb, grid, rows, 0)
             near = near + [pltpu.roll(here, 1, 0), pltpu.roll(here, window - 1, 0)]
             near = functools.reduce(jnp.add, near)
             for k in range(K):
@@ -409,11 +423,11 @@
                 one[k, j] = value
     for sb in range(ns):
         for rb in range(nr):
-            j = sb * nr + rb
+            j = rb * ns + sb
             logits = []
             for k in range(K):
                 here = one[k, j]
-                near = around(lambda a, b: one[k, a * nr + b], sb, rb, grid, rows, 0.0)
+                near = around(lambda a, b: one[k, b * ns + a], sb, rb, grid, rows, 0.0)
                 near = near + [pltpu.roll(here, 1, 0), pltpu.roll(here, window - 1, 0)]
                 logits.append(dens[k, j] + functools.reduce(jnp.add, near))
             inside = (codes[j] < float(K)).astype(jnp.float32)
@@ -422,7 +436,7 @@
     sums = [[jnp.zeros((SUB, LANES), jnp.float32) for _ in range(STATS)] for _ in range(K)]
     for sb in range(ns):
         for rb in range(nr):
-            j = sb * nr + rb
+            j = rb * ns + sb
             values = [shaded[j, m, EDGE : EDGE + core, :] for m in range(M)]
             totals = []
             for k in range(K):
@@ -435,7 +449,7 @@
                     line[1 + m] = line[1 + m] + fold(value)
                     line[1 + M + m] = line[1 + M + m] + fold(value * values[m])
                 near = around(
-                    lambda a, b: two[k, a * nr + b, EDGE : EDGE + core, :], sb, rb, grid, rows, 0.0
+                    lambda a, b: two[k, b * ns + a, EDGE : EDGE + core, :], sb, rb, grid, rows, 0.0
                 )
                 near = near + [
                     two[k, j, EDGE - 1 : EDGE - 1 + core, :],
@@ -457,7 +471,7 @@
     means = mean_rows(stat_a[...] + stat_b[...])
     for sb in range(ns):
         for rb in range(nr):
-            j = sb * nr + rb
+            j = rb * ns + sb
             for m in range(M):
                 base = m * pack.wide + 2
                 field = raw[j, base : base + core, :]
@@ -470,7 +484,7 @@
     done = slab_row_filter(rows, slab_table, row_table, first, second, grid)
     for sb in range(ns):
         for rb in range(nr):
-            send[sb * nr + rb] = done[sb * rows : (sb + 1) * rows, rb * LANES : (rb + 1) * LANES]
+            send[rb * ns + sb] = done[sb * rows : (sb + 1) * rows, rb * LANES : (rb + 1) * LANES]
 
 
 def columns_of(ref, m, core):
@@ -480,7 +494,7 @@
 def half_kernel(got, near, table, field, around):
     core = got.shape[1] // M
     for m in range(M):
-        field[m] = dot(columns_of(got, m, core), table[:LANES, :])
+        field[m] = dot(columns_of(got, m, core), (table[0, :LANES, :], table[1, :LANES, :]))
     for k in range(K - 1):
         around[k] = columns_of(near, k, core)
 
@@ -495,7 +509,7 @@
     stat_b,
     table,
     place,
-    bias_h,
+    bias,
     centers,
     dens,
     belief,
@@ -503,20 +517,19 @@
     down,
     side,
     edge,
-    bias,
-    sems,
 ):
     core = got.shape[1] // M
     slabs = LANES // rows
     means, halves, shift = class_stats(stat_a[...] + stat_b[...])
     for m in range(M):
         centers[:, m : m + 1] = means[m][:, :1]
-        bias[m] = field[m] + dot(columns_of(got, m, core), table[LANES:, :])
-    copy = pltpu.make_async_copy(bias, bias_h, sems.at[0])
-    copy.start()
+        bias[m] = field[m] + dot(
+            columns_of(got, m, core), (table[0, LANES:, :], table[1, LANES:, :])
+        )
     lane = lax.broadcasted_iota(jnp.int32, (1, LANES), 1)
-    even = jnp.full((rows, LANES), place[0] % 2, jnp.int32) == 0
-    amounts = [jnp.where(place[2] == 0, k + 1, k) for k in range(K)]
+    even = place[0, 0:1, :] == 0
+    shiftback = jnp.where(place[2, 0:1, :] == 0, 1, 0)
+    marks = [(lane + shiftback) % LANES == k for k in range(K)]
     for s in range(slabs):
         low, high = s * rows, (s + 1) * rows
         corrected = [own[m, low:high, :] - bias[m, low:high, :] for m in range(M)]
@@ -529,22 +542,23 @@
         column = jnp.zeros((rows, LANES), jnp.float32)
         for k, value in enumerate(soft(logits, inside)):
             belief[k, low:high, :] = value
-            column = jnp.where(lane == k, pltpu.roll(value, amounts[k], 1), column)
+            column = jnp.where(marks[k], pltpu.roll(value, k, 1), column)
         edge[low:high, :] = column
     for k in range(K):
         first = belief[k, :rows, :]
         final = belief[k, LANES - rows :, :]
         up[k] = jnp.where(even, final, first)
         down[k] = jnp.where(even, first, final)
-    lead = jnp.full((slabs, LANES), place[1], jnp.int32) == 0
+    lead = place[1, 0:1, :] == 0
     for k in range(K):
         head = belief[k, pl.ds(0, slabs, rows), :]
         tail = belief[k, pl.ds(rows - 1, slabs, rows), :]
         side[k] = jnp.where(lead, tail, head)
-    copy.wait()
-
-
-def inner_kernel(rows, dens, belief, logits):
+
+
+def inner_kernel(rows, dens, belief, bias, logits, bias_h, sems):
+    copy = pltpu.make_async_copy(bias, bias_h, sems.at[0])
+    copy.start()
     lane = lax.broadcasted_iota(jnp.int32, (1, LANES), 1)
     line = lax.broadcasted_iota(jnp.int32, (rows, 1), 0)
     for k in range(K):
@@ -560,20 +574,22 @@
             total = total + jnp.where(lane > 0, pltpu.roll(here, 1, 1), 0.0)
             total = total + jnp.where(lane < LANES - 1, pltpu.roll(here, LANES - 1, 1), 0.0)
             logits[k, low : low + rows, :] = total
+    copy.wait()
 
 
 def last_kernel(rows, inner, own, up, down, side, edge, place, post_h, post, sems):
     slabs = LANES // rows
     lane = lax.broadcasted_iota(jnp.int32, (1, LANES), 1)
     line = lax.broadcasted_iota(jnp.int32, (rows, 1), 0)
-    even = jnp.full((rows, LANES), place[0] % 2, jnp.int32) == 0
-    spot = jnp.where(place[2] == 0, LANES - 1, 0)
-    face = jnp.where(place[1] == 0, rows - 1, 0)
-    amounts = [jnp.where(place[2] == 0, LANES - 1 - k, (LANES - k) % LANES) for k in range(K)]
+    even = place[0, 0:1, :] == 0
+    left = place[2, 0:1, :] == 0
+    spot = lane == jnp.where(left, LANES - 1, 0)
+    face = line == jnp.where(place[1, 0:1, :] == 0, rows - 1, 0)
     copies = []
     for s in range(slabs):
         low, high = s * rows, (s + 1) * rows
         column = edge[low:high, :]
+        column = jnp.where(left, column, pltpu.roll(column, 2, 1))
         logits = []
         for k in range(K):
             total = inner[k, low:high, :]
@@ -581,8 +597,8 @@
                 total = total + jnp.where(even, down[k], up[k])
             if s == slabs - 1:
                 total = total + jnp.where(even, up[k], down[k])
-            total = total + jnp.where(line == face, side[k, s : s + 1, :], 0.0)
-            total = total + jnp.where(lane == spot, pltpu.roll(column, amounts[k], 1), 0.0)
+            total = total + jnp.where(face, side[k, s : s + 1, :], 0.0)
+            total = total + jnp.where(spot, pltpu.roll(column, LANES - 1 - k, 1), 0.0)
             logits.append(total)
         inside = (own[M, low:high, :] < float(K)).astype(jnp.float32)
         for k, value in enumerate(soft(logits, inside)):
@@ -608,9 +624,8 @@
     return -(-rows // SUB) * SUB
 
 
-def call(kernel, outs, scratch=(), scalars=(), micros=1, far_out=()):
+def call(kernel, outs, scratch=(), micros=1, far_out=()):
     vmem = pl.BlockSpec(memory_space=pltpu.VMEM)
-    smem = pl.BlockSpec(memory_space=pltpu.SMEM)
     far = pl.BlockSpec(memory_space=pltpu.HBM)
     shapes = [jax.ShapeDtypeStruct(shape, kind) for shape, kind in outs]
 
@@ -618,7 +633,7 @@
         return pl.pallas_call(
             kernel,
             out_shape=shapes,
-            in_specs=[smem if i in scalars else vmem for i in range(len(args))],
+            in_specs=[vmem] * len(args),
             out_specs=[far if i in far_out else vmem for i in range(len(shapes))],
             scratch_shapes=[
                 pltpu.VMEM(x, jnp.float32) if isinstance(x, tuple) else x for x in scratch
@@ -643,26 +658,28 @@
     wide_rows = core + 4
     pack = Pack(core, wide_rows, M * wide_rows, M * wide_rows + core + 2)
     f32 = jnp.float32
-    place = jnp.stack([lax.axis_index(a) for a in ("slab", "row", "col")]).astype(jnp.int32)
+    place = jnp.stack([lax.axis_index("slab") % 2, lax.axis_index("row"), lax.axis_index("col")])
+    place = jnp.broadcast_to(place.astype(jnp.int32)[:, None, None], (3, SUB, LANES))
     swap = [(0, 1), (1, 0)]
 
     taps = impulse(columns * nc)
     reach = np.arange(-MARGIN, columns + MARGIN)
     source = np.concatenate([np.arange(columns), np.arange(columns) + columns])
-    spread = taps[(reach[:, None] - source[None, :]) % (columns * nc)].astype(np.float32)
-    gather = np.ascontiguousarray(spread[MARGIN : MARGIN + columns].T)
-    slab_table = np.kron(dense(slabs * ns), np.eye(rows)).astype(np.float32)
+    spread = taps[(reach[:, None] - source[None, :]) % (columns * nc)]
+    gather = table_of(spread[MARGIN : MARGIN + columns].T)
+    spread = table_of(spread)
+    slab_table = table_of(np.kron(dense(slabs * ns), np.eye(rows)))
     row_table = np.einsum(
         "arbq,st->asrbtq", dense(rows * nr).reshape(nr, rows, nr, rows), np.eye(slabs)
     )
-    row_table = row_table.reshape(nr * LANES, nr * LANES).astype(np.float32)
+    row_table = table_of(row_table.reshape(nr * LANES, nr * LANES))
 
     code = jnp.where(brain_mask > 0, labels, K).astype(f32)
     own = jnp.concatenate([image, code[None]]).reshape(M + 1, LANES, columns)
     oth = lax.ppermute(own, "col", swap)
 
     def trade(x):
-        return lax.all_to_all(x, ("slab", "row"), split_axis=0, concat_axis=0, tiled=True)
+        return lax.all_to_all(x, ("row", "slab"), split_axis=0, concat_axis=0, tiled=True)
 
     turned, stat = call(
         own_kernel, [((M + 1, columns, LANES), f32), ((SUB, LANES), f32)]
@@ -671,7 +688,6 @@
         functools.partial(prepare_kernel, pack),
         [((peers, padded(pack.stat + 1), LANES), f32), ((peers, SUB, LANES), f32)],
         [(M + 1, columns + 2 * MARGIN, LANES)],
-        (3,),
     )(turned, stat, oth, place)
     raw = trade(sent)
     (sent,) = call(
@@ -724,10 +740,7 @@
             ((K, slabs, columns), f32),
             ((LANES, LANES), f32),
         ],
-        [(M, LANES, columns), pltpu.SemaphoreType.DMA((1,))],
-        (7,),
-        2,
-        far_out=(0,),
+        micros=2,
     )(field, yours, near, own, stat_a, stat_b, gather, place)
     pairs = [(i, i + 1) for i in range(0, ns - 1, 2)]
     between = [(i, i + 1) for i in range(1, ns - 1, 2)]
@@ -735,9 +748,12 @@
     down = lax.ppermute(down, "slab", between + [(b, a) for a, b in between])
     side = lax.ppermute(side, "row", swap)
     edge = lax.ppermute(edge, "col", swap)
-    (inner,) = call(functools.partial(inner_kernel, rows), [((K, LANES, columns), f32)])(
-        dens, belief
-    )
+    inner, bias = call(
+        functools.partial(inner_kernel, rows),
+        [((K, LANES, columns), f32), ((M, LANES, columns), f32)],
+        [pltpu.SemaphoreType.DMA((1,))],
+        far_out=(1,),
+    )(dens, belief, bias)
     (post,) = call(
         functools.partial(last_kernel, rows),
         [((K, LANES, columns), jnp.bfloat16)],
@@ -745,7 +761,6 @@
             pltpu.VMEM((K, LANES, columns), jnp.bfloat16),
             pltpu.SemaphoreType.DMA((slabs // 2,)),
         ],
-        (6,),
         far_out=(0,),
     )(inner, own, up, down, side, edge, place)
     shape = (slabs, rows, columns)

time: 80.4 us -> 76.9 us (0.956)
  Pallas kernels: 11 us -> 8.31 us
  blocking collectives: 55.5 us -> 54.5 us
    pallas_call x9, Pallas kernels: 11 us -> 8.31 us  [run(): pl.pallas_call(kernel, out_shape=shapes, in_specs=[vmem] * len(args), out...]
    all_to_all x4, blocking collectives: 55.5 us -> 54.5 us  [trade(): lax.all_to_all(x, ('row', 'slab'), split_axis=0, concat_axis=0, tiled=True)]
  transfers between devices with their start and end apart: 7 -> 7, of which waited for: 4 -> 4; matrix products, arithmetic and copies ran while one was open for 1% -> 1% of each run, Pallas kernels for 1% -> 2%
where the time goes in v4:
time: 76.9 us; the launch traced here: 76.6 us
  blocking collectives  54.5 us (71%)
  Pallas kernels  8.31 us (11%)
  starting transfers between devices  6.16 us (8%)
  waiting for transfers between devices  4.99 us (6%)
  other arithmetic  1.04 us (1%)
  local copies, waits for them, and re-layouts  0.8 us (1%)
  between operations  0.77 us (1%)
    all_to_all x4, blocking collectives, trade(): lax.all_to_all(x, ('row', 'slab'), split_axis=0, concat_axis=0, tiled=True)  54.5 us
    pallas_call x9, Pallas kernels, run(): pl.pallas_call(kernel, out_shape=shapes, in_specs=[vmem] * len(args), out...  8.31 us
    ppermute x1, starting transfers between devices, pencils(): down = lax.ppermute(down, 'slab', between + [(b, a) for a, b in between])  4.87 us
    ppermute x1, waiting for transfers between devices, pencils(): side = lax.ppermute(side, 'row', swap)  1.75 us
  transfers between devices with their start and end apart: 7, of which 4 were waited for; matrix products, arithmetic and copies ran while one was open for 1% of the time, Pallas kernels for 2%

profile of v4, /device:TPU:16, one launch (start us, length us, event | category | flops | bytes accessed | tf_op | source)
XLA Modules:
  0.0 76.6 jit_solution(10089355627870771097)
XLA Ops:
  0.6 0.9 %select_convert_fusion = f32[8,16,128]{2,1,0:T(8,128)S(1)} fusion(s32[8,16,128]{2,1,0:T(8,128)} %param.9, s32[8,16,128]{2,1,0:T(8,128)} %param.8), kind=kLoop, calls=%fused_computation.1 | loop fusion | flops 49152 | bytes 196608 | tf_op jit(solution)/shard_map/convert_element_type | solution.py:677
  1.6 0.1 copy-done.4
  1.6 0.1 collective-permute-start
  1.7 0.5 own_kernel.1
  2.2 0.1 pad_add_fusion
  2.3 0.9 %collective-permute-done.oth = f32[4,128,128]{2,1,0:T(8,128)S(1)} collective-permute-done((f32[4,128,128]{2,1,0:T(8,128)S(1)}, f32[4,128,128]{2,1,0:T(8,128)S(1)}, u32[]{:S(2)}, u32[]{:S(2)}) %collective-permute-start) | collective-permute-done | bytes 262176 | tf_op jit(solution)/shard_map/ppermute | solution.py:679
  3.2 0.1 broadcast_in_dim.12.place
  3.3 0.5 prepare_kernel.1
  3.8 0.0 copy-start.3
  3.8 15.1 %all_to_all.20.got.raw = f32[8,80,128]{2,1,0:T(8,128)S(1)} all-to-all(f32[8,80,128]{2,1,0:T(8,128)S(1)} %get-tuple-element.23), channel_id=1, replica_groups=mesh['grp'=2,'slab'=4,'row'=2,'col'=2] {'row','slab'}, dimensions={0} | all-to-all | bytes 655360 | tf_op jit(solution)/shard_map/all_to_all | solution.py:682
  18.9 0.6 column_kernel.1
  19.6 0.0 copy-start.1
  19.6 11.7 %all_to_all.21.got = f32[8,64,128]{2,1,0:T(8,128)S(1)} all-to-all(f32[8,64,128]{2,1,0:T(8,128)S(1)} %column_kernel.1), channel_id=1, replica_groups=mesh['grp'=2,'slab'=4,'row'=2,'col'=2] {'row','slab'}, dimensions={0} | all-to-all | bytes 524288 | tf_op jit(solution)/shard_map/all_to_all | solution.py:682
  31.3 3.0 %pencil_kernel.1 = (f32[8,120,128]{2,1,0:T(8,128)S(1)}, f32[8,8,16,128]{3,2,1,0:T(8,128)S(1)}) custom-call(f32[8,64,128]{2,1,0:T(8,128)S(1)} %all_to_all.21.got, f32[8,80,128]{2,1,0:T(8,128)S(1)} %all_to_all.20.got.raw, bf16[2,512,512]{2,1,0:T(8,128)(2,1)S(1)} %copy-done, bf16[2,256,256]{2,1,0:T(8,128)(2,1)S(1)} %copy-done.1), custom_call_target="tpu_custom_call" | custom-call | flops 40000000 | bytes 1048576 | tf_op jit(solution)/shard_map/pencil_kernel/pallas_call | solution.py:633
  34.3 16.4 %all_to_all.22.near = f32[8,120,128]{2,1,0:T(8,128)S(1)} all-to-all(f32[8,120,128]{2,1,0:T(8,128)S(1)} %get-tuple-element.25), channel_id=1, replica_groups=mesh['grp'=2,'slab'=4,'row'=2,'col'=2] {'row','slab'}, dimensions={0} | all-to-all | bytes 983040 | tf_op jit(solution)/shard_map/all_to_all | solution.py:682
  50.7 0.1 collective-permute-start.1
  50.7 1.1 %collective-permute-done.1.stat_b = f32[1,128]{1,0:T(1,128)S(1)} collective-permute-done((f32[1,128]{1,0:T(1,128)S(1)}, f32[1,128]{1,0:T(1,128)S(1)}, u32[]{:S(2)}, u32[]{:S(2)}) %collective-permute-start.1) | collective-permute-done | bytes 544 | tf_op jit(solution)/shard_map/ppermute | solution.py:720
  51.9 0.7 residual_kernel.1
  52.6 0.0 copy-start.2
  52.6 11.4 %all_to_all.23.got = f32[8,48,128]{2,1,0:T(8,128)S(1)} all-to-all(f32[8,48,128]{2,1,0:T(8,128)S(1)} %residual_kernel.1), channel_id=1, replica_groups=mesh['grp'=2,'slab'=4,'row'=2,'col'=2] {'row','slab'}, dimensions={0} | all-to-all | bytes 393216 | tf_op jit(solution)/shard_map/all_to_all | solution.py:682
  64.0 0.0 collective-permute-start.2
  64.0 0.3 half_kernel.1
  64.3 1.1 %collective-permute-done.2.got = f32[8,48,128]{2,1,0:T(8,128)S(1)} collective-permute-done((f32[8,48,128]{2,1,0:T(8,128)S(1)}, f32[8,48,128]{2,1,0:T(8,128)S(1)}, u32[]{:S(2)}, u32[]{:S(2)}) %collective-permute-start.2) | collective-permute-done | bytes 196640 | tf_op jit(solution)/shard_map/ppermute | solution.py:727
  65.4 0.7 third_kernel.1
  66.2 0.5 collective-permute-start.3
  66.6 4.9 %collective-permute-start.4 = (f32[8,16,128]{2,1,0:T(8,128)S(1)}, f32[8,16,128]{2,1,0:T(8,128)S(1)}, u32[]{:S(2)}, u32[]{:S(2)}) collective-permute-start(f32[8,16,128]{2,1,0:T(8,128)S(1)} %get-tuple-element.34), channel_id=1, source_target_pairs={{4,8},{8,4},{5,9},{9,5},{6,10},{10,6},{7,11},{11,7},{20,24},{24,20... | collective-permute-start | bytes 196616 | tf_op jit(solution)/shard_map/ppermute | solution.py:748
  71.5 0.1 collective-permute-start.6
  71.6 0.6 collective-permute-start.5
  72.2 0.7 copy.10
  72.9 1.0 %inner_kernel.1 = (f32[8,128,128]{2,1,0:T(8,128)S(1)}, f32[3,128,128]{2,1,0:T(8,128)}) custom-call(f32[8,128,128]{2,1,0:T(8,128)S(1)} %get-tuple-element.29.dens, f32[8,128,128]{2,1,0:T(8,128)S(1)} %get-tuple-element.30.belief, f32[3,128,128]{2,1,0:T(8,128)S(1)} %get-tuple-element.31.bias), custom_call_target="tpu_custom_call" | custom-call | flops 10000000 | bytes 1048576 | tf_op jit(solution)/shard_map/inner_kernel/pallas_call | solution.py:633
  73.8 1.7 %collective-permute-done.5.side = f32[8,8,128]{2,1,0:T(8,128)S(1)} collective-permute-done((f32[8,8,128]{2,1,0:T(8,128)S(1)}, f32[8,8,128]{2,1,0:T(8,128)S(1)}, u32[]{:S(2)}, u32[]{:S(2)}) %collective-permute-start.5) | collective-permute-done | bytes 32800 | tf_op jit(solution)/shard_map/ppermute | solution.py:749
  75.6 1.0 %last_kernel.1 = bf16[8,128,128]{2,1,0:T(8,128)(2,1)} custom-call(f32[8,128,128]{2,1,0:T(8,128)S(1)} %get-tuple-element.32.inner, f32[4,128,128]{2,1,0:T(8,128)S(1)} %pad_maximum_fusion.own, f32[8,16,128]{2,1,0:T(8,128)S(1)} %collective-permute-done.3.up, f32[8,16,128]{2,1,0:T(8,128)S(1)} %collective-permute-done.4.down, ...), custom_call_target="tpu_custom_call" | custom-call | flops 10000000 | bytes 1048576 | tf_op jit(solution)/shard_map/last_kernel/pallas_call | solution.py:633
  (11 shorter events, 0.1 us)
Async XLA Ops:
  0.6 1.0 %copy-start.4 = (f32[3,8,16,128]{3,2,1,0:T(8,128)S(1)}, f32[3,8,16,128]{3,2,1,0:T(8,128)}, u32[]{:S(2)}) copy-start(f32[3,8,16,128]{3,2,1,0:T(8,128)} %param.7) | copy-start | bytes 589828
  1.6 1.6 %collective-permute-start = (f32[4,128,128]{2,1,0:T(8,128)S(1)}, f32[4,128,128]{2,1,0:T(8,128)S(1)}, u32[]{:S(2)}, u32[]{:S(2)}) collective-permute-start(f32[4,128,128]{2,1,0:T(8,128)S(1)} %pad_maximum_fusion.own), channel_id=1, source_target_pairs={{0,1},{1,0},{2,3},{3,2},{4,5},{5,4},{6,7},{7,6},{8,9},{9,8},{10,11... | collective-permute-start | bytes 786440 | tf_op jit(solution)/shard_map/ppermute | solution.py:679
  3.8 15.1 %copy-start.3 = (bf16[2,144,256]{2,1,0:T(8,128)(2,1)S(1)}, bf16[2,144,256]{2,1,0:T(8,128)(2,1)}, u32[]{:S(2)}) copy-start(bf16[2,144,256]{2,1,0:T(8,128)(2,1)} %constant.37.clone.table) | copy-start | bytes 442372
  18.9 12.4 %copy-start = (bf16[2,512,512]{2,1,0:T(8,128)(2,1)S(1)}, bf16[2,512,512]{2,1,0:T(8,128)(2,1)}, u32[]{:S(2)}) copy-start(bf16[2,512,512]{2,1,0:T(8,128)(2,1)} %constant.38.clone.slab_table) | copy-start | bytes 3145732
  19.6 11.7 %copy-start.1 = (bf16[2,256,256]{2,1,0:T(8,128)(2,1)S(1)}, bf16[2,256,256]{2,1,0:T(8,128)(2,1)}, u32[]{:S(2)}) copy-start(bf16[2,256,256]{2,1,0:T(8,128)(2,1)} %constant.39.clone.row_table) | copy-start | bytes 786436
  50.7 1.2 %collective-permute-start.1 = (f32[1,128]{1,0:T(1,128)S(1)}, f32[1,128]{1,0:T(1,128)S(1)}, u32[]{:S(2)}, u32[]{:S(2)}) collective-permute-start(f32[1,128]{1,0:T(1,128)S(1)} %bitcast.8), channel_id=1, source_target_pairs={{0,1},{1,0},{2,3},{3,2},{4,5},{5,4},{6,7},{7,6},{8,9},{9,8},{10,11... | collective-permute-start | bytes 1544 | tf_op jit(solution)/shard_map/ppermute | solution.py:720
  52.6 11.4 %copy-start.2 = (bf16[2,256,128]{2,1,0:T(8,128)(2,1)S(1)}, bf16[2,256,128]{2,1,0:T(8,128)(2,1)}, u32[]{:S(2)}) copy-start(bf16[2,256,128]{2,1,0:T(8,128)(2,1)} %constant.40.clone.table) | copy-start | bytes 393220
  64.0 1.4 %collective-permute-start.2 = (f32[8,48,128]{2,1,0:T(8,128)S(1)}, f32[8,48,128]{2,1,0:T(8,128)S(1)}, u32[]{:S(2)}, u32[]{:S(2)}) collective-permute-start(f32[8,48,128]{2,1,0:T(8,128)S(1)} %all_to_all.23.got), channel_id=1, source_target_pairs={{0,1},{1,0},{2,3},{3,2},{4,5},{5,4},{6,7},{7,6},{8,9},{9,8},{10,11... | collective-permute-start | bytes 589832 | tf_op jit(solution)/shard_map/ppermute | solution.py:727
  66.2 9.4 %collective-permute-start.3 = (f32[8,16,128]{2,1,0:T(8,128)S(1)}, f32[8,16,128]{2,1,0:T(8,128)S(1)}, u32[]{:S(2)}, u32[]{:S(2)}) collective-permute-start(f32[8,16,128]{2,1,0:T(8,128)S(1)} %get-tuple-element.33), channel_id=1, source_target_pairs={{0,4},{8,12},{4,0},{12,8},{1,5},{9,13},{5,1},{13,9},{2,6},{10,14},... | collective-permute-start | bytes 196616 | tf_op jit(solution)/shard_map/ppermute | solution.py:747
  66.6 8.9 %collective-permute-start.4 = (f32[8,16,128]{2,1,0:T(8,128)S(1)}, f32[8,16,128]{2,1,0:T(8,128)S(1)}, u32[]{:S(2)}, u32[]{:S(2)}) collective-permute-start(f32[8,16,128]{2,1,0:T(8,128)S(1)} %get-tuple-element.34), channel_id=1, source_target_pairs={{4,8},{8,4},{5,9},{9,5},{6,10},{10,6},{7,11},{11,7},{20,24},{24,20... | collective-permute-start | bytes 196616 | tf_op jit(solution)/shard_map/ppermute | solution.py:748
  71.5 4.1 %collective-permute-start.6 = (f32[128,128]{1,0:T(8,128)S(1)}, f32[128,128]{1,0:T(8,128)S(1)}, u32[]{:S(2)}, u32[]{:S(2)}) collective-permute-start(f32[128,128]{1,0:T(8,128)S(1)} %get-tuple-element.36), channel_id=1, source_target_pairs={{0,1},{1,0},{2,3},{3,2},{4,5},{5,4},{6,7},{7,6},{8,9},{9,8},{10,11... | collective-permute-start | bytes 196616 | tf_op jit(solution)/shard_map/ppermute | solution.py:750
  71.6 4.0 %collective-permute-start.5 = (f32[8,8,128]{2,1,0:T(8,128)S(1)}, f32[8,8,128]{2,1,0:T(8,128)S(1)}, u32[]{:S(2)}, u32[]{:S(2)}) collective-permute-start(f32[8,8,128]{2,1,0:T(8,128)S(1)} %get-tuple-element.35), channel_id=1, source_target_pairs={{0,2},{2,0},{1,3},{3,1},{4,6},{6,4},{5,7},{7,5},{8,10},{10,8},{9,1... | collective-permute-start | bytes 98312 | tf_op jit(solution)/shard_map/ppermute | solution.py:749

commit v5 on v4

--- a/solution.py
+++ b/solution.py
@@ -274,14 +274,17 @@
         turned[f] = own[f].T
 
 
-def prepare_kernel(pack, turned, stat, oth, place, send, rest, ext):
+def prepare_kernel(
+    pack, turned, stat, image_o, mask_o, labels_o, place, send, rest, code_o, ext
+):
     peers = send.shape[0]
     step = LANES // peers
     first = place[2] == 0
-    row = stat[0:1, :] + stat_row(class_sums(oth[M], oth))
+    code_o[...] = jnp.where(mask_o[...] > 0, labels_o[...], K).astype(jnp.float32)
+    row = stat[0:1, :] + stat_row(class_sums(code_o[...], image_o))
     for f in range(M + 1):
         blank = jnp.full((SUB, LANES), float(K) if f == M else 0.0, jnp.float32)
-        other = oth[f].T
+        other = (image_o[f] if f < M else code_o[...]).T
         ext[f, 0:MARGIN, :] = jnp.where(first, blank, other[LANES - MARGIN :, :])
         ext[f, MARGIN : MARGIN + LANES, :] = turned[f]
         ext[f, MARGIN + LANES :, :] = jnp.where(first, other[:MARGIN, :], blank)
@@ -295,12 +298,11 @@
         rest[p, 2:4, :] = ext[M, at + step + 1 : at + step + 3, :]
 
 
-def column_kernel(pack, own, oth, got, rest, table, send, flat, out):
+def column_kernel(pack, own, image_o, code_o, got, rest, table, send, flat, out):
     peers = send.shape[0]
     step = LANES // peers
     means = mean_rows(peer_sum(got, pack.stat))
-    for h, ref in enumerate((own, oth)):
-        code = ref[M]
+    for h, (ref, code) in enumerate(((own, own[M]), (image_o, code_o[...]))):
         flags = [code == float(k) for k in range(K)]
         for m in range(M):
             center = jnp.zeros_like(code)
@@ -433,21 +435,11 @@
             inside = (codes[j] < float(K)).astype(jnp.float32)
             for k, value in enumerate(soft(logits, inside)):
                 two[k, j] = value
-    sums = [[jnp.zeros((SUB, LANES), jnp.float32) for _ in range(STATS)] for _ in range(K)]
     for sb in range(ns):
         for rb in range(nr):
             j = rb * ns + sb
-            values = [shaded[j, m, EDGE : EDGE + core, :] for m in range(M)]
             totals = []
             for k in range(K):
-                here = two[k, j, EDGE : EDGE + core, :]
-                keep[k, j] = here
-                line = sums[k]
-                line[0] = line[0] + fold(here)
-                for m in range(M):
-                    value = here * values[m]
-                    line[1 + m] = line[1 + m] + fold(value)
-                    line[1 + M + m] = line[1 + M + m] + fold(value * values[m])
                 near = around(
                     lambda a, b: two[k, b * ns + a, EDGE : EDGE + core, :], sb, rb, grid, rows, 0.0
                 )
@@ -458,33 +450,61 @@
                 totals.append(functools.reduce(jnp.add, near))
             for k in range(K - 1):
                 send[j, k * core : (k + 1) * core, :] = totals[k] - totals[K - 1]
+    sums = []
+    for k in range(K):
+        line = [jnp.zeros((SUB, LANES), jnp.float32) for _ in range(STATS)]
+        for j in range(peers):
+            here = two[k, j, EDGE : EDGE + core, :]
+            keep[k, j] = here
+            line[0] = line[0] + fold(here)
+            for m in range(M):
+                field = shaded[j, m, EDGE : EDGE + core, :]
+                value = here * field
+                line[1 + m] = line[1 + m] + fold(value)
+                line[1 + M + m] = line[1 + M + m] + fold(value * field)
+        sums.append([jnp.sum(x, axis=0, keepdims=True) for x in line])
     row = stat_row(sums)
     for p in range(peers):
         send[p, (K - 1) * core : (K - 1) * core + 1, :] = row
 
 
-def residual_kernel(
-    pack, grid, stat_a, stat_b, keep, raw, slab_table, row_table, send, first, second
-):
+def early_residual_kernel(pack, grid, keep, raw, slab_table, row_table, out, first, second):
     ns, nr = grid
     core = pack.core
-    means = mean_rows(stat_a[...] + stat_b[...])
+    fields = M + K
     for sb in range(ns):
         for rb in range(nr):
             j = rb * ns + sb
-            for m in range(M):
-                base = m * pack.wide + 2
-                field = raw[j, base : base + core, :]
-                total = jnp.zeros_like(field)
-                for k in range(K):
-                    total = total + keep[k, j] * (field - means[m][k : k + 1, :])
-                base = (rb * M + m) * core
-                first[base : base + core, sb * LANES : (sb + 1) * LANES] = total
-    rows = M * core
-    done = slab_row_filter(rows, slab_table, row_table, first, second, grid)
+            shares = [keep[k, j] for k in range(K)]
+            total = functools.reduce(jnp.add, shares)
+            span = slice(sb * LANES, (sb + 1) * LANES)
+            for f in range(fields):
+                line = (rb * fields + f) * core
+                if f < M:
+                    base = f * pack.wide + 2
+                    value = raw[j, base : base + core, :] * total
+                else:
+                    value = shares[f - M]
+                first[line : line + core, span] = value
+    out[...] = slab_row_filter(fields * core, slab_table, row_table, first, second, grid)
+
+
+def residual_kernel(pack, grid, stat_a, stat_b, early, send, stat):
+    ns, nr = grid
+    core = pack.core
+    row = stat_a[...] + stat_b[...]
+    stat[...] = wide(row)
+    means = mean_rows(row)
     for sb in range(ns):
         for rb in range(nr):
-            send[rb * ns + sb] = done[sb * rows : (sb + 1) * rows, rb * LANES : (rb + 1) * LANES]
+            base = sb * (M + K) * core
+            span = slice(rb * LANES, (rb + 1) * LANES)
+            parts = [early[base + f * core : base + (f + 1) * core, span] for f in range(M + K)]
+            for m in range(M):
+                total = parts[m]
+                for k in range(K):
+                    total = total - parts[M + k] * means[m][k : k + 1, :]
+                send[rb * ns + sb, m * core : (m + 1) * core, :] = total
 
 
 def columns_of(ref, m, core):
@@ -505,8 +525,7 @@
     got,
     near,
     own,
-    stat_a,
-    stat_b,
+    stat,
     table,
     place,
     bias,
@@ -520,7 +539,7 @@
 ):
     core = got.shape[1] // M
     slabs = LANES // rows
-    means, halves, shift = class_stats(stat_a[...] + stat_b[...])
+    means, halves, shift = class_stats(stat[0:1, :])
     for m in range(M):
         centers[:, m : m + 1] = means[m][:, :1]
         bias[m] = field[m] + dot(
@@ -603,12 +622,11 @@
         inside = (own[M, low:high, :] < float(K)).astype(jnp.float32)
         for k, value in enumerate(soft(logits, inside)):
             post[k, low:high, :] = value.astype(jnp.bfloat16)
-        if s % 2:
-            span = pl.ds(low - rows, 2 * rows)
-            copies.append(
-                pltpu.make_async_copy(post.at[:, span, :], post_h.at[:, span, :], sems.at[s // 2])
-            )
-            copies[-1].start()
+        span = pl.ds(low, rows)
+        copies.append(
+            pltpu.make_async_copy(post.at[:, span, :], post_h.at[:, span, :], sems.at[s])
+        )
+        copies[-1].start()
     for copy in copies:
         copy.wait()
 
@@ -676,7 +694,9 @@
 
     code = jnp.where(brain_mask > 0, labels, K).astype(f32)
     own = jnp.concatenate([image, code[None]]).reshape(M + 1, LANES, columns)
-    oth = lax.ppermute(own, "col", swap)
+    image_o = lax.ppermute(image.reshape(M, LANES, columns), "col", swap)
+    mask_o = lax.ppermute(brain_mask.reshape(LANES, columns), "col", swap)
+    labels_o = lax.ppermute(labels.reshape(LANES, columns), "col", swap)
 
     def trade(x):
         return lax.all_to_all(x, ("row", "slab"), split_axis=0, concat_axis=0, tiled=True)
@@ -684,17 +704,21 @@
     turned, stat = call(
         own_kernel, [((M + 1, columns, LANES), f32), ((SUB, LANES), f32)]
     )(own)
-    sent, rest = call(
+    sent, rest, code_o = call(
         functools.partial(prepare_kernel, pack),
-        [((peers, padded(pack.stat + 1), LANES), f32), ((peers, SUB, LANES), f32)],
+        [
+            ((peers, padded(pack.stat + 1), LANES), f32),
+            ((peers, SUB, LANES), f32),
+            ((LANES, columns), f32),
+        ],
         [(M + 1, columns + 2 * MARGIN, LANES)],
-    )(turned, stat, oth, place)
+    )(turned, stat, image_o, mask_o, labels_o, place)
     raw = trade(sent)
     (sent,) = call(
         functools.partial(column_kernel, pack),
         [((peers, padded(pack.code + 4), LANES), f32)],
         [(M * LANES, 2 * columns), (columns + 2 * MARGIN, M * LANES)],
-    )(own, oth, raw, rest, spread)
+    )(own, image_o, code_o, raw, rest, spread)
     got = trade(sent)
     sent, keep = call(
         functools.partial(pencil_kernel, pack, grid, rows),
@@ -716,13 +740,18 @@
         micros=4,
     )(got, raw, slab_table, row_table)
     near = trade(sent)
+    (early,) = call(
+        functools.partial(early_residual_kernel, pack, grid),
+        [((ns * (M + K) * core, nr * LANES), f32)],
+        [(nr * (M + K) * core, ns * LANES), (ns * (M + K) * core, nr * LANES)],
+        micros=8,
+    )(keep, raw, slab_table, row_table)
     stat_a = jnp.sum(near[:, (K - 1) * core : (K - 1) * core + 1, :], axis=0)
     stat_b = lax.ppermute(stat_a, "col", swap)
-    (sent,) = call(
+    sent, stat = call(
         functools.partial(residual_kernel, pack, grid),
-        [((peers, M * core, LANES), f32)],
-        [(nr * M * core, ns * LANES), (ns * M * core, nr * LANES)],
-    )(stat_a, stat_b, keep, raw, slab_table, row_table)
+        [((peers, M * core, LANES), f32), ((SUB, LANES), f32)],
+    )(stat_a, stat_b, early)
     got = trade(sent)
     yours = lax.ppermute(got, "col", swap)
     field, near = call(
@@ -741,7 +770,7 @@
             ((LANES, LANES), f32),
         ],
         micros=2,
-    )(field, yours, near, own, stat_a, stat_b, gather, place)
+    )(field, yours, near, own, stat, gather, place)
     pairs = [(i, i + 1) for i in range(0, ns - 1, 2)]
     between = [(i, i + 1) for i in range(1, ns - 1, 2)]
     up = lax.ppermute(up, "slab", pairs + [(b, a) for a, b in pairs])
@@ -759,7 +788,7 @@
         [((K, LANES, columns), jnp.bfloat16)],
         [
             pltpu.VMEM((K, LANES, columns), jnp.bfloat16),
-            pltpu.SemaphoreType.DMA((slabs // 2,)),
+            pltpu.SemaphoreType.DMA((slabs,)),
         ],
         far_out=(0,),
     )(inner, own, up, down, side, edge, place)

time: 76.9 us -> 76.7 us (level)
  waiting for transfers between devices: 4.99 us -> 2.95 us
    ppermute x1, waiting for transfers between devices: 1.15 us -> 0.01 us  [pencils(): stat_b = lax.ppermute(stat_a, 'col', swap)]
    ppermute x1 -> x3, waiting for transfers between devices: 0.95 us -> 0.08 us  [the longest x1 0.08 us: pencils(): image_o = lax.ppermute(image.reshape(M, LANES, columns), 'col', swap)]
    pallas_call x9 -> x10, Pallas kernels: 8.31 us -> 9.01 us  [run(): pl.pallas_call(kernel, out_shape=shapes, in_specs=[vmem] * len(args), out...]
  transfers between devices with their start and end apart: 7 -> 9, of which waited for: 4 -> 3; matrix products, arithmetic and copies ran while one was open for 1% -> 2% of each run, Pallas kernels for 2% -> 4%
where the time goes in v5:
time: 76.7 us; the launch traced here: 76.3 us
  blocking collectives  55 us (72%)
  Pallas kernels  9.01 us (12%)
  starting transfers between devices  6.8 us (9%)
  waiting for transfers between devices  2.95 us (4%)
  other arithmetic  1 us (1%)
  between operations  0.79 us (1%)
    all_to_all x4, blocking collectives, trade(): lax.all_to_all(x, ('row', 'slab'), split_axis=0, concat_axis=0, tiled=True)  55 us
    pallas_call x10, Pallas kernels, run(): pl.pallas_call(kernel, out_shape=shapes, in_specs=[vmem] * len(args), out...  9.01 us
    ppermute x1, starting transfers between devices, pencils(): down = lax.ppermute(down, 'slab', between + [(b, a) for a, b in between])  4.9 us
    ppermute x1, waiting for transfers between devices, pencils(): side = lax.ppermute(side, 'row', swap)  1.75 us
  transfers between devices with their start and end apart: 9, of which 3 were waited for; matrix products, arithmetic and copies ran while one was open for 2% of the time, Pallas kernels for 4%

profile of v5, /device:TPU:16, one launch (start us, length us, event | category | flops | bytes accessed | tf_op | source)
XLA Modules:
  0.0 76.3 jit_solution(14907706108326085290)
XLA Ops:
  0.6 0.1 collective-permute-start.2
  0.7 0.5 collective-permute-start.1
  1.2 0.1 collective-permute-start
  1.3 0.9 %select_convert_fusion = f32[8,16,128]{2,1,0:T(8,128)S(1)} fusion(s32[8,16,128]{2,1,0:T(8,128)} %param.9, s32[8,16,128]{2,1,0:T(8,128)} %param.8), kind=kLoop, calls=%fused_computation.1 | loop fusion | flops 49152 | bytes 196608 | tf_op jit(solution)/shard_map/convert_element_type | solution.py:695
  2.2 0.5 own_kernel.1
  2.7 0.1 pad_add_fusion
  2.8 0.1 collective-permute-done.image_o
  2.9 0.1 broadcast_in_dim.12.place
  2.9 0.5 prepare_kernel.1
  3.4 0.0 copy-start.3
  3.5 15.3 %all_to_all.20.got.raw = f32[8,80,128]{2,1,0:T(8,128)S(1)} all-to-all(f32[8,80,128]{2,1,0:T(8,128)S(1)} %get-tuple-element.27), channel_id=1, replica_groups=mesh['grp'=2,'slab'=4,'row'=2,'col'=2] {'row','slab'}, dimensions={0} | all-to-all | bytes 655360 | tf_op jit(solution)/shard_map/all_to_all | solution.py:702
  18.8 0.6 column_kernel.1
  19.4 11.7 %all_to_all.21.got = f32[8,64,128]{2,1,0:T(8,128)S(1)} all-to-all(f32[8,64,128]{2,1,0:T(8,128)S(1)} %column_kernel.1), channel_id=1, replica_groups=mesh['grp'=2,'slab'=4,'row'=2,'col'=2] {'row','slab'}, dimensions={0} | all-to-all | bytes 524288 | tf_op jit(solution)/shard_map/all_to_all | solution.py:702
  31.1 3.0 %pencil_kernel.1 = (f32[8,120,128]{2,1,0:T(8,128)S(1)}, f32[8,8,16,128]{3,2,1,0:T(8,128)S(1)}) custom-call(f32[8,64,128]{2,1,0:T(8,128)S(1)} %all_to_all.21.got, f32[8,80,128]{2,1,0:T(8,128)S(1)} %all_to_all.20.got.raw, bf16[2,512,512]{2,1,0:T(8,128)(2,1)S(1)} %copy-done, bf16[2,256,256]{2,1,0:T(8,128)(2,1)S(1)} %copy-done.1), custom_call_target="tpu_custom_call" | custom-call | flops 40000000 | bytes 1048576 | tf_op jit(solution)/shard_map/pencil_kernel/pallas_call | solution.py:651
  34.2 16.3 %all_to_all.22.near = f32[8,120,128]{2,1,0:T(8,128)S(1)} all-to-all(f32[8,120,128]{2,1,0:T(8,128)S(1)} %get-tuple-element.29), channel_id=1, replica_groups=mesh['grp'=2,'slab'=4,'row'=2,'col'=2] {'row','slab'}, dimensions={0} | all-to-all | bytes 983040 | tf_op jit(solution)/shard_map/all_to_all | solution.py:702
  50.5 0.1 collective-permute-start.3
  50.6 1.2 %early_residual_kernel.1.early = f32[704,256]{1,0:T(8,128)S(1)} custom-call(f32[8,8,16,128]{3,2,1,0:T(8,128)S(1)} %get-tuple-element.30.keep, f32[8,80,128]{2,1,0:T(8,128)S(1)} %all_to_all.20.got.raw, bf16[2,512,512]{2,1,0:T(8,128)(2,1)S(1)} %copy-done, bf16[2,256,256]{2,1,0:T(8,128)(2,1)S(1)} %copy-done.1), custom_call_target="tpu_custom_call" | custom-call | flops 80000000 | bytes 1048576 | tf_op jit(solution)/shard_map/early_residual_kernel/pallas_call | solution.py:651
  51.8 0.2 residual_kernel.1
  52.0 0.0 copy-start.2
  52.0 11.7 %all_to_all.23.got = f32[8,48,128]{2,1,0:T(8,128)S(1)} all-to-all(f32[8,48,128]{2,1,0:T(8,128)S(1)} %get-tuple-element.31), channel_id=1, replica_groups=mesh['grp'=2,'slab'=4,'row'=2,'col'=2] {'row','slab'}, dimensions={0} | all-to-all | bytes 393216 | tf_op jit(solution)/shard_map/all_to_all | solution.py:702
  63.7 0.0 collective-permute-start.4
  63.7 0.3 half_kernel.1
  64.0 1.1 %collective-permute-done.4.got = f32[8,48,128]{2,1,0:T(8,128)S(1)} collective-permute-done((f32[8,48,128]{2,1,0:T(8,128)S(1)}, f32[8,48,128]{2,1,0:T(8,128)S(1)}, u32[]{:S(2)}, u32[]{:S(2)}) %collective-permute-start.4) | collective-permute-done | bytes 196640 | tf_op jit(solution)/shard_map/ppermute | solution.py:756
  65.1 0.7 third_kernel.1
  65.8 0.5 collective-permute-start.5
  66.3 4.9 %collective-permute-start.6 = (f32[8,16,128]{2,1,0:T(8,128)S(1)}, f32[8,16,128]{2,1,0:T(8,128)S(1)}, u32[]{:S(2)}, u32[]{:S(2)}) collective-permute-start(f32[8,16,128]{2,1,0:T(8,128)S(1)} %get-tuple-element.40), channel_id=1, source_target_pairs={{4,8},{8,4},{5,9},{9,5},{6,10},{10,6},{7,11},{11,7},{20,24},{24,20... | collective-permute-start | bytes 196616 | tf_op jit(solution)/shard_map/ppermute | solution.py:777
  71.2 0.1 collective-permute-start.8
  71.3 0.6 collective-permute-start.7
  71.9 0.7 copy.10
  72.6 1.0 %inner_kernel.1 = (f32[8,128,128]{2,1,0:T(8,128)S(1)}, f32[3,128,128]{2,1,0:T(8,128)}) custom-call(f32[8,128,128]{2,1,0:T(8,128)S(1)} %get-tuple-element.35.dens, f32[8,128,128]{2,1,0:T(8,128)S(1)} %get-tuple-element.36.belief, f32[3,128,128]{2,1,0:T(8,128)S(1)} %get-tuple-element.37.bias), custom_call_target="tpu_custom_call" | custom-call | flops 10000000 | bytes 1048576 | tf_op jit(solution)/shard_map/inner_kernel/pallas_call | solution.py:651
  73.5 1.8 %collective-permute-done.7.side = f32[8,8,128]{2,1,0:T(8,128)S(1)} collective-permute-done((f32[8,8,128]{2,1,0:T(8,128)S(1)}, f32[8,8,128]{2,1,0:T(8,128)S(1)}, u32[]{:S(2)}, u32[]{:S(2)}) %collective-permute-start.7) | collective-permute-done | bytes 32800 | tf_op jit(solution)/shard_map/ppermute | solution.py:778
  75.3 1.0 %last_kernel.1 = bf16[8,128,128]{2,1,0:T(8,128)(2,1)} custom-call(f32[8,128,128]{2,1,0:T(8,128)S(1)} %get-tuple-element.38.inner, f32[4,128,128]{2,1,0:T(8,128)S(1)} %pad_maximum_fusion.own, f32[8,16,128]{2,1,0:T(8,128)S(1)} %collective-permute-done.5.up, f32[8,16,128]{2,1,0:T(8,128)S(1)} %collective-permute-done.6.down, ...), custom_call_target="tpu_custom_call" | custom-call | flops 10000000 | bytes 1048576 | tf_op jit(solution)/shard_map/last_kernel/pallas_call | solution.py:651
  (16 shorter events, 0.1 us)
Async XLA Ops:
  0.6 1.6 %copy-start.4 = (f32[3,8,16,128]{3,2,1,0:T(8,128)S(1)}, f32[3,8,16,128]{3,2,1,0:T(8,128)}, u32[]{:S(2)}) copy-start(f32[3,8,16,128]{3,2,1,0:T(8,128)} %param.7) | copy-start | bytes 589828
  0.6 2.1 %collective-permute-start.2 = (s32[128,128]{1,0:T(8,128)}, s32[128,128]{1,0:T(8,128)S(1)}, u32[]{:S(2)}, u32[]{:S(2)}) collective-permute-start(s32[128,128]{1,0:T(8,128)} %bitcast.16), channel_id=1, source_target_pairs={{0,1},{1,0},{2,3},{3,2},{4,5},{5,4},{6,7},{7,6},{8,9},{9,8},{10,11... | collective-permute-start | bytes 196616 | tf_op jit(solution)/shard_map/ppermute | solution.py:699
  0.7 2.1 %collective-permute-start.1 = (s32[128,128]{1,0:T(8,128)}, s32[128,128]{1,0:T(8,128)S(1)}, u32[]{:S(2)}, u32[]{:S(2)}) collective-permute-start(s32[128,128]{1,0:T(8,128)} %bitcast.17), channel_id=1, source_target_pairs={{0,1},{1,0},{2,3},{3,2},{4,5},{5,4},{6,7},{7,6},{8,9},{9,8},{10,11... | collective-permute-start | bytes 196616 | tf_op jit(solution)/shard_map/ppermute | solution.py:698
  1.2 1.7 %collective-permute-start = (f32[3,128,128]{2,1,0:T(8,128)}, f32[3,128,128]{2,1,0:T(8,128)S(1)}, u32[]{:S(2)}, u32[]{:S(2)}) collective-permute-start(f32[3,128,128]{2,1,0:T(8,128)} %bitcast.14), channel_id=1, source_target_pairs={{0,1},{1,0},{2,3},{3,2},{4,5},{5,4},{6,7},{7,6},{8,9},{9,8},{10,11... | collective-permute-start | bytes 589832 | tf_op jit(solution)/shard_map/ppermute | solution.py:697
  3.4 15.3 %copy-start.3 = (bf16[2,144,256]{2,1,0:T(8,128)(2,1)S(1)}, bf16[2,144,256]{2,1,0:T(8,128)(2,1)}, u32[]{:S(2)}) copy-start(bf16[2,144,256]{2,1,0:T(8,128)(2,1)} %constant.37.clone.table) | copy-start | bytes 442372
  18.8 12.4 %copy-start = (bf16[2,512,512]{2,1,0:T(8,128)(2,1)S(1)}, bf16[2,512,512]{2,1,0:T(8,128)(2,1)}, u32[]{:S(2)}) copy-start(bf16[2,512,512]{2,1,0:T(8,128)(2,1)} %constant.38.clone.slab_table) | copy-start | bytes 3145732
  19.4 11.7 %copy-start.1 = (bf16[2,256,256]{2,1,0:T(8,128)(2,1)S(1)}, bf16[2,256,256]{2,1,0:T(8,128)(2,1)}, u32[]{:S(2)}) copy-start(bf16[2,256,256]{2,1,0:T(8,128)(2,1)} %constant.39.clone.row_table) | copy-start | bytes 786436
  50.5 1.3 %collective-permute-start.3 = (f32[1,128]{1,0:T(1,128)S(1)}, f32[1,128]{1,0:T(1,128)S(1)}, u32[]{:S(2)}, u32[]{:S(2)}) collective-permute-start(f32[1,128]{1,0:T(1,128)S(1)} %bitcast.10), channel_id=1, source_target_pairs={{0,1},{1,0},{2,3},{3,2},{4,5},{5,4},{6,7},{7,6},{8,9},{9,8},{10,11... | collective-permute-start | bytes 1544 | tf_op jit(solution)/shard_map/ppermute | solution.py:750
  52.0 11.7 %copy-start.2 = (bf16[2,256,128]{2,1,0:T(8,128)(2,1)S(1)}, bf16[2,256,128]{2,1,0:T(8,128)(2,1)}, u32[]{:S(2)}) copy-start(bf16[2,256,128]{2,1,0:T(8,128)(2,1)} %constant.40.clone.table) | copy-start | bytes 393220
  63.7 1.4 %collective-permute-start.4 = (f32[8,48,128]{2,1,0:T(8,128)S(1)}, f32[8,48,128]{2,1,0:T(8,128)S(1)}, u32[]{:S(2)}, u32[]{:S(2)}) collective-permute-start(f32[8,48,128]{2,1,0:T(8,128)S(1)} %all_to_all.23.got), channel_id=1, source_target_pairs={{0,1},{1,0},{2,3},{3,2},{4,5},{5,4},{6,7},{7,6},{8,9},{9,8},{10,11... | collective-permute-start | bytes 589832 | tf_op jit(solution)/shard_map/ppermute | solution.py:756
  65.8 9.4 %collective-permute-start.5 = (f32[8,16,128]{2,1,0:T(8,128)S(1)}, f32[8,16,128]{2,1,0:T(8,128)S(1)}, u32[]{:S(2)}, u32[]{:S(2)}) collective-permute-start(f32[8,16,128]{2,1,0:T(8,128)S(1)} %get-tuple-element.39), channel_id=1, source_target_pairs={{0,4},{8,12},{4,0},{12,8},{1,5},{9,13},{5,1},{13,9},{2,6},{10,14},... | collective-permute-start | bytes 196616 | tf_op jit(solution)/shard_map/ppermute | solution.py:776
  66.3 9.0 %collective-permute-start.6 = (f32[8,16,128]{2,1,0:T(8,128)S(1)}, f32[8,16,128]{2,1,0:T(8,128)S(1)}, u32[]{:S(2)}, u32[]{:S(2)}) collective-permute-start(f32[8,16,128]{2,1,0:T(8,128)S(1)} %get-tuple-element.40), channel_id=1, source_target_pairs={{4,8},{8,4},{5,9},{9,5},{6,10},{10,6},{7,11},{11,7},{20,24},{24,20... | collective-permute-start | bytes 196616 | tf_op jit(solution)/shard_map/ppermute | solution.py:777
  71.2 4.1 %collective-permute-start.8 = (f32[128,128]{1,0:T(8,128)S(1)}, f32[128,128]{1,0:T(8,128)S(1)}, u32[]{:S(2)}, u32[]{:S(2)}) collective-permute-start(f32[128,128]{1,0:T(8,128)S(1)} %get-tuple-element.42), channel_id=1, source_target_pairs={{0,1},{1,0},{2,3},{3,2},{4,5},{5,4},{6,7},{7,6},{8,9},{9,8},{10,11... | collective-permute-start | bytes 196616 | tf_op jit(solution)/shard_map/ppermute | solution.py:779
  71.3 4.0 %collective-permute-start.7 = (f32[8,8,128]{2,1,0:T(8,128)S(1)}, f32[8,8,128]{2,1,0:T(8,128)S(1)}, u32[]{:S(2)}, u32[]{:S(2)}) collective-permute-start(f32[8,8,128]{2,1,0:T(8,128)S(1)} %get-tuple-element.41), channel_id=1, source_target_pairs={{0,2},{2,0},{1,3},{3,1},{4,6},{6,4},{5,7},{7,5},{8,10},{10,8},{9,1... | collective-permute-start | bytes 98312 | tf_op jit(solution)/shard_map/ppermute | solution.py:778

commit v6 on v5

--- a/solution.py
+++ b/solution.py
@@ -468,43 +468,28 @@
         send[p, (K - 1) * core : (K - 1) * core + 1, :] = row
 
 
-def early_residual_kernel(pack, grid, keep, raw, slab_table, row_table, out, first, second):
+def residual_kernel(
+    pack, grid, stat_a, stat_b, keep, raw, slab_table, row_table, send, first, second
+):
     ns, nr = grid
     core = pack.core
-    fields = M + K
+    means = mean_rows(stat_a[...] + stat_b[...])
     for sb in range(ns):
         for rb in range(nr):
             j = rb * ns + sb
-            shares = [keep[k, j] for k in range(K)]
-            total = functools.reduce(jnp.add, shares)
-            span = slice(sb * LANES, (sb + 1) * LANES)
-            for f in range(fields):
-                line = (rb * fields + f) * core
-                if f < M:
-                    base = f * pack.wide + 2
-                    value = raw[j, base : base + core, :] * total
-                else:
-                    value = shares[f - M]
-                first[line : line + core, span] = value
-    out[...] = slab_row_filter(fields * core, slab_table, row_table, first, second, grid)
-
-
-def residual_kernel(pack, grid, stat_a, stat_b, early, send, stat):
-    ns, nr = grid
-    core = pack.core
-    row = stat_a[...] + stat_b[...]
-    stat[...] = wide(row)
-    means = mean_rows(row)
+            for m in range(M):
+                base = m * pack.wide + 2
+                field = raw[j, base : base + core, :]
+                total = jnp.zeros_like(field)
+                for k in range(K):
+                    total = total + keep[k, j] * (field - means[m][k : k + 1, :])
+                base = (rb * M + m) * core
+                first[base : base + core, sb * LANES : (sb + 1) * LANES] = total
+    rows = M * core
+    done = slab_row_filter(rows, slab_table, row_table, first, second, grid)
     for sb in range(ns):
         for rb in range(nr):
-            base = sb * (M + K) * core
-            span = slice(rb * LANES, (rb + 1) * LANES)
-            parts = [early[base + f * core : base + (f + 1) * core, span] for f in range(M + K)]
-            for m in range(M):
-                total = parts[m]
-                for k in range(K):
-                    total = total - parts[M + k] * means[m][k : k + 1, :]
-                send[rb * ns + sb, m * core : (m + 1) * core, :] = total
+            send[rb * ns + sb] = done[sb * rows : (sb + 1) * rows, rb * LANES : (rb + 1) * LANES]
 
 
 def columns_of(ref, m, core):
@@ -525,7 +510,8 @@
     got,
     near,
     own,
-    stat,
+    stat_a,
+    stat_b,
     table,
     place,
     bias,
@@ -539,7 +525,7 @@
 ):
     core = got.shape[1] // M
     slabs = LANES // rows
-    means, halves, shift = class_stats(stat[0:1, :])
+    means, halves, shift = class_stats(stat_a[...] + stat_b[...])
     for m in range(M):
         centers[:, m : m + 1] = means[m][:, :1]
         bias[m] = field[m] + dot(
@@ -740,18 +726,13 @@
         micros=4,
     )(got, raw, slab_table, row_table)
     near = trade(sent)
-    (early,) = call(
-        functools.partial(early_residual_kernel, pack, grid),
-        [((ns * (M + K) * core, nr * LANES), f32)],
-        [(nr * (M + K) * core, ns * LANES), (ns * (M + K) * core, nr * LANES)],
-        micros=8,
-    )(keep, raw, slab_table, row_table)
     stat_a = jnp.sum(near[:, (K - 1) * core : (K - 1) * core + 1, :], axis=0)
     stat_b = lax.ppermute(stat_a, "col", swap)
-    sent, stat = call(
+    (sent,) = call(
         functools.partial(residual_kernel, pack, grid),
-        [((peers, M * core, LANES), f32), ((SUB, LANES), f32)],
-    )(stat_a, stat_b, early)
+        [((peers, M * core, LANES), f32)],
+        [(nr * M * core, ns * LANES), (ns * M * core, nr * LANES)],
+    )(stat_a, stat_b, keep, raw, slab_table, row_table)
     got = trade(sent)
     yours = lax.ppermute(got, "col", swap)
     field, near = call(
@@ -770,7 +751,7 @@
             ((LANES, LANES), f32),
         ],
         micros=2,
-    )(field, yours, near, own, stat, gather, place)
+    )(field, yours, near, own, stat_a, stat_b, gather, place)
     pairs = [(i, i + 1) for i in range(0, ns - 1, 2)]
     between = [(i, i + 1) for i in range(1, ns - 1, 2)]
     up = lax.ppermute(up, "slab", pairs + [(b, a) for a, b in pairs])

time: 76.7 us -> 76.8 us (level)
  waiting for transfers between devices: 2.95 us -> 4.12 us
    ppermute x1, waiting for transfers between devices: 0.01 us -> 1.15 us  [pencils(): stat_b = lax.ppermute(stat_a, 'col', swap)]
    pallas_call x10 -> x9, Pallas kernels: 9.01 us -> 8.35 us  [run(): pl.pallas_call(kernel, out_shape=shapes, in_specs=[vmem] * len(args), out...]
  transfers between devices with their start and end apart: 9 -> 9, of which waited for: 3 -> 4; matrix products, arithmetic and copies ran while one was open for 2% -> 2% of each run, Pallas kernels for 4% -> 2%
where the time goes in v6:
time: 76.8 us; the launch traced here: 76.5 us
  blocking collectives  54.7 us (71%)
  Pallas kernels  8.35 us (11%)
  starting transfers between devices  6.74 us (9%)
  waiting for transfers between devices  4.12 us (5%)
  other arithmetic  1 us (1%)
  between operations  0.78 us (1%)
    all_to_all x4, blocking collectives, trade(): lax.all_to_all(x, ('row', 'slab'), split_axis=0, concat_axis=0, tiled=True)  54.7 us
    pallas_call x9, Pallas kernels, run(): pl.pallas_call(kernel, out_shape=shapes, in_specs=[vmem] * len(args), out...  8.35 us
    ppermute x1, starting transfers between devices, pencils(): down = lax.ppermute(down, 'slab', between + [(b, a) for a, b in between])  4.87 us
    ppermute x1, waiting for transfers between devices, pencils(): side = lax.ppermute(side, 'row', swap)  1.75 us
  transfers between devices with their start and end apart: 9, of which 4 were waited for; matrix products, arithmetic and copies ran while one was open for 2% of the time, Pallas kernels for 2%

profile of v6, /device:TPU:16, one launch (start us, length us, event | category | flops | bytes accessed | tf_op | source)
XLA Modules:
  0.0 76.5 jit_solution(10998514800686424618)
XLA Ops:
  0.6 0.1 collective-permute-start.2
  0.7 0.5 collective-permute-start.1
  1.2 0.1 collective-permute-start
  1.3 0.9 %select_convert_fusion = f32[8,16,128]{2,1,0:T(8,128)S(1)} fusion(s32[8,16,128]{2,1,0:T(8,128)} %param.9, s32[8,16,128]{2,1,0:T(8,128)} %param.8), kind=kLoop, calls=%fused_computation.1 | loop fusion | flops 49152 | bytes 196608 | tf_op jit(solution)/shard_map/convert_element_type | solution.py:681
  2.2 0.5 own_kernel.1
  2.7 0.1 pad_add_fusion
  2.8 0.1 collective-permute-done.image_o
  2.9 0.1 broadcast_in_dim.12.place
  2.9 0.5 prepare_kernel.1
  3.4 0.0 copy-start.3
  3.5 15.3 %all_to_all.20.got.raw = f32[8,80,128]{2,1,0:T(8,128)S(1)} all-to-all(f32[8,80,128]{2,1,0:T(8,128)S(1)} %get-tuple-element.25), channel_id=1, replica_groups=mesh['grp'=2,'slab'=4,'row'=2,'col'=2] {'row','slab'}, dimensions={0} | all-to-all | bytes 655360 | tf_op jit(solution)/shard_map/all_to_all | solution.py:688
  18.8 0.6 column_kernel.1
  19.4 0.0 copy-start.1
  19.4 11.7 %all_to_all.21.got = f32[8,64,128]{2,1,0:T(8,128)S(1)} all-to-all(f32[8,64,128]{2,1,0:T(8,128)S(1)} %column_kernel.1), channel_id=1, replica_groups=mesh['grp'=2,'slab'=4,'row'=2,'col'=2] {'row','slab'}, dimensions={0} | all-to-all | bytes 524288 | tf_op jit(solution)/shard_map/all_to_all | solution.py:688
  31.1 3.0 %pencil_kernel.1 = (f32[8,120,128]{2,1,0:T(8,128)S(1)}, f32[8,8,16,128]{3,2,1,0:T(8,128)S(1)}) custom-call(f32[8,64,128]{2,1,0:T(8,128)S(1)} %all_to_all.21.got, f32[8,80,128]{2,1,0:T(8,128)S(1)} %all_to_all.20.got.raw, bf16[2,512,512]{2,1,0:T(8,128)(2,1)S(1)} %copy-done, bf16[2,256,256]{2,1,0:T(8,128)(2,1)S(1)} %copy-done.1), custom_call_target="tpu_custom_call" | custom-call | flops 40000000 | bytes 1048576 | tf_op jit(solution)/shard_map/pencil_kernel/pallas_call | solution.py:637
  34.2 16.3 %all_to_all.22.near = f32[8,120,128]{2,1,0:T(8,128)S(1)} all-to-all(f32[8,120,128]{2,1,0:T(8,128)S(1)} %get-tuple-element.27), channel_id=1, replica_groups=mesh['grp'=2,'slab'=4,'row'=2,'col'=2] {'row','slab'}, dimensions={0} | all-to-all | bytes 983040 | tf_op jit(solution)/shard_map/all_to_all | solution.py:688
  50.5 0.1 collective-permute-start.3
  50.6 1.1 %collective-permute-done.3.stat_b = f32[1,128]{1,0:T(1,128)S(1)} collective-permute-done((f32[1,128]{1,0:T(1,128)S(1)}, f32[1,128]{1,0:T(1,128)S(1)}, u32[]{:S(2)}, u32[]{:S(2)}) %collective-permute-start.3) | collective-permute-done | bytes 544 | tf_op jit(solution)/shard_map/ppermute | solution.py:730
  51.7 0.7 residual_kernel.1
  52.5 0.0 copy-start.2
  52.5 11.4 %all_to_all.23.got = f32[8,48,128]{2,1,0:T(8,128)S(1)} all-to-all(f32[8,48,128]{2,1,0:T(8,128)S(1)} %residual_kernel.1), channel_id=1, replica_groups=mesh['grp'=2,'slab'=4,'row'=2,'col'=2] {'row','slab'}, dimensions={0} | all-to-all | bytes 393216 | tf_op jit(solution)/shard_map/all_to_all | solution.py:688
  63.8 0.3 half_kernel.1
  64.1 1.1 %collective-permute-done.4.got = f32[8,48,128]{2,1,0:T(8,128)S(1)} collective-permute-done((f32[8,48,128]{2,1,0:T(8,128)S(1)}, f32[8,48,128]{2,1,0:T(8,128)S(1)}, u32[]{:S(2)}, u32[]{:S(2)}) %collective-permute-start.4) | collective-permute-done | bytes 196640 | tf_op jit(solution)/shard_map/ppermute | solution.py:737
  65.3 0.7 third_kernel.1
  66.0 0.5 collective-permute-start.5
  66.5 4.9 %collective-permute-start.6 = (f32[8,16,128]{2,1,0:T(8,128)S(1)}, f32[8,16,128]{2,1,0:T(8,128)S(1)}, u32[]{:S(2)}, u32[]{:S(2)}) collective-permute-start(f32[8,16,128]{2,1,0:T(8,128)S(1)} %get-tuple-element.36), channel_id=1, source_target_pairs={{4,8},{8,4},{5,9},{9,5},{6,10},{10,6},{7,11},{11,7},{20,24},{24,20... | collective-permute-start | bytes 196616 | tf_op jit(solution)/shard_map/ppermute | solution.py:758
  71.4 0.1 collective-permute-start.8
  71.4 0.6 collective-permute-start.7
  72.1 0.7 copy.10
  72.7 1.0 %inner_kernel.1 = (f32[8,128,128]{2,1,0:T(8,128)S(1)}, f32[3,128,128]{2,1,0:T(8,128)}) custom-call(f32[8,128,128]{2,1,0:T(8,128)S(1)} %get-tuple-element.31.dens, f32[8,128,128]{2,1,0:T(8,128)S(1)} %get-tuple-element.32.belief, f32[3,128,128]{2,1,0:T(8,128)S(1)} %get-tuple-element.33.bias), custom_call_target="tpu_custom_call" | custom-call | flops 10000000 | bytes 1048576 | tf_op jit(solution)/shard_map/inner_kernel/pallas_call | solution.py:637
  73.7 1.7 %collective-permute-done.7.side = f32[8,8,128]{2,1,0:T(8,128)S(1)} collective-permute-done((f32[8,8,128]{2,1,0:T(8,128)S(1)}, f32[8,8,128]{2,1,0:T(8,128)S(1)}, u32[]{:S(2)}, u32[]{:S(2)}) %collective-permute-start.7) | collective-permute-done | bytes 32800 | tf_op jit(solution)/shard_map/ppermute | solution.py:759
  75.4 1.0 %last_kernel.1 = bf16[8,128,128]{2,1,0:T(8,128)(2,1)} custom-call(f32[8,128,128]{2,1,0:T(8,128)S(1)} %get-tuple-element.34.inner, f32[4,128,128]{2,1,0:T(8,128)S(1)} %pad_maximum_fusion.own, f32[8,16,128]{2,1,0:T(8,128)S(1)} %collective-permute-done.5.up, f32[8,16,128]{2,1,0:T(8,128)S(1)} %collective-permute-done.6.down, ...), custom_call_target="tpu_custom_call" | custom-call | flops 10000000 | bytes 1048576 | tf_op jit(solution)/shard_map/last_kernel/pallas_call | solution.py:637
  (15 shorter events, 0.1 us)
Async XLA Ops:
  0.6 1.6 %copy-start.4 = (f32[3,8,16,128]{3,2,1,0:T(8,128)S(1)}, f32[3,8,16,128]{3,2,1,0:T(8,128)}, u32[]{:S(2)}) copy-start(f32[3,8,16,128]{3,2,1,0:T(8,128)} %param.7) | copy-start | bytes 589828
  0.6 2.1 %collective-permute-start.2 = (s32[128,128]{1,0:T(8,128)}, s32[128,128]{1,0:T(8,128)S(1)}, u32[]{:S(2)}, u32[]{:S(2)}) collective-permute-start(s32[128,128]{1,0:T(8,128)} %bitcast.17), channel_id=1, source_target_pairs={{0,1},{1,0},{2,3},{3,2},{4,5},{5,4},{6,7},{7,6},{8,9},{9,8},{10,11... | collective-permute-start | bytes 196616 | tf_op jit(solution)/shard_map/ppermute | solution.py:685
  0.7 2.1 %collective-permute-start.1 = (s32[128,128]{1,0:T(8,128)}, s32[128,128]{1,0:T(8,128)S(1)}, u32[]{:S(2)}, u32[]{:S(2)}) collective-permute-start(s32[128,128]{1,0:T(8,128)} %bitcast.18), channel_id=1, source_target_pairs={{0,1},{1,0},{2,3},{3,2},{4,5},{5,4},{6,7},{7,6},{8,9},{9,8},{10,11... | collective-permute-start | bytes 196616 | tf_op jit(solution)/shard_map/ppermute | solution.py:684
  1.2 1.7 %collective-permute-start = (f32[3,128,128]{2,1,0:T(8,128)}, f32[3,128,128]{2,1,0:T(8,128)S(1)}, u32[]{:S(2)}, u32[]{:S(2)}) collective-permute-start(f32[3,128,128]{2,1,0:T(8,128)} %bitcast.15), channel_id=1, source_target_pairs={{0,1},{1,0},{2,3},{3,2},{4,5},{5,4},{6,7},{7,6},{8,9},{9,8},{10,11... | collective-permute-start | bytes 589832 | tf_op jit(solution)/shard_map/ppermute | solution.py:683
  3.4 15.3 %copy-start.3 = (bf16[2,144,256]{2,1,0:T(8,128)(2,1)S(1)}, bf16[2,144,256]{2,1,0:T(8,128)(2,1)}, u32[]{:S(2)}) copy-start(bf16[2,144,256]{2,1,0:T(8,128)(2,1)} %constant.37.clone.table) | copy-start | bytes 442372
  18.8 12.4 %copy-start = (bf16[2,512,512]{2,1,0:T(8,128)(2,1)S(1)}, bf16[2,512,512]{2,1,0:T(8,128)(2,1)}, u32[]{:S(2)}) copy-start(bf16[2,512,512]{2,1,0:T(8,128)(2,1)} %constant.38.clone.slab_table) | copy-start | bytes 3145732
  19.4 11.7 %copy-start.1 = (bf16[2,256,256]{2,1,0:T(8,128)(2,1)S(1)}, bf16[2,256,256]{2,1,0:T(8,128)(2,1)}, u32[]{:S(2)}) copy-start(bf16[2,256,256]{2,1,0:T(8,128)(2,1)} %constant.39.clone.row_table) | copy-start | bytes 786436
  50.5 1.2 %collective-permute-start.3 = (f32[1,128]{1,0:T(1,128)S(1)}, f32[1,128]{1,0:T(1,128)S(1)}, u32[]{:S(2)}, u32[]{:S(2)}) collective-permute-start(f32[1,128]{1,0:T(1,128)S(1)} %bitcast.10), channel_id=1, source_target_pairs={{0,1},{1,0},{2,3},{3,2},{4,5},{5,4},{6,7},{7,6},{8,9},{9,8},{10,11... | collective-permute-start | bytes 1544 | tf_op jit(solution)/shard_map/ppermute | solution.py:730
  52.5 11.4 %copy-start.2 = (bf16[2,256,128]{2,1,0:T(8,128)(2,1)S(1)}, bf16[2,256,128]{2,1,0:T(8,128)(2,1)}, u32[]{:S(2)}) copy-start(bf16[2,256,128]{2,1,0:T(8,128)(2,1)} %constant.40.clone.table) | copy-start | bytes 393220
  63.8 1.4 %collective-permute-start.4 = (f32[8,48,128]{2,1,0:T(8,128)S(1)}, f32[8,48,128]{2,1,0:T(8,128)S(1)}, u32[]{:S(2)}, u32[]{:S(2)}) collective-permute-start(f32[8,48,128]{2,1,0:T(8,128)S(1)} %all_to_all.23.got), channel_id=1, source_target_pairs={{0,1},{1,0},{2,3},{3,2},{4,5},{5,4},{6,7},{7,6},{8,9},{9,8},{10,11... | collective-permute-start | bytes 589832 | tf_op jit(solution)/shard_map/ppermute | solution.py:737
  66.0 9.4 %collective-permute-start.5 = (f32[8,16,128]{2,1,0:T(8,128)S(1)}, f32[8,16,128]{2,1,0:T(8,128)S(1)}, u32[]{:S(2)}, u32[]{:S(2)}) collective-permute-start(f32[8,16,128]{2,1,0:T(8,128)S(1)} %get-tuple-element.35), channel_id=1, source_target_pairs={{0,4},{8,12},{4,0},{12,8},{1,5},{9,13},{5,1},{13,9},{2,6},{10,14},... | collective-permute-start | bytes 196616 | tf_op jit(solution)/shard_map/ppermute | solution.py:757
  66.5 8.9 %collective-permute-start.6 = (f32[8,16,128]{2,1,0:T(8,128)S(1)}, f32[8,16,128]{2,1,0:T(8,128)S(1)}, u32[]{:S(2)}, u32[]{:S(2)}) collective-permute-start(f32[8,16,128]{2,1,0:T(8,128)S(1)} %get-tuple-element.36), channel_id=1, source_target_pairs={{4,8},{8,4},{5,9},{9,5},{6,10},{10,6},{7,11},{11,7},{20,24},{24,20... | collective-permute-start | bytes 196616 | tf_op jit(solution)/shard_map/ppermute | solution.py:758
  71.4 4.1 %collective-permute-start.8 = (f32[128,128]{1,0:T(8,128)S(1)}, f32[128,128]{1,0:T(8,128)S(1)}, u32[]{:S(2)}, u32[]{:S(2)}) collective-permute-start(f32[128,128]{1,0:T(8,128)S(1)} %get-tuple-element.38), channel_id=1, source_target_pairs={{0,1},{1,0},{2,3},{3,2},{4,5},{5,4},{6,7},{7,6},{8,9},{9,8},{10,11... | collective-permute-start | bytes 196616 | tf_op jit(solution)/shard_map/ppermute | solution.py:760
  71.4 4.0 %collective-permute-start.7 = (f32[8,8,128]{2,1,0:T(8,128)S(1)}, f32[8,8,128]{2,1,0:T(8,128)S(1)}, u32[]{:S(2)}, u32[]{:S(2)}) collective-permute-start(f32[8,8,128]{2,1,0:T(8,128)S(1)} %get-tuple-element.37), channel_id=1, source_target_pairs={{0,2},{2,0},{1,3},{3,1},{4,6},{6,4},{5,7},{7,5},{8,10},{10,8},{9,1... | collective-permute-start | bytes 98312 | tf_op jit(solution)/shard_map/ppermute | solution.py:759

commit v7 on v6

--- a/solution.py
+++ b/solution.py
@@ -534,7 +534,7 @@
     lane = lax.broadcasted_iota(jnp.int32, (1, LANES), 1)
     even = place[0, 0:1, :] == 0
     shiftback = jnp.where(place[2, 0:1, :] == 0, 1, 0)
-    marks = [(lane + shiftback) % LANES == k for k in range(K)]
+    marks = [(lane + shiftback) % LANES == k for k in range(K - 1)]
     for s in range(slabs):
         low, high = s * rows, (s + 1) * rows
         corrected = [own[m, low:high, :] - bias[m, low:high, :] for m in range(M)]
@@ -545,17 +545,19 @@
                 logits[k] = logits[k] + near[k, low:high, :]
         inside = (own[M, low:high, :] < float(K)).astype(jnp.float32)
         column = jnp.zeros((rows, LANES), jnp.float32)
-        for k, value in enumerate(soft(logits, inside)):
+        shares = soft(logits, inside)
+        for k in range(K - 1):
+            value = shares[k] - shares[K - 1]
             belief[k, low:high, :] = value
             column = jnp.where(marks[k], pltpu.roll(value, k, 1), column)
         edge[low:high, :] = column
-    for k in range(K):
+    for k in range(K - 1):
         first = belief[k, :rows, :]
         final = belief[k, LANES - rows :, :]
         up[k] = jnp.where(even, final, first)
         down[k] = jnp.where(even, first, final)
     lead = place[1, 0:1, :] == 0
-    for k in range(K):
+    for k in range(K - 1):
         head = belief[k, pl.ds(0, slabs, rows), :]
         tail = belief[k, pl.ds(rows - 1, slabs, rows), :]
         side[k] = jnp.where(lead, tail, head)
@@ -566,7 +568,7 @@
     copy.start()
     lane = lax.broadcasted_iota(jnp.int32, (1, LANES), 1)
     line = lax.broadcasted_iota(jnp.int32, (rows, 1), 0)
-    for k in range(K):
+    for k in range(K - 1):
         for low in range(0, LANES, rows):
             here = belief[k, low : low + rows, :]
             total = dens[k, low : low + rows, :]
@@ -582,12 +584,14 @@
     copy.wait()
 
 
-def last_kernel(rows, inner, own, up, down, side, edge, place, post_h, post, sems):
+def last_kernel(rows, inner, dens, own, up, down, side, edge, place, post_h, post, sems):
     slabs = LANES // rows
     lane = lax.broadcasted_iota(jnp.int32, (1, LANES), 1)
     line = lax.broadcasted_iota(jnp.int32, (rows, 1), 0)
     even = place[0, 0:1, :] == 0
     left = place[2, 0:1, :] == 0
+    bottom = place[3, 0:1, :] == 0
+    top = place[4, 0:1, :] == 0
     spot = lane == jnp.where(left, LANES - 1, 0)
     face = line == jnp.where(place[1, 0:1, :] == 0, rows - 1, 0)
     copies = []
@@ -596,15 +600,16 @@
         column = edge[low:high, :]
         column = jnp.where(left, column, pltpu.roll(column, 2, 1))
         logits = []
-        for k in range(K):
+        for k in range(K - 1):
             total = inner[k, low:high, :]
             if s == 0:
-                total = total + jnp.where(even, down[k], up[k])
+                total = total + jnp.where(bottom, 0.0, jnp.where(even, down[k], up[k]))
             if s == slabs - 1:
-                total = total + jnp.where(even, up[k], down[k])
+                total = total + jnp.where(top, 0.0, jnp.where(even, up[k], down[k]))
             total = total + jnp.where(face, side[k, s : s + 1, :], 0.0)
             total = total + jnp.where(spot, pltpu.roll(column, LANES - 1 - k, 1), 0.0)
             logits.append(total)
+        logits.append(dens[K - 1, low:high, :])
         inside = (own[M, low:high, :] < float(K)).astype(jnp.float32)
         for k, value in enumerate(soft(logits, inside)):
             post[k, low:high, :] = value.astype(jnp.bfloat16)
@@ -652,6 +657,16 @@
     return run
 
 
+def both_ways(pairs, count):
+    steps = []
+    for i in range(count):
+        other = [b if a == i else a for a, b in pairs if i in (a, b)]
+        for side in range(2):
+            target = other[0] * 2 + side if other else i * 2 + 1 - side
+            steps.append((i * 2 + side, target))
+    return steps
+
+
 def pencils(image, brain_mask, labels):
     _, slabs, rows, columns = image.shape
     ns, nr, nc = (lax.axis_size(a) for a in ("slab", "row", "col"))
@@ -662,8 +677,9 @@
     wide_rows = core + 4
     pack = Pack(core, wide_rows, M * wide_rows, M * wide_rows + core + 2)
     f32 = jnp.float32
-    place = jnp.stack([lax.axis_index("slab") % 2, lax.axis_index("row"), lax.axis_index("col")])
-    place = jnp.broadcast_to(place.astype(jnp.int32)[:, None, None], (3, SUB, LANES))
+    slab = lax.axis_index("slab")
+    place = [slab % 2, lax.axis_index("row"), lax.axis_index("col"), slab, ns - 1 - slab]
+    place = jnp.broadcast_to(jnp.stack(place).astype(jnp.int32)[:, None, None], (5, SUB, LANES))
     swap = [(0, 1), (1, 0)]
 
     taps = impulse(columns * nc)
@@ -744,23 +760,23 @@
             ((M, LANES, columns), f32),
             ((K, M), f32),
             ((K, LANES, columns), f32),
-            ((K, LANES, columns), f32),
-            ((K, rows, columns), f32),
-            ((K, rows, columns), f32),
-            ((K, slabs, columns), f32),
+            ((K - 1, LANES, columns), f32),
+            ((K - 1, rows, columns), f32),
+            ((K - 1, rows, columns), f32),
+            ((K - 1, slabs, columns), f32),
             ((LANES, LANES), f32),
         ],
         micros=2,
     )(field, yours, near, own, stat_a, stat_b, gather, place)
     pairs = [(i, i + 1) for i in range(0, ns - 1, 2)]
     between = [(i, i + 1) for i in range(1, ns - 1, 2)]
-    up = lax.ppermute(up, "slab", pairs + [(b, a) for a, b in pairs])
-    down = lax.ppermute(down, "slab", between + [(b, a) for a, b in between])
+    up = lax.ppermute(up, ("slab", "col"), both_ways(pairs, ns))
+    down = lax.ppermute(down, ("slab", "col"), both_ways(between, ns))
     side = lax.ppermute(side, "row", swap)
     edge = lax.ppermute(edge, "col", swap)
     inner, bias = call(
         functools.partial(inner_kernel, rows),
-        [((K, LANES, columns), f32), ((M, LANES, columns), f32)],
+        [((K - 1, LANES, columns), f32), ((M, LANES, columns), f32)],
         [pltpu.SemaphoreType.DMA((1,))],
         far_out=(1,),
     )(dens, belief, bias)
@@ -772,7 +788,7 @@
             pltpu.SemaphoreType.DMA((slabs,)),
         ],
         far_out=(0,),
-    )(inner, own, up, down, side, edge, place)
+    )(inner, dens, own, up, down, side, edge, place)
     shape = (slabs, rows, columns)
     return post.reshape((K,) + shape), bias.reshape((M,) + shape), centers
 

time: 76.8 us -> 76.3 us (level); the launches traced: 76.5 us -> 75.1 us
  starting transfers between devices: 6.74 us -> 4.84 us
    ppermute x2, starting transfers between devices: 5.34 us -> 3.39 us  [the longest x1 2.98 us: pencils(): down = lax.ppermute(down, ('slab', 'col'), both_ways(between, ns))]
where the time goes in v7:
time: 76.3 us; the launch traced here: 75.1 us
  blocking collectives  55.3 us (72%)
  Pallas kernels  8.3 us (11%)
  starting transfers between devices  4.84 us (6%)
  waiting for transfers between devices  4.1 us (5%)
  other arithmetic  0.92 us (1%)
  local copies, waits for them, and re-layouts  0.83 us (1%)
  between operations  0.77 us (1%)
    all_to_all x4, blocking collectives, trade(): lax.all_to_all(x, ('row', 'slab'), split_axis=0, concat_axis=0, tiled=True)  55.3 us
    pallas_call x9, Pallas kernels, run(): pl.pallas_call(kernel, out_shape=shapes, in_specs=[vmem] * len(args), out...  8.3 us
    ppermute x1, starting transfers between devices, pencils(): down = lax.ppermute(down, ('slab', 'col'), both_ways(between, ns))  2.98 us
    ppermute x1, waiting for transfers between devices, pencils(): side = lax.ppermute(side, 'row', swap)  1.74 us
  transfers between devices with their start and end apart: 9, of which 4 were waited for; matrix products, arithmetic and copies ran while one was open for 2% of the time, Pallas kernels for 2%

profile of v7, /device:TPU:16, one launch (start us, length us, event | category | flops | bytes accessed | tf_op | source)
XLA Modules:
  0.0 75.1 jit_solution(14738908946084581943)
XLA Ops:
  0.6 0.1 collective-permute-start.2
  0.7 0.5 collective-permute-start.1
  1.2 0.1 collective-permute-start
  1.3 0.9 %select_convert_fusion = f32[8,16,128]{2,1,0:T(8,128)S(1)} fusion(s32[8,16,128]{2,1,0:T(8,128)} %param.9, s32[8,16,128]{2,1,0:T(8,128)} %param.8), kind=kLoop, calls=%fused_computation.1 | loop fusion | flops 49152 | bytes 196608 | tf_op jit(solution)/shard_map/convert_element_type | solution.py:697
  2.2 0.1 stack.23
  2.3 0.5 own_kernel.1
  2.8 0.1 collective-permute-done.image_o
  2.9 0.1 broadcast_in_dim.12.place
  2.9 0.5 prepare_kernel.1
  3.4 0.0 copy-start.3
  3.5 15.3 %all_to_all.20.got.raw = f32[8,80,128]{2,1,0:T(8,128)S(1)} all-to-all(f32[8,80,128]{2,1,0:T(8,128)S(1)} %get-tuple-element.25), channel_id=1, replica_groups=mesh['grp'=2,'slab'=4,'row'=2,'col'=2] {'row','slab'}, dimensions={0} | all-to-all | bytes 655360 | tf_op jit(solution)/shard_map/all_to_all | solution.py:704
  18.8 0.6 column_kernel.1
  19.4 0.0 copy-start.1
  19.4 11.8 %all_to_all.21.got = f32[8,64,128]{2,1,0:T(8,128)S(1)} all-to-all(f32[8,64,128]{2,1,0:T(8,128)S(1)} %column_kernel.1), channel_id=1, replica_groups=mesh['grp'=2,'slab'=4,'row'=2,'col'=2] {'row','slab'}, dimensions={0} | all-to-all | bytes 524288 | tf_op jit(solution)/shard_map/all_to_all | solution.py:704
  31.3 3.0 %pencil_kernel.1 = (f32[8,120,128]{2,1,0:T(8,128)S(1)}, f32[8,8,16,128]{3,2,1,0:T(8,128)S(1)}) custom-call(f32[8,64,128]{2,1,0:T(8,128)S(1)} %all_to_all.21.got, f32[8,80,128]{2,1,0:T(8,128)S(1)} %all_to_all.20.got.raw, bf16[2,512,512]{2,1,0:T(8,128)(2,1)S(1)} %copy-done, bf16[2,256,256]{2,1,0:T(8,128)(2,1)S(1)} %copy-done.1), custom_call_target="tpu_custom_call" | custom-call | flops 40000000 | bytes 1048576 | tf_op jit(solution)/shard_map/pencil_kernel/pallas_call | solution.py:642
  34.3 16.8 %all_to_all.22.near = f32[8,120,128]{2,1,0:T(8,128)S(1)} all-to-all(f32[8,120,128]{2,1,0:T(8,128)S(1)} %get-tuple-element.27), channel_id=1, replica_groups=mesh['grp'=2,'slab'=4,'row'=2,'col'=2] {'row','slab'}, dimensions={0} | all-to-all | bytes 983040 | tf_op jit(solution)/shard_map/all_to_all | solution.py:704
  51.1 0.1 collective-permute-start.3
  51.2 1.1 %collective-permute-done.3.stat_b = f32[1,128]{1,0:T(1,128)S(1)} collective-permute-done((f32[1,128]{1,0:T(1,128)S(1)}, f32[1,128]{1,0:T(1,128)S(1)}, u32[]{:S(2)}, u32[]{:S(2)}) %collective-permute-start.3) | collective-permute-done | bytes 544 | tf_op jit(solution)/shard_map/ppermute | solution.py:746
  52.4 0.7 residual_kernel.1
  53.1 0.0 copy-start.2
  53.1 11.3 %all_to_all.23.got = f32[8,48,128]{2,1,0:T(8,128)S(1)} all-to-all(f32[8,48,128]{2,1,0:T(8,128)S(1)} %residual_kernel.1), channel_id=1, replica_groups=mesh['grp'=2,'slab'=4,'row'=2,'col'=2] {'row','slab'}, dimensions={0} | all-to-all | bytes 393216 | tf_op jit(solution)/shard_map/all_to_all | solution.py:704
  64.4 0.3 half_kernel.1
  64.7 1.1 %collective-permute-done.4.got = f32[8,48,128]{2,1,0:T(8,128)S(1)} collective-permute-done((f32[8,48,128]{2,1,0:T(8,128)S(1)}, f32[8,48,128]{2,1,0:T(8,128)S(1)}, u32[]{:S(2)}, u32[]{:S(2)}) %collective-permute-start.4) | collective-permute-done | bytes 196640 | tf_op jit(solution)/shard_map/ppermute | solution.py:753
  65.8 0.7 third_kernel.1
  66.6 0.2 collective-permute-start.8
  66.8 0.4 collective-permute-start.5
  67.2 3.0 %collective-permute-start.6 = (f32[7,16,128]{2,1,0:T(8,128)S(1)}, f32[7,16,128]{2,1,0:T(8,128)S(1)}, u32[]{:S(2)}, u32[]{:S(2)}) collective-permute-start(f32[7,16,128]{2,1,0:T(8,128)S(1)} %get-tuple-element.36), channel_id=1, source_target_pairs={{0,1},{1,0},{4,8},{5,9},{8,4},{9,5},{12,13},{13,12},{2,3},{3,2},{6... | collective-permute-start | bytes 172040 | tf_op jit(solution)/shard_map/ppermute | solution.py:774
  70.2 0.6 collective-permute-start.7
  70.7 0.7 copy.10
  71.4 0.9 %inner_kernel.1 = (f32[7,128,128]{2,1,0:T(8,128)S(1)}, f32[3,128,128]{2,1,0:T(8,128)}) custom-call(f32[8,128,128]{2,1,0:T(8,128)S(1)} %get-tuple-element.31.dens, f32[7,128,128]{2,1,0:T(8,128)S(1)} %get-tuple-element.32.belief, f32[3,128,128]{2,1,0:T(8,128)S(1)} %get-tuple-element.33.bias), custom_call_target="tpu_custom_call" | custom-call | flops 10000000 | bytes 1048576 | tf_op jit(solution)/shard_map/inner_kernel/pallas_call | solution.py:642
  72.3 1.7 %collective-permute-done.7.side = f32[7,8,128]{2,1,0:T(8,128)S(1)} collective-permute-done((f32[7,8,128]{2,1,0:T(8,128)S(1)}, f32[7,8,128]{2,1,0:T(8,128)S(1)}, u32[]{:S(2)}, u32[]{:S(2)}) %collective-permute-start.7) | collective-permute-done | bytes 28704 | tf_op jit(solution)/shard_map/ppermute | solution.py:775
  74.0 1.0 %last_kernel.1 = bf16[8,128,128]{2,1,0:T(8,128)(2,1)} custom-call(f32[7,128,128]{2,1,0:T(8,128)S(1)} %get-tuple-element.34.inner, f32[8,128,128]{2,1,0:T(8,128)S(1)} %get-tuple-element.31.dens, f32[4,128,128]{2,1,0:T(8,128)S(1)} %pad_maximum_fusion.own, f32[7,16,128]{2,1,0:T(8,128)S(1)} %collective-permute-done.5.up, ...), custom_call_target="tpu_custom_call" | custom-call | flops 10000000 | bytes 1048576 | tf_op jit(solution)/shard_map/last_kernel/pallas_call | solution.py:642
  (15 shorter events, 0.1 us)
Async XLA Ops:
  0.6 1.6 %copy-start.4 = (f32[3,8,16,128]{3,2,1,0:T(8,128)S(1)}, f32[3,8,16,128]{3,2,1,0:T(8,128)}, u32[]{:S(2)}) copy-start(f32[3,8,16,128]{3,2,1,0:T(8,128)} %param.7) | copy-start | bytes 589828
  0.6 2.1 %collective-permute-start.2 = (s32[128,128]{1,0:T(8,128)}, s32[128,128]{1,0:T(8,128)S(1)}, u32[]{:S(2)}, u32[]{:S(2)}) collective-permute-start(s32[128,128]{1,0:T(8,128)} %bitcast.19), channel_id=1, source_target_pairs={{0,1},{1,0},{2,3},{3,2},{4,5},{5,4},{6,7},{7,6},{8,9},{9,8},{10,11... | collective-permute-start | bytes 196616 | tf_op jit(solution)/shard_map/ppermute | solution.py:701
  0.7 2.1 %collective-permute-start.1 = (s32[128,128]{1,0:T(8,128)}, s32[128,128]{1,0:T(8,128)S(1)}, u32[]{:S(2)}, u32[]{:S(2)}) collective-permute-start(s32[128,128]{1,0:T(8,128)} %bitcast.20), channel_id=1, source_target_pairs={{0,1},{1,0},{2,3},{3,2},{4,5},{5,4},{6,7},{7,6},{8,9},{9,8},{10,11... | collective-permute-start | bytes 196616 | tf_op jit(solution)/shard_map/ppermute | solution.py:700
  1.2 1.7 %collective-permute-start = (f32[3,128,128]{2,1,0:T(8,128)}, f32[3,128,128]{2,1,0:T(8,128)S(1)}, u32[]{:S(2)}, u32[]{:S(2)}) collective-permute-start(f32[3,128,128]{2,1,0:T(8,128)} %bitcast.17), channel_id=1, source_target_pairs={{0,1},{1,0},{2,3},{3,2},{4,5},{5,4},{6,7},{7,6},{8,9},{9,8},{10,11... | collective-permute-start | bytes 589832 | tf_op jit(solution)/shard_map/ppermute | solution.py:699
  3.4 15.3 %copy-start.3 = (bf16[2,144,256]{2,1,0:T(8,128)(2,1)S(1)}, bf16[2,144,256]{2,1,0:T(8,128)(2,1)}, u32[]{:S(2)}) copy-start(bf16[2,144,256]{2,1,0:T(8,128)(2,1)} %constant.39.clone.table) | copy-start | bytes 442372
  18.8 12.5 %copy-start = (bf16[2,512,512]{2,1,0:T(8,128)(2,1)S(1)}, bf16[2,512,512]{2,1,0:T(8,128)(2,1)}, u32[]{:S(2)}) copy-start(bf16[2,512,512]{2,1,0:T(8,128)(2,1)} %constant.40.clone.slab_table) | copy-start | bytes 3145732
  19.4 11.8 %copy-start.1 = (bf16[2,256,256]{2,1,0:T(8,128)(2,1)S(1)}, bf16[2,256,256]{2,1,0:T(8,128)(2,1)}, u32[]{:S(2)}) copy-start(bf16[2,256,256]{2,1,0:T(8,128)(2,1)} %constant.41.clone.row_table) | copy-start | bytes 786436
  51.1 1.2 %collective-permute-start.3 = (f32[1,128]{1,0:T(1,128)S(1)}, f32[1,128]{1,0:T(1,128)S(1)}, u32[]{:S(2)}, u32[]{:S(2)}) collective-permute-start(f32[1,128]{1,0:T(1,128)S(1)} %bitcast.12), channel_id=1, source_target_pairs={{0,1},{1,0},{2,3},{3,2},{4,5},{5,4},{6,7},{7,6},{8,9},{9,8},{10,11... | collective-permute-start | bytes 1544 | tf_op jit(solution)/shard_map/ppermute | solution.py:746
  53.1 11.3 %copy-start.2 = (bf16[2,256,128]{2,1,0:T(8,128)(2,1)S(1)}, bf16[2,256,128]{2,1,0:T(8,128)(2,1)}, u32[]{:S(2)}) copy-start(bf16[2,256,128]{2,1,0:T(8,128)(2,1)} %constant.42.clone.table) | copy-start | bytes 393220
  64.4 1.4 %collective-permute-start.4 = (f32[8,48,128]{2,1,0:T(8,128)S(1)}, f32[8,48,128]{2,1,0:T(8,128)S(1)}, u32[]{:S(2)}, u32[]{:S(2)}) collective-permute-start(f32[8,48,128]{2,1,0:T(8,128)S(1)} %all_to_all.23.got), channel_id=1, source_target_pairs={{0,1},{1,0},{2,3},{3,2},{4,5},{5,4},{6,7},{7,6},{8,9},{9,8},{10,11... | collective-permute-start | bytes 589832 | tf_op jit(solution)/shard_map/ppermute | solution.py:753
  66.6 7.5 %collective-permute-start.8 = (f32[128,128]{1,0:T(8,128)S(1)}, f32[128,128]{1,0:T(8,128)S(1)}, u32[]{:S(2)}, u32[]{:S(2)}) collective-permute-start(f32[128,128]{1,0:T(8,128)S(1)} %get-tuple-element.38), channel_id=1, source_target_pairs={{0,1},{1,0},{2,3},{3,2},{4,5},{5,4},{6,7},{7,6},{8,9},{9,8},{10,11... | collective-permute-start | bytes 196616 | tf_op jit(solution)/shard_map/ppermute | solution.py:776
  66.8 7.3 %collective-permute-start.5 = (f32[7,16,128]{2,1,0:T(8,128)S(1)}, f32[7,16,128]{2,1,0:T(8,128)S(1)}, u32[]{:S(2)}, u32[]{:S(2)}) collective-permute-start(f32[7,16,128]{2,1,0:T(8,128)S(1)} %get-tuple-element.35), channel_id=1, source_target_pairs={{0,4},{1,5},{4,0},{5,1},{8,12},{9,13},{12,8},{13,9},{2,6},{3,7},{6... | collective-permute-start | bytes 172040 | tf_op jit(solution)/shard_map/ppermute | solution.py:773
  67.2 6.9 %collective-permute-start.6 = (f32[7,16,128]{2,1,0:T(8,128)S(1)}, f32[7,16,128]{2,1,0:T(8,128)S(1)}, u32[]{:S(2)}, u32[]{:S(2)}) collective-permute-start(f32[7,16,128]{2,1,0:T(8,128)S(1)} %get-tuple-element.36), channel_id=1, source_target_pairs={{0,1},{1,0},{4,8},{5,9},{8,4},{9,5},{12,13},{13,12},{2,3},{3,2},{6... | collective-permute-start | bytes 172040 | tf_op jit(solution)/shard_map/ppermute | solution.py:774
  70.2 3.9 %collective-permute-start.7 = (f32[7,8,128]{2,1,0:T(8,128)S(1)}, f32[7,8,128]{2,1,0:T(8,128)S(1)}, u32[]{:S(2)}, u32[]{:S(2)}) collective-permute-start(f32[7,8,128]{2,1,0:T(8,128)S(1)} %get-tuple-element.37), channel_id=1, source_target_pairs={{0,2},{2,0},{1,3},{3,1},{4,6},{6,4},{5,7},{7,5},{8,10},{10,8},{9,1... | collective-permute-start | bytes 86024 | tf_op jit(solution)/shard_map/ppermute | solution.py:775

commit v8 on v7

--- a/solution.py
+++ b/solution.py
@@ -275,11 +275,11 @@
 
 
 def prepare_kernel(
-    pack, turned, stat, image_o, mask_o, labels_o, place, send, rest, code_o, ext
+    pack, turned, stat, image_o, mask_o, labels_o, send, rest, code_o, ext
 ):
     peers = send.shape[0]
     step = LANES // peers
-    first = place[2] == 0
+    first = jnp.full((SUB, LANES), lax.axis_index("col"), jnp.int32) == 0
     code_o[...] = jnp.where(mask_o[...] > 0, labels_o[...], K).astype(jnp.float32)
     row = stat[0:1, :] + stat_row(class_sums(code_o[...], image_o))
     for f in range(M + 1):
@@ -714,7 +714,7 @@
             ((LANES, columns), f32),
         ],
         [(M + 1, columns + 2 * MARGIN, LANES)],
-    )(turned, stat, image_o, mask_o, labels_o, place)
+    )(turned, stat, image_o, mask_o, labels_o)
     raw = trade(sent)
     (sent,) = call(
         functools.partial(column_kernel, pack),

time: 76.3 us -> 75.7 us (level)
  no operation moved by 1% of the time
where the time goes in v8:
time: 75.7 us; the launch traced here: 74.4 us
  blocking collectives  54.7 us (72%)
  Pallas kernels  8.3 us (11%)
  starting transfers between devices  4.84 us (6%)
  waiting for transfers between devices  4.11 us (5%)
  other arithmetic  0.92 us (1%)
  local copies, waits for them, and re-layouts  0.83 us (1%)
  between operations  0.77 us (1%)
    all_to_all x4, blocking collectives, trade(): lax.all_to_all(x, ('row', 'slab'), split_axis=0, concat_axis=0, tiled=True)  54.7 us
    pallas_call x9, Pallas kernels, run(): pl.pallas_call(kernel, out_shape=shapes, in_specs=[vmem] * len(args), out...  8.3 us
    ppermute x1, starting transfers between devices, pencils(): down = lax.ppermute(down, ('slab', 'col'), both_ways(between, ns))  2.98 us
    ppermute x1, waiting for transfers between devices, pencils(): side = lax.ppermute(side, 'row', swap)  1.74 us
  transfers between devices with their start and end apart: 9, of which 4 were waited for; matrix products, arithmetic and copies ran while one was open for 2% of the time, Pallas kernels for 2%

profile of v8, /device:TPU:16, one launch (start us, length us, event | category | flops | bytes accessed | tf_op | source)
XLA Modules:
  0.0 74.4 jit_solution(345960988831488111)
XLA Ops:
  0.6 0.1 collective-permute-start.2
  0.7 0.5 collective-permute-start.1
  1.2 0.1 collective-permute-start
  1.3 0.9 %select_convert_fusion = f32[8,16,128]{2,1,0:T(8,128)S(1)} fusion(s32[8,16,128]{2,1,0:T(8,128)} %param.9, s32[8,16,128]{2,1,0:T(8,128)} %param.8), kind=kLoop, calls=%fused_computation.1 | loop fusion | flops 49152 | bytes 196608 | tf_op jit(solution)/shard_map/convert_element_type | solution.py:697
  2.2 0.5 own_kernel.1
  2.7 0.2 collective-permute-done.image_o
  2.9 0.5 prepare_kernel.1
  3.4 0.0 copy-start.3
  3.4 15.2 %all_to_all.20.got.raw = f32[8,80,128]{2,1,0:T(8,128)S(1)} all-to-all(f32[8,80,128]{2,1,0:T(8,128)S(1)} %get-tuple-element.25), channel_id=1, replica_groups=mesh['grp'=2,'slab'=4,'row'=2,'col'=2] {'row','slab'}, dimensions={0} | all-to-all | bytes 655360 | tf_op jit(solution)/shard_map/all_to_all | solution.py:704
  18.6 0.6 column_kernel.1
  19.3 0.0 copy-start.1
  19.3 11.7 %all_to_all.21.got = f32[8,64,128]{2,1,0:T(8,128)S(1)} all-to-all(f32[8,64,128]{2,1,0:T(8,128)S(1)} %column_kernel.1), channel_id=1, replica_groups=mesh['grp'=2,'slab'=4,'row'=2,'col'=2] {'row','slab'}, dimensions={0} | all-to-all | bytes 524288 | tf_op jit(solution)/shard_map/all_to_all | solution.py:704
  31.0 3.0 %pencil_kernel.1 = (f32[8,120,128]{2,1,0:T(8,128)S(1)}, f32[8,8,16,128]{3,2,1,0:T(8,128)S(1)}) custom-call(f32[8,64,128]{2,1,0:T(8,128)S(1)} %all_to_all.21.got, f32[8,80,128]{2,1,0:T(8,128)S(1)} %all_to_all.20.got.raw, bf16[2,512,512]{2,1,0:T(8,128)(2,1)S(1)} %copy-done, bf16[2,256,256]{2,1,0:T(8,128)(2,1)S(1)} %copy-done.1), custom_call_target="tpu_custom_call" | custom-call | flops 40000000 | bytes 1048576 | tf_op jit(solution)/shard_map/pencil_kernel/pallas_call | solution.py:642
  34.0 16.4 %all_to_all.22.near = f32[8,120,128]{2,1,0:T(8,128)S(1)} all-to-all(f32[8,120,128]{2,1,0:T(8,128)S(1)} %get-tuple-element.27), channel_id=1, replica_groups=mesh['grp'=2,'slab'=4,'row'=2,'col'=2] {'row','slab'}, dimensions={0} | all-to-all | bytes 983040 | tf_op jit(solution)/shard_map/all_to_all | solution.py:704
  50.4 0.1 collective-permute-start.3
  50.5 1.1 %collective-permute-done.3.stat_b = f32[1,128]{1,0:T(1,128)S(1)} collective-permute-done((f32[1,128]{1,0:T(1,128)S(1)}, f32[1,128]{1,0:T(1,128)S(1)}, u32[]{:S(2)}, u32[]{:S(2)}) %collective-permute-start.3) | collective-permute-done | bytes 544 | tf_op jit(solution)/shard_map/ppermute | solution.py:746
  51.6 0.7 residual_kernel.1
  52.3 0.0 copy-start.2
  52.3 11.4 %all_to_all.23.got = f32[8,48,128]{2,1,0:T(8,128)S(1)} all-to-all(f32[8,48,128]{2,1,0:T(8,128)S(1)} %residual_kernel.1), channel_id=1, replica_groups=mesh['grp'=2,'slab'=4,'row'=2,'col'=2] {'row','slab'}, dimensions={0} | all-to-all | bytes 393216 | tf_op jit(solution)/shard_map/all_to_all | solution.py:704
  63.7 0.1 stack.23
  63.8 0.3 half_kernel.1
  64.1 1.1 %collective-permute-done.4.got = f32[8,48,128]{2,1,0:T(8,128)S(1)} collective-permute-done((f32[8,48,128]{2,1,0:T(8,128)S(1)}, f32[8,48,128]{2,1,0:T(8,128)S(1)}, u32[]{:S(2)}, u32[]{:S(2)}) %collective-permute-start.4) | collective-permute-done | bytes 196640 | tf_op jit(solution)/shard_map/ppermute | solution.py:753
  65.1 0.1 broadcast_in_dim.12.place
  65.2 0.7 third_kernel.1
  65.9 0.2 collective-permute-start.8
  66.1 0.4 collective-permute-start.5
  66.5 3.0 %collective-permute-start.6 = (f32[7,16,128]{2,1,0:T(8,128)S(1)}, f32[7,16,128]{2,1,0:T(8,128)S(1)}, u32[]{:S(2)}, u32[]{:S(2)}) collective-permute-start(f32[7,16,128]{2,1,0:T(8,128)S(1)} %get-tuple-element.36), channel_id=1, source_target_pairs={{0,1},{1,0},{4,8},{5,9},{8,4},{9,5},{12,13},{13,12},{2,3},{3,2},{6... | collective-permute-start | bytes 172040 | tf_op jit(solution)/shard_map/ppermute | solution.py:774
  69.5 0.5 collective-permute-start.7
  70.1 0.7 copy.10
  70.7 0.9 %inner_kernel.1 = (f32[7,128,128]{2,1,0:T(8,128)S(1)}, f32[3,128,128]{2,1,0:T(8,128)}) custom-call(f32[8,128,128]{2,1,0:T(8,128)S(1)} %get-tuple-element.31.dens, f32[7,128,128]{2,1,0:T(8,128)S(1)} %get-tuple-element.32.belief, f32[3,128,128]{2,1,0:T(8,128)S(1)} %get-tuple-element.33.bias), custom_call_target="tpu_custom_call" | custom-call | flops 10000000 | bytes 1048576 | tf_op jit(solution)/shard_map/inner_kernel/pallas_call | solution.py:642
  71.7 1.7 %collective-permute-done.7.side = f32[7,8,128]{2,1,0:T(8,128)S(1)} collective-permute-done((f32[7,8,128]{2,1,0:T(8,128)S(1)}, f32[7,8,128]{2,1,0:T(8,128)S(1)}, u32[]{:S(2)}, u32[]{:S(2)}) %collective-permute-start.7) | collective-permute-done | bytes 28704 | tf_op jit(solution)/shard_map/ppermute | solution.py:775
  73.4 1.0 %last_kernel.1 = bf16[8,128,128]{2,1,0:T(8,128)(2,1)} custom-call(f32[7,128,128]{2,1,0:T(8,128)S(1)} %get-tuple-element.34.inner, f32[8,128,128]{2,1,0:T(8,128)S(1)} %get-tuple-element.31.dens, f32[4,128,128]{2,1,0:T(8,128)S(1)} %pad_maximum_fusion.own, f32[7,16,128]{2,1,0:T(8,128)S(1)} %collective-permute-done.5.up, ...), custom_call_target="tpu_custom_call" | custom-call | flops 10000000 | bytes 1048576 | tf_op jit(solution)/shard_map/last_kernel/pallas_call | solution.py:642
  (15 shorter events, 0.1 us)
Async XLA Ops:
  0.6 1.6 %copy-start.4 = (f32[3,8,16,128]{3,2,1,0:T(8,128)S(1)}, f32[3,8,16,128]{3,2,1,0:T(8,128)}, u32[]{:S(2)}) copy-start(f32[3,8,16,128]{3,2,1,0:T(8,128)} %param.7) | copy-start | bytes 589828
  0.6 2.1 %collective-permute-start.2 = (s32[128,128]{1,0:T(8,128)}, s32[128,128]{1,0:T(8,128)S(1)}, u32[]{:S(2)}, u32[]{:S(2)}) collective-permute-start(s32[128,128]{1,0:T(8,128)} %bitcast.19), channel_id=1, source_target_pairs={{0,1},{1,0},{2,3},{3,2},{4,5},{5,4},{6,7},{7,6},{8,9},{9,8},{10,11... | collective-permute-start | bytes 196616 | tf_op jit(solution)/shard_map/ppermute | solution.py:701
  0.7 2.0 %collective-permute-start.1 = (s32[128,128]{1,0:T(8,128)}, s32[128,128]{1,0:T(8,128)S(1)}, u32[]{:S(2)}, u32[]{:S(2)}) collective-permute-start(s32[128,128]{1,0:T(8,128)} %bitcast.20), channel_id=1, source_target_pairs={{0,1},{1,0},{2,3},{3,2},{4,5},{5,4},{6,7},{7,6},{8,9},{9,8},{10,11... | collective-permute-start | bytes 196616 | tf_op jit(solution)/shard_map/ppermute | solution.py:700
  1.2 1.7 %collective-permute-start = (f32[3,128,128]{2,1,0:T(8,128)}, f32[3,128,128]{2,1,0:T(8,128)S(1)}, u32[]{:S(2)}, u32[]{:S(2)}) collective-permute-start(f32[3,128,128]{2,1,0:T(8,128)} %bitcast.17), channel_id=1, source_target_pairs={{0,1},{1,0},{2,3},{3,2},{4,5},{5,4},{6,7},{7,6},{8,9},{9,8},{10,11... | collective-permute-start | bytes 589832 | tf_op jit(solution)/shard_map/ppermute | solution.py:699
  3.4 15.3 %copy-start.3 = (bf16[2,144,256]{2,1,0:T(8,128)(2,1)S(1)}, bf16[2,144,256]{2,1,0:T(8,128)(2,1)}, u32[]{:S(2)}) copy-start(bf16[2,144,256]{2,1,0:T(8,128)(2,1)} %constant.39.clone.table) | copy-start | bytes 442372
  18.6 12.4 %copy-start = (bf16[2,512,512]{2,1,0:T(8,128)(2,1)S(1)}, bf16[2,512,512]{2,1,0:T(8,128)(2,1)}, u32[]{:S(2)}) copy-start(bf16[2,512,512]{2,1,0:T(8,128)(2,1)} %constant.40.clone.slab_table) | copy-start | bytes 3145732
  19.3 11.7 %copy-start.1 = (bf16[2,256,256]{2,1,0:T(8,128)(2,1)S(1)}, bf16[2,256,256]{2,1,0:T(8,128)(2,1)}, u32[]{:S(2)}) copy-start(bf16[2,256,256]{2,1,0:T(8,128)(2,1)} %constant.41.clone.row_table) | copy-start | bytes 786436
  50.4 1.2 %collective-permute-start.3 = (f32[1,128]{1,0:T(1,128)S(1)}, f32[1,128]{1,0:T(1,128)S(1)}, u32[]{:S(2)}, u32[]{:S(2)}) collective-permute-start(f32[1,128]{1,0:T(1,128)S(1)} %bitcast.12), channel_id=1, source_target_pairs={{0,1},{1,0},{2,3},{3,2},{4,5},{5,4},{6,7},{7,6},{8,9},{9,8},{10,11... | collective-permute-start | bytes 1544 | tf_op jit(solution)/shard_map/ppermute | solution.py:746
  52.3 11.5 %copy-start.2 = (bf16[2,256,128]{2,1,0:T(8,128)(2,1)S(1)}, bf16[2,256,128]{2,1,0:T(8,128)(2,1)}, u32[]{:S(2)}) copy-start(bf16[2,256,128]{2,1,0:T(8,128)(2,1)} %constant.42.clone.table) | copy-start | bytes 393220
  63.7 1.4 %collective-permute-start.4 = (f32[8,48,128]{2,1,0:T(8,128)S(1)}, f32[8,48,128]{2,1,0:T(8,128)S(1)}, u32[]{:S(2)}, u32[]{:S(2)}) collective-permute-start(f32[8,48,128]{2,1,0:T(8,128)S(1)} %all_to_all.23.got), channel_id=1, source_target_pairs={{0,1},{1,0},{2,3},{3,2},{4,5},{5,4},{6,7},{7,6},{8,9},{9,8},{10,11... | collective-permute-start | bytes 589832 | tf_op jit(solution)/shard_map/ppermute | solution.py:753
  65.9 7.5 %collective-permute-start.8 = (f32[128,128]{1,0:T(8,128)S(1)}, f32[128,128]{1,0:T(8,128)S(1)}, u32[]{:S(2)}, u32[]{:S(2)}) collective-permute-start(f32[128,128]{1,0:T(8,128)S(1)} %get-tuple-element.38), channel_id=1, source_target_pairs={{0,1},{1,0},{2,3},{3,2},{4,5},{5,4},{6,7},{7,6},{8,9},{9,8},{10,11... | collective-permute-start | bytes 196616 | tf_op jit(solution)/shard_map/ppermute | solution.py:776
  66.1 7.3 %collective-permute-start.5 = (f32[7,16,128]{2,1,0:T(8,128)S(1)}, f32[7,16,128]{2,1,0:T(8,128)S(1)}, u32[]{:S(2)}, u32[]{:S(2)}) collective-permute-start(f32[7,16,128]{2,1,0:T(8,128)S(1)} %get-tuple-element.35), channel_id=1, source_target_pairs={{0,4},{1,5},{4,0},{5,1},{8,12},{9,13},{12,8},{13,9},{2,6},{3,7},{6... | collective-permute-start | bytes 172040 | tf_op jit(solution)/shard_map/ppermute | solution.py:773
  66.5 6.9 %collective-permute-start.6 = (f32[7,16,128]{2,1,0:T(8,128)S(1)}, f32[7,16,128]{2,1,0:T(8,128)S(1)}, u32[]{:S(2)}, u32[]{:S(2)}) collective-permute-start(f32[7,16,128]{2,1,0:T(8,128)S(1)} %get-tuple-element.36), channel_id=1, source_target_pairs={{0,1},{1,0},{4,8},{5,9},{8,4},{9,5},{12,13},{13,12},{2,3},{3,2},{6... | collective-permute-start | bytes 172040 | tf_op jit(solution)/shard_map/ppermute | solution.py:774
  69.5 3.9 %collective-permute-start.7 = (f32[7,8,128]{2,1,0:T(8,128)S(1)}, f32[7,8,128]{2,1,0:T(8,128)S(1)}, u32[]{:S(2)}, u32[]{:S(2)}) collective-permute-start(f32[7,8,128]{2,1,0:T(8,128)S(1)} %get-tuple-element.37), channel_id=1, source_target_pairs={{0,2},{2,0},{1,3},{3,1},{4,6},{6,4},{5,7},{7,5},{8,10},{10,8},{9,1... | collective-permute-start | bytes 86024 | tf_op jit(solution)/shard_map/ppermute | solution.py:775

commit v9 on v8

--- a/solution.py
+++ b/solution.py
@@ -513,7 +513,6 @@
     stat_a,
     stat_b,
     table,
-    place,
     bias,
     centers,
     dens,
@@ -532,8 +531,8 @@
             columns_of(got, m, core), (table[0, LANES:, :], table[1, LANES:, :])
         )
     lane = lax.broadcasted_iota(jnp.int32, (1, LANES), 1)
-    even = place[0, 0:1, :] == 0
-    shiftback = jnp.where(place[2, 0:1, :] == 0, 1, 0)
+    even = lanes_of(lax.rem(lax.axis_index("slab"), 2)) == 0
+    shiftback = jnp.where(lanes_of(lax.axis_index("col")) == 0, 1, 0)
     marks = [(lane + shiftback) % LANES == k for k in range(K - 1)]
     for s in range(slabs):
         low, high = s * rows, (s + 1) * rows
@@ -556,7 +555,7 @@
         final = belief[k, LANES - rows :, :]
         up[k] = jnp.where(even, final, first)
         down[k] = jnp.where(even, first, final)
-    lead = place[1, 0:1, :] == 0
+    lead = lanes_of(lax.axis_index("row")) == 0
     for k in range(K - 1):
         head = belief[k, pl.ds(0, slabs, rows), :]
         tail = belief[k, pl.ds(rows - 1, slabs, rows), :]
@@ -584,16 +583,16 @@
     copy.wait()
 
 
-def last_kernel(rows, inner, dens, own, up, down, side, edge, place, post_h, post, sems):
+def last_kernel(rows, inner, dens, own, up, down, side, edge, post_h, post, sems):
     slabs = LANES // rows
     lane = lax.broadcasted_iota(jnp.int32, (1, LANES), 1)
     line = lax.broadcasted_iota(jnp.int32, (rows, 1), 0)
-    even = place[0, 0:1, :] == 0
-    left = place[2, 0:1, :] == 0
-    bottom = place[3, 0:1, :] == 0
-    top = place[4, 0:1, :] == 0
+    even = lanes_of(lax.rem(lax.axis_index("slab"), 2)) == 0
+    left = lanes_of(lax.axis_index("col")) == 0
+    bottom = lanes_of(lax.axis_index("slab")) == 0
+    top = lanes_of(lax.axis_size("slab") - 1 - lax.axis_index("slab")) == 0
     spot = lane == jnp.where(left, LANES - 1, 0)
-    face = line == jnp.where(place[1, 0:1, :] == 0, rows - 1, 0)
+    face = line == jnp.where(lanes_of(lax.axis_index("row")) == 0, rows - 1, 0)
     copies = []
     for s in range(slabs):
         low, high = s * rows, (s + 1) * rows
@@ -622,6 +621,10 @@
         copy.wait()
 
 
+def lanes_of(value):
+    return jnp.full((1, LANES), value, jnp.int32)
+
+
 class Pack(typing.NamedTuple):
     core: int
     wide: int
@@ -677,9 +680,6 @@
     wide_rows = core + 4
     pack = Pack(core, wide_rows, M * wide_rows, M * wide_rows + core + 2)
     f32 = jnp.float32
-    slab = lax.axis_index("slab")
-    place = [slab % 2, lax.axis_index("row"), lax.axis_index("col"), slab, ns - 1 - slab]
-    place = jnp.broadcast_to(jnp.stack(place).astype(jnp.int32)[:, None, None], (5, SUB, LANES))
     swap = [(0, 1), (1, 0)]
 
     taps = impulse(columns * nc)
@@ -767,7 +767,7 @@
             ((LANES, LANES), f32),
         ],
         micros=2,
-    )(field, yours, near, own, stat_a, stat_b, gather, place)
+    )(field, yours, near, own, stat_a, stat_b, gather)
     pairs = [(i, i + 1) for i in range(0, ns - 1, 2)]
     between = [(i, i + 1) for i in range(1, ns - 1, 2)]
     up = lax.ppermute(up, ("slab", "col"), both_ways(pairs, ns))
@@ -788,7 +788,7 @@
             pltpu.SemaphoreType.DMA((slabs,)),
         ],
         far_out=(0,),
-    )(inner, dens, own, up, down, side, edge, place)
+    )(inner, dens, own, up, down, side, edge)
     shape = (slabs, rows, columns)
     return post.reshape((K,) + shape), bias.reshape((M,) + shape), centers
 

time: 75.7 us -> 75.7 us (level)
  no operation moved by 1% of the time
where the time goes in v9:
time: 75.7 us; the launch traced here: 74.4 us
  blocking collectives  54.7 us (72%)
  Pallas kernels  8.31 us (11%)
  starting transfers between devices  4.84 us (6%)
  waiting for transfers between devices  4.19 us (6%)
  other arithmetic  0.92 us (1%)
  between operations  0.77 us (1%)
    all_to_all x4, blocking collectives, trade(): lax.all_to_all(x, ('row', 'slab'), split_axis=0, concat_axis=0, tiled=True)  54.7 us
    pallas_call x9, Pallas kernels, run(): pl.pallas_call(kernel, out_shape=shapes, in_specs=[vmem] * len(args), out...  8.31 us
    ppermute x1, starting transfers between devices, pencils(): down = lax.ppermute(down, ('slab', 'col'), both_ways(between, ns))  2.98 us
    ppermute x1, waiting for transfers between devices, pencils(): side = lax.ppermute(side, 'row', swap)  1.74 us
  transfers between devices with their start and end apart: 9, of which 4 were waited for; matrix products, arithmetic and copies ran while one was open for 2% of the time, Pallas kernels for 2%

profile of v9, /device:TPU:16, one launch (start us, length us, event | category | flops | bytes accessed | tf_op | source)
XLA Modules:
  0.0 74.4 jit_solution(13977262388930738731)
XLA Ops:
  0.6 0.1 collective-permute-start.2
  0.7 0.5 collective-permute-start.1
  1.2 0.1 collective-permute-start
  1.3 0.9 %select_convert_fusion = f32[8,16,128]{2,1,0:T(8,128)S(1)} fusion(s32[8,16,128]{2,1,0:T(8,128)} %param.9, s32[8,16,128]{2,1,0:T(8,128)} %param.8), kind=kLoop, calls=%fused_computation.1 | loop fusion | flops 49152 | bytes 196608 | tf_op jit(solution)/shard_map/convert_element_type | solution.py:697
  2.2 0.5 own_kernel.1
  2.7 0.0 collective-permute-done.2.labels_o
  2.7 0.2 collective-permute-done.image_o
  2.9 0.5 prepare_kernel.1
  3.4 0.0 copy-start.3
  3.4 15.2 %all_to_all.20.got.raw = f32[8,80,128]{2,1,0:T(8,128)S(1)} all-to-all(f32[8,80,128]{2,1,0:T(8,128)S(1)} %get-tuple-element.25), channel_id=1, replica_groups=mesh['grp'=2,'slab'=4,'row'=2,'col'=2] {'row','slab'}, dimensions={0} | all-to-all | bytes 655360 | tf_op jit(solution)/shard_map/all_to_all | solution.py:704
  18.6 0.6 column_kernel.1
  19.3 0.0 copy-start.1
  19.3 11.7 %all_to_all.21.got = f32[8,64,128]{2,1,0:T(8,128)S(1)} all-to-all(f32[8,64,128]{2,1,0:T(8,128)S(1)} %column_kernel.1), channel_id=1, replica_groups=mesh['grp'=2,'slab'=4,'row'=2,'col'=2] {'row','slab'}, dimensions={0} | all-to-all | bytes 524288 | tf_op jit(solution)/shard_map/all_to_all | solution.py:704
  31.0 3.0 %pencil_kernel.1 = (f32[8,120,128]{2,1,0:T(8,128)S(1)}, f32[8,8,16,128]{3,2,1,0:T(8,128)S(1)}) custom-call(f32[8,64,128]{2,1,0:T(8,128)S(1)} %all_to_all.21.got, f32[8,80,128]{2,1,0:T(8,128)S(1)} %all_to_all.20.got.raw, bf16[2,512,512]{2,1,0:T(8,128)(2,1)S(1)} %copy-done, bf16[2,256,256]{2,1,0:T(8,128)(2,1)S(1)} %copy-done.1), custom_call_target="tpu_custom_call" | custom-call | flops 40000000 | bytes 1048576 | tf_op jit(solution)/shard_map/pencil_kernel/pallas_call | solution.py:645
  34.0 16.4 %all_to_all.22.near = f32[8,120,128]{2,1,0:T(8,128)S(1)} all-to-all(f32[8,120,128]{2,1,0:T(8,128)S(1)} %get-tuple-element.27), channel_id=1, replica_groups=mesh['grp'=2,'slab'=4,'row'=2,'col'=2] {'row','slab'}, dimensions={0} | all-to-all | bytes 983040 | tf_op jit(solution)/shard_map/all_to_all | solution.py:704
  50.4 0.1 collective-permute-start.3
  50.5 1.1 %collective-permute-done.3.stat_b = f32[1,128]{1,0:T(1,128)S(1)} collective-permute-done((f32[1,128]{1,0:T(1,128)S(1)}, f32[1,128]{1,0:T(1,128)S(1)}, u32[]{:S(2)}, u32[]{:S(2)}) %collective-permute-start.3) | collective-permute-done | bytes 544 | tf_op jit(solution)/shard_map/ppermute | solution.py:746
  51.6 0.7 residual_kernel.1
  52.3 0.0 copy-start.2
  52.3 11.4 %all_to_all.23.got = f32[8,48,128]{2,1,0:T(8,128)S(1)} all-to-all(f32[8,48,128]{2,1,0:T(8,128)S(1)} %residual_kernel.1), channel_id=1, replica_groups=mesh['grp'=2,'slab'=4,'row'=2,'col'=2] {'row','slab'}, dimensions={0} | all-to-all | bytes 393216 | tf_op jit(solution)/shard_map/all_to_all | solution.py:704
  63.7 0.0 collective-permute-start.4
  63.7 0.3 half_kernel.1
  64.0 1.1 %collective-permute-done.4.got = f32[8,48,128]{2,1,0:T(8,128)S(1)} collective-permute-done((f32[8,48,128]{2,1,0:T(8,128)S(1)}, f32[8,48,128]{2,1,0:T(8,128)S(1)}, u32[]{:S(2)}, u32[]{:S(2)}) %collective-permute-start.4) | collective-permute-done | bytes 196640 | tf_op jit(solution)/shard_map/ppermute | solution.py:753
  65.1 0.7 %third_kernel.1 = (f32[3,128,128]{2,1,0:T(8,128)S(1)}, f32[8,3]{1,0:T(8,128)S(1)}, f32[8,128,128]{2,1,0:T(8,128)S(1)}, f32[7,128,128]{2,1,0:T(8,128)S(1)}, f32[7...) custom-call(f32[3,128,128]{2,1,0:T(8,128)S(1)} %get-tuple-element.29.field,, ...), custom_call_target="tpu_custom_call" | custom-call | flops 20000000 | bytes 1048576 | tf_op jit(solution)/shard_map/third_kernel/pallas_call | solution.py:645
  65.9 0.2 collective-permute-start.8
  66.1 0.4 collective-permute-start.5
  66.5 3.0 %collective-permute-start.6 = (f32[7,16,128]{2,1,0:T(8,128)S(1)}, f32[7,16,128]{2,1,0:T(8,128)S(1)}, u32[]{:S(2)}, u32[]{:S(2)}) collective-permute-start(f32[7,16,128]{2,1,0:T(8,128)S(1)} %get-tuple-element.36), channel_id=1, source_target_pairs={{0,1},{1,0},{4,8},{5,9},{8,4},{9,5},{12,13},{13,12},{2,3},{3,2},{6... | collective-permute-start | bytes 172040 | tf_op jit(solution)/shard_map/ppermute | solution.py:774
  69.5 0.6 collective-permute-start.7
  70.0 0.7 copy.10
  70.7 0.9 %inner_kernel.1 = (f32[7,128,128]{2,1,0:T(8,128)S(1)}, f32[3,128,128]{2,1,0:T(8,128)}) custom-call(f32[8,128,128]{2,1,0:T(8,128)S(1)} %get-tuple-element.31.dens, f32[7,128,128]{2,1,0:T(8,128)S(1)} %get-tuple-element.32.belief, f32[3,128,128]{2,1,0:T(8,128)S(1)} %get-tuple-element.33.bias), custom_call_target="tpu_custom_call" | custom-call | flops 10000000 | bytes 1048576 | tf_op jit(solution)/shard_map/inner_kernel/pallas_call | solution.py:645
  71.6 1.7 %collective-permute-done.7.side = f32[7,8,128]{2,1,0:T(8,128)S(1)} collective-permute-done((f32[7,8,128]{2,1,0:T(8,128)S(1)}, f32[7,8,128]{2,1,0:T(8,128)S(1)}, u32[]{:S(2)}, u32[]{:S(2)}) %collective-permute-start.7) | collective-permute-done | bytes 28704 | tf_op jit(solution)/shard_map/ppermute | solution.py:775
  73.4 1.0 %last_kernel.1 = bf16[8,128,128]{2,1,0:T(8,128)(2,1)} custom-call(f32[7,128,128]{2,1,0:T(8,128)S(1)} %get-tuple-element.34.inner, f32[8,128,128]{2,1,0:T(8,128)S(1)} %get-tuple-element.31.dens, f32[4,128,128]{2,1,0:T(8,128)S(1)} %pad_maximum_fusion.own, f32[7,16,128]{2,1,0:T(8,128)S(1)} %collective-permute-done.5.up, ...), custom_call_target="tpu_custom_call" | custom-call | flops 10000000 | bytes 1048576 | tf_op jit(solution)/shard_map/last_kernel/pallas_call | solution.py:645
  (13 shorter events, 0.1 us)
Async XLA Ops:
  0.6 1.6 %copy-start.4 = (f32[3,8,16,128]{3,2,1,0:T(8,128)S(1)}, f32[3,8,16,128]{3,2,1,0:T(8,128)}, u32[]{:S(2)}) copy-start(f32[3,8,16,128]{3,2,1,0:T(8,128)} %param.7) | copy-start | bytes 589828
  0.6 2.1 %collective-permute-start.2 = (s32[128,128]{1,0:T(8,128)}, s32[128,128]{1,0:T(8,128)S(1)}, u32[]{:S(2)}, u32[]{:S(2)}) collective-permute-start(s32[128,128]{1,0:T(8,128)} %bitcast.14), channel_id=1, source_target_pairs={{0,1},{1,0},{2,3},{3,2},{4,5},{5,4},{6,7},{7,6},{8,9},{9,8},{10,11... | collective-permute-start | bytes 196616 | tf_op jit(solution)/shard_map/ppermute | solution.py:701
  0.7 2.0 %collective-permute-start.1 = (s32[128,128]{1,0:T(8,128)}, s32[128,128]{1,0:T(8,128)S(1)}, u32[]{:S(2)}, u32[]{:S(2)}) collective-permute-start(s32[128,128]{1,0:T(8,128)} %bitcast.15), channel_id=1, source_target_pairs={{0,1},{1,0},{2,3},{3,2},{4,5},{5,4},{6,7},{7,6},{8,9},{9,8},{10,11... | collective-permute-start | bytes 196616 | tf_op jit(solution)/shard_map/ppermute | solution.py:700
  1.2 1.7 %collective-permute-start = (f32[3,128,128]{2,1,0:T(8,128)}, f32[3,128,128]{2,1,0:T(8,128)S(1)}, u32[]{:S(2)}, u32[]{:S(2)}) collective-permute-start(f32[3,128,128]{2,1,0:T(8,128)} %bitcast.12), channel_id=1, source_target_pairs={{0,1},{1,0},{2,3},{3,2},{4,5},{5,4},{6,7},{7,6},{8,9},{9,8},{10,11... | collective-permute-start | bytes 589832 | tf_op jit(solution)/shard_map/ppermute | solution.py:699
  3.4 15.3 %copy-start.3 = (bf16[2,144,256]{2,1,0:T(8,128)(2,1)S(1)}, bf16[2,144,256]{2,1,0:T(8,128)(2,1)}, u32[]{:S(2)}) copy-start(bf16[2,144,256]{2,1,0:T(8,128)(2,1)} %constant.14.clone.table) | copy-start | bytes 442372
  18.6 12.4 %copy-start = (bf16[2,512,512]{2,1,0:T(8,128)(2,1)S(1)}, bf16[2,512,512]{2,1,0:T(8,128)(2,1)}, u32[]{:S(2)}) copy-start(bf16[2,512,512]{2,1,0:T(8,128)(2,1)} %constant.15.clone.slab_table) | copy-start | bytes 3145732
  19.3 11.7 %copy-start.1 = (bf16[2,256,256]{2,1,0:T(8,128)(2,1)S(1)}, bf16[2,256,256]{2,1,0:T(8,128)(2,1)}, u32[]{:S(2)}) copy-start(bf16[2,256,256]{2,1,0:T(8,128)(2,1)} %constant.16.clone.row_table) | copy-start | bytes 786436
  50.4 1.2 %collective-permute-start.3 = (f32[1,128]{1,0:T(1,128)S(1)}, f32[1,128]{1,0:T(1,128)S(1)}, u32[]{:S(2)}, u32[]{:S(2)}) collective-permute-start(f32[1,128]{1,0:T(1,128)S(1)} %bitcast.7), channel_id=1, source_target_pairs={{0,1},{1,0},{2,3},{3,2},{4,5},{5,4},{6,7},{7,6},{8,9},{9,8},{10,11... | collective-permute-start | bytes 1544 | tf_op jit(solution)/shard_map/ppermute | solution.py:746
  52.3 11.4 %copy-start.2 = (bf16[2,256,128]{2,1,0:T(8,128)(2,1)S(1)}, bf16[2,256,128]{2,1,0:T(8,128)(2,1)}, u32[]{:S(2)}) copy-start(bf16[2,256,128]{2,1,0:T(8,128)(2,1)} %constant.17.clone.table) | copy-start | bytes 393220
  63.7 1.4 %collective-permute-start.4 = (f32[8,48,128]{2,1,0:T(8,128)S(1)}, f32[8,48,128]{2,1,0:T(8,128)S(1)}, u32[]{:S(2)}, u32[]{:S(2)}) collective-permute-start(f32[8,48,128]{2,1,0:T(8,128)S(1)} %all_to_all.23.got), channel_id=1, source_target_pairs={{0,1},{1,0},{2,3},{3,2},{4,5},{5,4},{6,7},{7,6},{8,9},{9,8},{10,11... | collective-permute-start | bytes 589832 | tf_op jit(solution)/shard_map/ppermute | solution.py:753
  65.9 7.5 %collective-permute-start.8 = (f32[128,128]{1,0:T(8,128)S(1)}, f32[128,128]{1,0:T(8,128)S(1)}, u32[]{:S(2)}, u32[]{:S(2)}) collective-permute-start(f32[128,128]{1,0:T(8,128)S(1)} %get-tuple-element.38), channel_id=1, source_target_pairs={{0,1},{1,0},{2,3},{3,2},{4,5},{5,4},{6,7},{7,6},{8,9},{9,8},{10,11... | collective-permute-start | bytes 196616 | tf_op jit(solution)/shard_map/ppermute | solution.py:776
  66.1 7.3 %collective-permute-start.5 = (f32[7,16,128]{2,1,0:T(8,128)S(1)}, f32[7,16,128]{2,1,0:T(8,128)S(1)}, u32[]{:S(2)}, u32[]{:S(2)}) collective-permute-start(f32[7,16,128]{2,1,0:T(8,128)S(1)} %get-tuple-element.35), channel_id=1, source_target_pairs={{0,4},{1,5},{4,0},{5,1},{8,12},{9,13},{12,8},{13,9},{2,6},{3,7},{6... | collective-permute-start | bytes 172040 | tf_op jit(solution)/shard_map/ppermute | solution.py:773
  66.5 6.9 %collective-permute-start.6 = (f32[7,16,128]{2,1,0:T(8,128)S(1)}, f32[7,16,128]{2,1,0:T(8,128)S(1)}, u32[]{:S(2)}, u32[]{:S(2)}) collective-permute-start(f32[7,16,128]{2,1,0:T(8,128)S(1)} %get-tuple-element.36), channel_id=1, source_target_pairs={{0,1},{1,0},{4,8},{5,9},{8,4},{9,5},{12,13},{13,12},{2,3},{3,2},{6... | collective-permute-start | bytes 172040 | tf_op jit(solution)/shard_map/ppermute | solution.py:774
  69.5 3.9 %collective-permute-start.7 = (f32[7,8,128]{2,1,0:T(8,128)S(1)}, f32[7,8,128]{2,1,0:T(8,128)S(1)}, u32[]{:S(2)}, u32[]{:S(2)}) collective-permute-start(f32[7,8,128]{2,1,0:T(8,128)S(1)} %get-tuple-element.37), channel_id=1, source_target_pairs={{0,2},{2,0},{1,3},{3,1},{4,6},{6,4},{5,7},{7,5},{8,10},{10,8},{9,1... | collective-permute-start | bytes 86024 | tf_op jit(solution)/shard_map/ppermute | solution.py:775
